TPU v7x, 16 devices: a 4x2x1 block of a 4x4x8 slice. The times are simulated.
16 devices in a mesh: sys: 2 (over y, z), row: 8 (over x, core).
Axes of the slice: x: 4, y: 2, z: 1, core: 2. Of those that a mesh axis runs over, the one named last changes fastest.
The devices are a block of a 4x4x8 slice.
Arguments:
- positions: bfloat16 [32768, 384], P(('sys', 'row')), parts along dimension 0
- charges: float32 [32768], P(('sys', 'row')), parts along dimension 0
- counts: int32 [16], P(('sys', 'row')), parts along dimension 0
Outputs:
- output 1: float32 [32768, 384], P(('sys', 'row')), parts along dimension 0
- output 2: float32 [2], P('sys'), parts along dimension 0
There are 2 independent parts. A program takes and returns all parts, laid end to end along the dimension named above; each array names one.
All inputs are finite; a program needn't handle non-finite values.
Results may differ from a plain program's by a relative error of at most 0.001.
Values are sent between devices in bfloat16 or wider.
A program may use at most 768 MiB of HBM per device.

v0:
```python
import jax
import jax.numpy as jnp
from jax import lax
from jax.sharding import PartitionSpec as P


def sq_norm(block_pos):
    pos_f32 = block_pos.astype(jnp.float32)
    return jnp.sum(pos_f32 * pos_f32, axis=1)


def pair_weight(row_pos, row_q, col_pos, col_q, neg_scale):
    gram_mat = jnp.einsum('id,jd->ij', row_pos, col_pos, preferred_element_type=jnp.float32)
    dist_sq = jnp.maximum(sq_norm(row_pos)[:, None] + sq_norm(col_pos)[None, :] - 2.0 * gram_mat, 0.0)
    return row_q[:, None] * col_q[None, :] * jnp.exp(dist_sq * neg_scale)


def row_force(weight, w_low, row_pos, col_pos, inv_len2):
    pulled = jnp.dot(w_low, col_pos, preferred_element_type=jnp.float32)
    return (jnp.sum(weight, axis=1)[:, None] * row_pos.astype(jnp.float32) - pulled) * inv_len2


def col_force(weight, w_low, row_pos, col_pos, inv_len2):
    pushed = jnp.einsum('ij,id->jd', w_low, row_pos, preferred_element_type=jnp.float32)
    return (jnp.sum(weight, axis=0)[:, None] * col_pos.astype(jnp.float32) - pushed) * inv_len2


def solution(mesh):
    num_blocks = mesh.shape['row']
    half_way = num_blocks // 2
    next_perm = [(src, (src + 1) % num_blocks) for src in range(num_blocks)]
    home_perm = [(src, (src - half_way) % num_blocks) for src in range(num_blocks)]

    def per_device(positions, charges, counts):
        block_rows, width = positions.shape
        half_rows = block_rows // 2
        neg_scale = -0.5 / width
        inv_len2 = 1.0 / width
        live_q = jnp.where(jnp.arange(block_rows) < counts[0], charges, 0.0)
        diag_mask = jnp.arange(block_rows)[:, None] == jnp.arange(block_rows)[None, :]
        own_w = jnp.where(diag_mask, 0.0, pair_weight(positions, live_q, positions, live_q, neg_scale))
        own_force = row_force(own_w, own_w.astype(jnp.bfloat16), positions, positions, inv_len2)
        energy = 0.5 * jnp.sum(own_w)
        vis_pos = lax.ppermute(positions, 'row', next_perm)
        vis_q = lax.ppermute(live_q, 'row', next_perm)
        vis_react = jnp.zeros((block_rows, width), jnp.float32)

        def full_step(step_idx, loop_state):
            vis_pos, vis_q, vis_react, own_force, energy = loop_state
            weight = pair_weight(positions, live_q, vis_pos, vis_q, neg_scale)
            w_low = weight.astype(jnp.bfloat16)
            own_force = own_force + row_force(weight, w_low, positions, vis_pos, inv_len2)
            vis_react = vis_react + col_force(weight, w_low, positions, vis_pos, inv_len2)
            energy = energy + jnp.sum(weight)
            vis_pos = lax.ppermute(vis_pos, 'row', next_perm)
            vis_q = lax.ppermute(vis_q, 'row', next_perm)
            vis_react = lax.ppermute(vis_react, 'row', next_perm)
            return vis_pos, vis_q, vis_react, own_force, energy

        loop_state = lax.fori_loop(0, half_way - 1, full_step, (vis_pos, vis_q, vis_react, own_force, energy))
        vis_pos, vis_q, vis_react, own_force, energy = loop_state
        is_lower = lax.axis_index('row') < half_way
        a_pos = jnp.where(is_lower, positions[:half_rows], vis_pos[half_rows:])
        a_q = jnp.where(is_lower, live_q[:half_rows], vis_q[half_rows:])
        b_pos = jnp.where(is_lower, vis_pos, positions)
        b_q = jnp.where(is_lower, vis_q, live_q)
        weight = pair_weight(a_pos, a_q, b_pos, b_q, neg_scale)
        w_low = weight.astype(jnp.bfloat16)
        a_force = row_force(weight, w_low, a_pos, b_pos, inv_len2)
        b_force = col_force(weight, w_low, a_pos, b_pos, inv_len2)
        zero_half = jnp.zeros((half_rows, width), jnp.float32)
        own_force = own_force + jnp.where(is_lower, jnp.concatenate([a_force, zero_half], axis=0), b_force)
        vis_react = vis_react + jnp.where(is_lower, b_force, jnp.concatenate([zero_half, a_force], axis=0))
        energy = energy + jnp.sum(weight)
        own_force = own_force + lax.ppermute(vis_react, 'row', home_perm)
        energy = lax.psum(energy, 'row')
        return own_force, energy.reshape(1)

    row_spec = P(('sys', 'row'), None)
    vec_spec = P(('sys', 'row'))
    return jax.shard_map(per_device, mesh=mesh, in_specs=(row_spec, vec_spec, vec_spec), out_specs=(row_spec, P('sys')), check_vma=False)
```

profile of v0, /device:TPU:112, one launch (start us, length us, event | category | flops | bytes accessed | tf_op | source)
XLA Modules:
  0.0 353.5 jit_solution(14342903831757952866)
XLA Ops:
  2.0 2.5 collective-permute-start.3
  4.4 1.8 fusion.18
  6.2 14.0 %fusion.36 = (f32[]{:T(128)}, f32[2048]{0:T(1024)S(1)}, bf16[2048,2048]{0,1:T(8,128)(2,1)S(1)}) fusion(bf16[2048,384]{1,0:T(8,128)(2,1)} %param.5, f32[2048]{0:T(1024)S(1)} %fusion.18, f32[2048]{0:T(1024)S(1)} %fusion.34), kind=kOutput, calls=%fused_computation.49 | convolution fusion | flops 3271555072 | bytes 9986052 | tf_op jit(solution)/shard_map/id,jd->ij/dot_general | solution.py:13
  20.2 6.4 %fusion.20 = f32[2048,384]{1,0:T(8,128)} fusion(bf16[2048,384]{1,0:T(8,128)(2,1)S(1)} %copy-done, bf16[2048,2048]{0,1:T(8,128)(2,1)S(1)} %get-tuple-element.84, f32[2048]{0:T(1024)S(1)} %get-tuple-element.57), kind=kOutput, calls=%fused_computation.28 | convolution fusion | flops 3224371200 | bytes 13115392 | tf_op jit(solution)/shard_map/dot_general | solution.py:19
  27.3 1.9 broadcast_in_dim.10
  29.2 226.3 %while.18 = (s32[]{:T(128)}, bf16[2048,384]{1,0:T(8,128)(2,1)}, f32[2048]{0:T(1024)S(1)}, f32[2048,384]{1,0:T(8,128)}, f32[2048,384]{1,0:T(8,128)}, /*index=5*/f...) while((s32[]{:T(128)}, bf16[2048,384]{1,0:T(8,128)(2,1)}, f32[2048]{0:T(1024)S(1)}, ...), condition=%wide.region_9.10_spmd, body=%wide.region_3.9_spmd.sunk | while | flops 9722388480 | bytes 97648912 | solution.py:60
  31.3 11.0 %fusion.71 = (f32[]{:T(128)}, f32[2048]{0:T(1024)S(1)}, f32[2048]{0:T(1024)S(1)}, bf16[2048,2048]{1,0:T(8,128)(2,1)S(1)}) fusion(bf16[2048,384]{1,0:T(8,128)(2,1)S(1)} %get-tuple-element.183, bf16[2048,384]{1,0:T(8,128)(2,1)S(1)} %copy.12, f32[2048]{0:T(1024)S(1)} %get-tuple-element.152, f32[2048]{0:T(1024)S(1)} %get-tuple-element.153, ...), kind=kOutput, calls=%fused_computation.48.clone.1 | convolution fusion | flops 3267358720 | bytes 11583492 | tf_op jit(solution)/shard_map/while/body/eval_jaxpr/id,jd->ij/dot_general | solution.py:13
  42.3 7.5 %fusion.72 = f32[2048,384]{1,0:T(8,128)} fusion(f32[2048,384]{1,0:T(8,128)} %get-tuple-element.170, bf16[2048,384]{1,0:T(8,128)(2,1)S(1)} %copy.12, bf16[2048,384]{1,0:T(8,128)(2,1)S(1)} %get-tuple-element.183, bf16[2048,2048]{1,0:T(8,128)(2,1)S(1)} %get-tuple-element.154, f32[2048]{0:T(1024)S(1)} %get-tuple-element.155), kind=kOutput, calls=%fused_computation.16.clone.1 | convolution fusion | flops 3225157632 | bytes 17833984 | tf_op jit(solution)/shard_map/while/body/eval_jaxpr/ij,id->jd/dot_general | solution.py:24
  49.8 1.7 collective-permute-start
  51.6 5.3 %fusion.73 = f32[2048,384]{1,0:T(8,128)S(1)} fusion(f32[2048,384]{1,0:T(8,128)S(1)} %copy-done.2, bf16[2048,384]{1,0:T(8,128)(2,1)S(1)} %get-tuple-element.183, bf16[2048,384]{1,0:T(8,128)(2,1)S(1)} %copy.12, bf16[2048,2048]{1,0:T(8,128)(2,1)S(1)} %get-tuple-element.154, f32[2048]{0:T(1024)S(1)} %get-tuple-element.156), kind=kOutput, calls=%fused_computation.12.clone.1 | convolution fusion | flops 3225157632 | bytes 17833984 | tf_op jit(solution)/shard_map/while/body/eval_jaxpr/dot_general | solution.py:19
  56.9 1.7 copy-done.3
  59.2 45.5 %collective-permute-done.1 = f32[2048]{0:T(1024)S(1)} collective-permute-done((f32[2048]{0:T(1024)S(1)}, f32[2048]{0:T(1024)S(1)}, u32[]{:S(2)}, u32[]{:S(2)}) %collective-permute-start.1) | collective-permute-done | bytes 8224 | tf_op jit(solution)/shard_map/while/body/eval_jaxpr/ppermute | solution.py:56
  104.6 1.4 copy.12
  106.8 11.0 %fusion.71 = (f32[]{:T(128)}, f32[2048]{0:T(1024)S(1)}, f32[2048]{0:T(1024)S(1)}, bf16[2048,2048]{1,0:T(8,128)(2,1)S(1)}) fusion(bf16[2048,384]{1,0:T(8,128)(2,1)S(1)} %get-tuple-element.183, bf16[2048,384]{1,0:T(8,128)(2,1)S(1)} %copy.12, f32[2048]{0:T(1024)S(1)} %get-tuple-element.152, f32[2048]{0:T(1024)S(1)} %get-tuple-element.153, ...), kind=kOutput, calls=%fused_computation.48.clone.1 | convolution fusion | flops 3267358720 | bytes 11583492 | tf_op jit(solution)/shard_map/while/body/eval_jaxpr/id,jd->ij/dot_general | solution.py:13
  117.7 7.5 %fusion.72 = f32[2048,384]{1,0:T(8,128)} fusion(f32[2048,384]{1,0:T(8,128)} %get-tuple-element.170, bf16[2048,384]{1,0:T(8,128)(2,1)S(1)} %copy.12, bf16[2048,384]{1,0:T(8,128)(2,1)S(1)} %get-tuple-element.183, bf16[2048,2048]{1,0:T(8,128)(2,1)S(1)} %get-tuple-element.154, f32[2048]{0:T(1024)S(1)} %get-tuple-element.155), kind=kOutput, calls=%fused_computation.16.clone.1 | convolution fusion | flops 3225157632 | bytes 17833984 | tf_op jit(solution)/shard_map/while/body/eval_jaxpr/ij,id->jd/dot_general | solution.py:24
  125.8 5.3 %fusion.73 = f32[2048,384]{1,0:T(8,128)S(1)} fusion(f32[2048,384]{1,0:T(8,128)S(1)} %copy-done.2, bf16[2048,384]{1,0:T(8,128)(2,1)S(1)} %get-tuple-element.183, bf16[2048,384]{1,0:T(8,128)(2,1)S(1)} %copy.12, bf16[2048,2048]{1,0:T(8,128)(2,1)S(1)} %get-tuple-element.154, f32[2048]{0:T(1024)S(1)} %get-tuple-element.156), kind=kOutput, calls=%fused_computation.12.clone.1 | convolution fusion | flops 3225157632 | bytes 17833984 | tf_op jit(solution)/shard_map/while/body/eval_jaxpr/dot_general | solution.py:19
  131.1 1.7 copy-done.3
  133.4 46.7 %collective-permute-done.1 = f32[2048]{0:T(1024)S(1)} collective-permute-done((f32[2048]{0:T(1024)S(1)}, f32[2048]{0:T(1024)S(1)}, u32[]{:S(2)}, u32[]{:S(2)}) %collective-permute-start.1) | collective-permute-done | bytes 8224 | tf_op jit(solution)/shard_map/while/body/eval_jaxpr/ppermute | solution.py:56
  180.1 1.4 copy.12
  182.2 11.0 %fusion.71 = (f32[]{:T(128)}, f32[2048]{0:T(1024)S(1)}, f32[2048]{0:T(1024)S(1)}, bf16[2048,2048]{1,0:T(8,128)(2,1)S(1)}) fusion(bf16[2048,384]{1,0:T(8,128)(2,1)S(1)} %get-tuple-element.183, bf16[2048,384]{1,0:T(8,128)(2,1)S(1)} %copy.12, f32[2048]{0:T(1024)S(1)} %get-tuple-element.152, f32[2048]{0:T(1024)S(1)} %get-tuple-element.153, ...), kind=kOutput, calls=%fused_computation.48.clone.1 | convolution fusion | flops 3267358720 | bytes 11583492 | tf_op jit(solution)/shard_map/while/body/eval_jaxpr/id,jd->ij/dot_general | solution.py:13
  193.2 7.5 %fusion.72 = f32[2048,384]{1,0:T(8,128)} fusion(f32[2048,384]{1,0:T(8,128)} %get-tuple-element.170, bf16[2048,384]{1,0:T(8,128)(2,1)S(1)} %copy.12, bf16[2048,384]{1,0:T(8,128)(2,1)S(1)} %get-tuple-element.183, bf16[2048,2048]{1,0:T(8,128)(2,1)S(1)} %get-tuple-element.154, f32[2048]{0:T(1024)S(1)} %get-tuple-element.155), kind=kOutput, calls=%fused_computation.16.clone.1 | convolution fusion | flops 3225157632 | bytes 17833984 | tf_op jit(solution)/shard_map/while/body/eval_jaxpr/ij,id->jd/dot_general | solution.py:24
  200.7 5.3 %fusion.73 = f32[2048,384]{1,0:T(8,128)S(1)} fusion(f32[2048,384]{1,0:T(8,128)S(1)} %copy-done.2, bf16[2048,384]{1,0:T(8,128)(2,1)S(1)} %get-tuple-element.183, bf16[2048,384]{1,0:T(8,128)(2,1)S(1)} %copy.12, bf16[2048,2048]{1,0:T(8,128)(2,1)S(1)} %get-tuple-element.154, f32[2048]{0:T(1024)S(1)} %get-tuple-element.156), kind=kOutput, calls=%fused_computation.12.clone.1 | convolution fusion | flops 3225157632 | bytes 17833984 | tf_op jit(solution)/shard_map/while/body/eval_jaxpr/dot_general | solution.py:19
  206.0 1.7 copy-done.3
  208.3 47.2 %collective-permute-done.1 = f32[2048]{0:T(1024)S(1)} collective-permute-done((f32[2048]{0:T(1024)S(1)}, f32[2048]{0:T(1024)S(1)}, u32[]{:S(2)}, u32[]{:S(2)}) %collective-permute-start.1) | collective-permute-done | bytes 8224 | tf_op jit(solution)/shard_map/while/body/eval_jaxpr/ppermute | solution.py:56
  255.5 2.1 fusion.21
  257.6 1.5 fusion.29
  259.1 6.1 %fusion.37 = (f32[]{:T(128)}, f32[2048]{0:T(1024)S(1)}, f32[1024]{0:T(1024)S(1)}, bf16[1024,2048]{1,0:T(8,128)(2,1)S(1)}) fusion(bf16[1024,384]{1,0:T(8,128)(2,1)S(1)} %get-tuple-element.78, bf16[2048,384]{1,0:T(8,128)(2,1)S(1)} %get-tuple-element.80, f32[2048]{0:T(1024)S(1)} %get-tuple-element.79, f32[1024]{0:T(1024)S(1)} %get-tuple-element.77, ...), kind=kOutput, calls=%fused_computation.50 | convolution fusion | flops 1633678336 | bytes 6590468 | tf_op jit(solution)/shard_map/id,jd->ij/dot_general | solution.py:13
  265.2 2.3 fusion.31
  267.6 2.5 fusion.23
  270.1 4.1 %select_add_fusion = f32[2048,384]{1,0:T(8,128)} fusion(f32[2048,384]{1,0:T(8,128)} %get-tuple-element.51, f32[2048,384]{1,0:T(8,128)S(1)} %fusion.23, f32[1024,384]{1,0:T(8,128)S(1)} %fusion.31, pred[]{:T(512)S(6)} %lt.14), kind=kLoop, calls=%fused_computation.32 | loop fusion | flops 1572864 | bytes 11010049 | tf_op jit(solution)/shard_map/add | solution.py:73
  274.8 73.3 %psum.7 = f32[1]{0:T(128)} all-reduce(f32[1]{0:T(128)} %bitcast.1), channel_id=1, replica_groups=mesh['sys'=2,'row'=8] {'row'}, use_global_device_ids=true, to_apply=%region_15.16 | all-reduce | flops 1 | bytes 8 | tf_op jit(solution)/shard_map/psum | solution.py:76
  348.1 5.4 %add_add_fusion = f32[2048,384]{1,0:T(8,128)} fusion(f32[2048,384]{1,0:T(8,128)} %collective-permute-done.5, f32[2048,384]{1,0:T(8,128)} %get-tuple-element.48, f32[2048,384]{1,0:T(8,128)S(1)} %fusion.23, f32[1024,384]{1,0:T(8,128)} %copy-done.1, pred[]{:T(512)S(6)} %lt.14), kind=kLoop, calls=%fused_computation.33 | loop fusion | flops 2359296 | bytes 14155777 | tf_op jit(solution)/shard_map/add | solution.py:75
  (44 shorter events, 4.9 us)
Async XLA Ops:
  2.0 25.3 %collective-permute-start.4 = (f32[2048]{0:T(1024)S(1)}, f32[2048]{0:T(1024)S(1)}, u32[]{:S(2)}, u32[]{:S(2)}) collective-permute-start(f32[2048]{0:T(1024)S(1)} %fusion.34), channel_id=1, source_target_pairs={{0,1},{1,2},{2,3},{3,4},{4,5},{5,6},{6,7},{7,0},{8,9},{9,10},{10,1... | collective-permute-start | bytes 24584 | tf_op jit(solution)/shard_map/ppermute | solution.py:45
  2.0 25.3 %collective-permute-start.3 = (bf16[2048,384]{1,0:T(8,128)(2,1)}, bf16[2048,384]{1,0:T(8,128)(2,1)}, u32[]{:S(2)}, u32[]{:S(2)}) collective-permute-start(bf16[2048,384]{1,0:T(8,128)(2,1)} %param.5), channel_id=1, source_target_pairs={{0,1},{1,2},{2,3},{3,4},{4,5},{5,6},{6,7},{7,0},{8,9},{9,10},{10,1... | collective-permute-start | bytes 4718600 | tf_op jit(solution)/shard_map/ppermute | solution.py:44
  6.2 14.0 %copy-start = (bf16[2048,384]{1,0:T(8,128)(2,1)S(1)}, bf16[2048,384]{1,0:T(8,128)(2,1)}, u32[]{:S(2)}) copy-start(bf16[2048,384]{1,0:T(8,128)(2,1)} %param.5) | copy-start | bytes 4718596
  42.3 9.2 %copy-start.2 = (f32[2048,384]{1,0:T(8,128)S(1)}, f32[2048,384]{1,0:T(8,128)}, u32[]{:S(2)}) copy-start(f32[2048,384]{1,0:T(8,128)} %get-tuple-element.171) | copy-start | bytes 9437188 | tf_op jit(solution)/shard_map/while
  49.8 54.9 %collective-permute-start.2 = (f32[2048,384]{1,0:T(8,128)}, f32[2048,384]{1,0:T(8,128)}, u32[]{:S(2)}, u32[]{:S(2)}) collective-permute-start(f32[2048,384]{1,0:T(8,128)} %fusion.72), channel_id=1, source_target_pairs={{0,1},{1,2},{2,3},{3,4},{4,5},{5,6},{6,7},{7,0},{8,9},{9,10},{10,1... | collective-permute-start | bytes 9437192 | tf_op jit(solution)/shard_map/while/body/eval_jaxpr/ppermute | solution.py:57
  49.8 54.8 %collective-permute-start = (bf16[2048,384]{1,0:T(8,128)(2,1)S(1)}, bf16[2048,384]{1,0:T(8,128)(2,1)}, u32[]{:S(2)}, u32[]{:S(2)}) collective-permute-start(bf16[2048,384]{1,0:T(8,128)(2,1)S(1)} %copy.12), channel_id=1, source_target_pairs={{0,1},{1,2},{2,3},{3,4},{4,5},{5,6},{6,7},{7,0},{8,9},{9,10},{10,1... | collective-permute-start | bytes 4718600 | tf_op jit(solution)/shard_map/while/body/eval_jaxpr/ppermute | solution.py:55
  51.5 53.1 %collective-permute-start.1 = (f32[2048]{0:T(1024)S(1)}, f32[2048]{0:T(1024)S(1)}, u32[]{:S(2)}, u32[]{:S(2)}) collective-permute-start(f32[2048]{0:T(1024)S(1)} %copy.13), channel_id=1, source_target_pairs={{0,1},{1,2},{2,3},{3,4},{4,5},{5,6},{6,7},{7,0},{8,9},{9,10},{10,1... | collective-permute-start | bytes 24584 | tf_op jit(solution)/shard_map/while/body/eval_jaxpr/ppermute | solution.py:56
  56.9 1.7 copy-start.3
  117.7 8.0 %copy-start.2 = (f32[2048,384]{1,0:T(8,128)S(1)}, f32[2048,384]{1,0:T(8,128)}, u32[]{:S(2)}) copy-start(f32[2048,384]{1,0:T(8,128)} %get-tuple-element.171) | copy-start | bytes 9437188 | tf_op jit(solution)/shard_map/while
  125.2 54.9 %collective-permute-start.2 = (f32[2048,384]{1,0:T(8,128)}, f32[2048,384]{1,0:T(8,128)}, u32[]{:S(2)}, u32[]{:S(2)}) collective-permute-start(f32[2048,384]{1,0:T(8,128)} %fusion.72), channel_id=1, source_target_pairs={{0,1},{1,2},{2,3},{3,4},{4,5},{5,6},{6,7},{7,0},{8,9},{9,10},{10,1... | collective-permute-start | bytes 9437192 | tf_op jit(solution)/shard_map/while/body/eval_jaxpr/ppermute | solution.py:57
  125.2 54.8 %collective-permute-start = (bf16[2048,384]{1,0:T(8,128)(2,1)S(1)}, bf16[2048,384]{1,0:T(8,128)(2,1)}, u32[]{:S(2)}, u32[]{:S(2)}) collective-permute-start(bf16[2048,384]{1,0:T(8,128)(2,1)S(1)} %copy.12), channel_id=1, source_target_pairs={{0,1},{1,2},{2,3},{3,4},{4,5},{5,6},{6,7},{7,0},{8,9},{9,10},{10,1... | collective-permute-start | bytes 4718600 | tf_op jit(solution)/shard_map/while/body/eval_jaxpr/ppermute | solution.py:55
  125.8 54.3 %collective-permute-start.1 = (f32[2048]{0:T(1024)S(1)}, f32[2048]{0:T(1024)S(1)}, u32[]{:S(2)}, u32[]{:S(2)}) collective-permute-start(f32[2048]{0:T(1024)S(1)} %copy.13), channel_id=1, source_target_pairs={{0,1},{1,2},{2,3},{3,4},{4,5},{5,6},{6,7},{7,0},{8,9},{9,10},{10,1... | collective-permute-start | bytes 24584 | tf_op jit(solution)/shard_map/while/body/eval_jaxpr/ppermute | solution.py:56
  131.1 1.7 copy-start.3
  193.2 7.6 %copy-start.2 = (f32[2048,384]{1,0:T(8,128)S(1)}, f32[2048,384]{1,0:T(8,128)}, u32[]{:S(2)}) copy-start(f32[2048,384]{1,0:T(8,128)} %get-tuple-element.171) | copy-start | bytes 9437188 | tf_op jit(solution)/shard_map/while
  200.6 54.9 %collective-permute-start.2 = (f32[2048,384]{1,0:T(8,128)}, f32[2048,384]{1,0:T(8,128)}, u32[]{:S(2)}, u32[]{:S(2)}) collective-permute-start(f32[2048,384]{1,0:T(8,128)} %fusion.72), channel_id=1, source_target_pairs={{0,1},{1,2},{2,3},{3,4},{4,5},{5,6},{6,7},{7,0},{8,9},{9,10},{10,1... | collective-permute-start | bytes 9437192 | tf_op jit(solution)/shard_map/while/body/eval_jaxpr/ppermute | solution.py:57
  200.7 54.8 %collective-permute-start = (bf16[2048,384]{1,0:T(8,128)(2,1)S(1)}, bf16[2048,384]{1,0:T(8,128)(2,1)}, u32[]{:S(2)}, u32[]{:S(2)}) collective-permute-start(bf16[2048,384]{1,0:T(8,128)(2,1)S(1)} %copy.12), channel_id=1, source_target_pairs={{0,1},{1,2},{2,3},{3,4},{4,5},{5,6},{6,7},{7,0},{8,9},{9,10},{10,1... | collective-permute-start | bytes 4718600 | tf_op jit(solution)/shard_map/while/body/eval_jaxpr/ppermute | solution.py:55
  200.7 54.8 %collective-permute-start.1 = (f32[2048]{0:T(1024)S(1)}, f32[2048]{0:T(1024)S(1)}, u32[]{:S(2)}, u32[]{:S(2)}) collective-permute-start(f32[2048]{0:T(1024)S(1)} %copy.13), channel_id=1, source_target_pairs={{0,1},{1,2},{2,3},{3,4},{4,5},{5,6},{6,7},{7,0},{8,9},{9,10},{10,1... | collective-permute-start | bytes 24584 | tf_op jit(solution)/shard_map/while/body/eval_jaxpr/ppermute | solution.py:56
  206.0 1.7 copy-start.3
  255.5 3.6 %copy-start.4 = (f32[2048]{0:T(1024)S(1)}, f32[2048]{0:T(1024)}, u32[]{:S(2)}) copy-start(f32[2048]{0:T(1024)} %param.6) | copy-start | bytes 24580
  267.5 2.5 copy-start.1
  274.1 74.0 %collective-permute-start.5 = (f32[2048,384]{1,0:T(8,128)}, f32[2048,384]{1,0:T(8,128)}, u32[]{:S(2)}, u32[]{:S(2)}) collective-permute-start(f32[2048,384]{1,0:T(8,128)} %select_add_fusion), channel_id=1, source_target_pairs={{0,4},{1,5},{2,6},{3,7},{4,0},{5,1},{6,2},{7,3},{8,12},{9,13},{10,... | collective-permute-start | bytes 9437192 | tf_op jit(solution)/shard_map/ppermute | solution.py:75
where the time goes:
time: 354 us; the launch traced here: 353 us
  waiting for transfers between devices  139 us (39%)
  matrix products  103 us (29%)
  blocking collectives  73.3 us (21%)
  other arithmetic  17.6 us (5%)
  local copies, waits for them, and re-layouts  11.1 us (3%)
  starting transfers between devices  4.84 us (1%)
    ppermute x3, waiting for transfers between devices, full_step(): vis_q = lax.ppermute(vis_q, 'row', next_perm)  139 us
    psum x1, blocking collectives, per_device(): energy = lax.psum(energy, 'row')  73.3 us
    dot_general x5, matrix products, pair_weight(): jnp.einsum('id,jd->ij', row_pos, col_pos, preferred_element_type=jnp.floa...  53.1 us
    dot_general x4, matrix products, col_force(): jnp.einsum('ij,id->jd', w_low, row_pos, preferred_element_type=jnp.float32)  24.9 us
    dot_general x5, matrix products, row_force(): pulled = jnp.dot(w_low, col_pos, preferred_element_type=jnp.float32)  24.6 us
    reduce_sum x6, other arithmetic, sq_norm(): return jnp.sum(pos_f32 * pos_f32, axis=1)  7.43 us
  transfers between devices with their start and end apart: 12, of which 3 were waited for; matrix products, arithmetic and copies ran while one was open for 11% of the time, Pallas kernels for 0%

commit v1 on v0

v1 whole, which is shorter than its diff:
```python
import functools
import math

import jax
import jax.numpy as jnp
from jax import lax
from jax.experimental import pallas as pl
from jax.experimental.pallas import tpu as pltpu
from jax.sharding import PartitionSpec as P


LANES = 128
TILE_I = 512
TILE_J = 512
BUDGET = 20
MESH = pl.DeviceIdType.MESH
VMEM_SPEC = pl.BlockSpec(memory_space=pltpu.VMEM)


def energy_kernel(n, part_ref, out_ref, seen, send_sem, recv_sem):
    me = lax.axis_index('row')
    barrier = pltpu.get_barrier_semaphore()
    for off in range(1, n):
        pl.semaphore_signal(barrier, inc=1, device_id={'row': lax.rem(me + off, n)}, device_id_type=MESH)
    pl.semaphore_wait(barrier, n - 1)
    copies = []
    for off in range(1, n):
        copies.append(pltpu.make_async_remote_copy(
            src_ref=part_ref, dst_ref=seen.at[me], send_sem=send_sem.at[off - 1], recv_sem=recv_sem.at[off - 1],
            device_id={'row': lax.rem(me + off, n)}, device_id_type=MESH))
    for copy in copies:
        copy.start()
    for copy in copies:
        copy.wait()
    total = jnp.zeros_like(part_ref)
    for k in range(n):
        total += jnp.where(me == k, part_ref[...], seen[k])
    out_ref[0] = 0.5 * jnp.sum(total)


def total_energy(part, n):
    return pl.pallas_call(
        functools.partial(energy_kernel, n),
        out_shape=jax.ShapeDtypeStruct((1,), jnp.float32),
        in_specs=[VMEM_SPEC],
        out_specs=pl.BlockSpec(memory_space=pltpu.SMEM),
        scratch_shapes=[pltpu.VMEM((n,) + part.shape, jnp.float32), pltpu.SemaphoreType.DMA((n - 1,)), pltpu.SemaphoreType.DMA((n - 1,))],
        compiler_params=pltpu.CompilerParams(collective_id=0, has_side_effects=True),
        name='energy',
    )(part)


def exchange_kernel(n, src_ref, out_ref, send_sem, recv_sem, local_sem):
    me = lax.axis_index('row')
    barrier = pltpu.get_barrier_semaphore()
    for off in range(1, n):
        pl.semaphore_signal(barrier, inc=1, device_id={'row': lax.rem(me + off, n)}, device_id_type=MESH)
    own = pltpu.make_async_copy(src_ref, out_ref.at[me], local_sem)
    own.start()
    pl.semaphore_wait(barrier, n - 1)
    copies = []
    for off in range(1, n):
        copies.append(pltpu.make_async_remote_copy(
            src_ref=src_ref, dst_ref=out_ref.at[me], send_sem=send_sem.at[off - 1], recv_sem=recv_sem.at[off - 1],
            device_id={'row': lax.rem(me + off, n)}, device_id_type=MESH))
    for copy in copies:
        copy.start()
    own.wait()
    for copy in copies:
        copy.wait()


def exchange(src, n):
    return pl.pallas_call(
        functools.partial(exchange_kernel, n),
        out_shape=jax.ShapeDtypeStruct((n,) + src.shape, src.dtype),
        in_specs=[pl.BlockSpec(memory_space=pltpu.HBM)],
        out_specs=pl.BlockSpec(memory_space=pltpu.HBM),
        scratch_shapes=[pltpu.SemaphoreType.DMA((n - 1,)), pltpu.SemaphoreType.DMA((n - 1,)), pltpu.SemaphoreType.DMA],
        compiler_params=pltpu.CompilerParams(collective_id=1, has_side_effects=True),
        cost_estimate=pl.CostEstimate(flops=0, bytes_accessed=8 << 20, transcendentals=0),
        name='exchange',
    )(src)


def up(value, step):
    return pl.cdiv(value, step) * step


def pair_kernel(cfg, *refs):
    rows, width, n, scale = cfg['rows'], cfg['width'], cfg['n'], cfg['scale']
    metas, refs = refs[0], refs[1:]
    loads, refs = refs[:len(cfg['loads'])], refs[len(cfg['loads']):]
    if cfg['stage'] == 0:
        partner_pos, spread_h, spread_c, refs = refs[0], refs[1], refs[2], refs[3:]
    if cfg['finish']:
        incoming, refs = refs[0], refs[1:]
    if cfg['stage'] > 0:
        refs = refs[6:]
    x_row, h_row_all, c_row_all, x_col, cols, sums = refs[:6]
    gram_a, gram_b = refs[-2:]
    extra = refs[6:-2]

    me = lax.axis_index('row')
    ahead = jnp.where(lax.rem(me, 2) == 0, n - 2, 2)
    mate = me + 1 - 2 * lax.rem(me, 2)
    block_of = {'own': me, 'near': lax.rem(me + ahead, n), 'next': lax.rem(me + n - ahead, n), 'far': lax.rem(me + n // 2, n),
                'mate': mate, 'away': lax.rem(mate + n // 2, n)}
    names = []
    for stage in cfg['plan'][:cfg['stage'] + 1]:
        names += [c[0] for c in stage]
    count = {k: jnp.max(metas[block_of[k], 2:3, 0:LANES]).astype(jnp.int32) for k in ['mate'] + sorted(set(names))}
    tiles_own = pl.cdiv(count['own'], TILE_I)
    row_mate = pl.multiple_of(up(count['own'], LANES), LANES)
    tiles_both = pl.cdiv(row_mate + count['mate'], TILE_I)

    end = jnp.int32(0)
    lo = jnp.int32(0)
    for stage, chunks in enumerate(cfg['plan'][:cfg['stage'] + 1]):
        mode = cfg['modes'][stage]
        for k, (name, start, size) in enumerate(chunks):
            if stage == cfg['stage']:
                at = pl.multiple_of(end, LANES)
                x_col[pl.ds(at, size), :] = loads[k][...]
                x_col[pl.ds(pl.multiple_of(at + size, LANES), TILE_J), :] = jnp.zeros((TILE_J, width), x_col.dtype)
                cols[:, pl.ds(at, size)] = metas[block_of[name], 0:2, start:start + size]
                cols[:, pl.ds(pl.multiple_of(at + size, LANES), TILE_J)] = jnp.zeros((2, TILE_J), jnp.float32)
            end = end + up(jnp.clip(count[name] - start, 0, size), LANES)
        tiles = tiles_own if mode == 'own' else tiles_both
        have = pl.cdiv(end, TILE_J) if cfg['close'][stage] else end // TILE_J
        budget = cfg['budget'][stage]
        hi = have if budget is None else jnp.minimum(have, lo + budget // jnp.maximum(tiles, 1))
        if stage < cfg['stage']:
            lo = hi
        if cfg['close'][stage]:
            end = up(end, TILE_J)
    n_j = hi - lo
    units = n_j * tiles

    if cfg['stage'] == 0:
        sums[...] = jnp.zeros_like(sums)
        x_row[0:rows, :] = loads[0][...]
        h_row_all[0:rows, :] = spread_h[0:rows, :]
        c_row_all[0:rows, :] = spread_c[0:rows, :]
        x_row[pl.ds(row_mate, rows), :] = partner_pos[...]
        h_row_all[pl.ds(row_mate, rows), :] = spread_h[rows:, :]
        c_row_all[pl.ds(row_mate, rows), :] = spread_c[rows:, :]

    def decode(unit):
        at = jnp.minimum(unit, units - 1)
        j = at // tiles
        return (at - j * tiles) * TILE_I, (j + lo) * TILE_J, jnp.where(unit < units, (j + lo) * TILE_J, cfg['null'])

    def aligned(pos):
        row, col, meta = pos
        return (pl.ds(pl.multiple_of(row, TILE_I), TILE_I), pl.ds(pl.multiple_of(col, TILE_J), TILE_J), pl.multiple_of(meta, TILE_J))

    def gram(pos, out):
        row, col, _ = aligned(pos)
        out[...] = lax.dot_general(x_row[row, :], x_col[col, :], (((1,), (1,)), ((), ())), preferred_element_type=jnp.float32)

    def weigh(pos, prod):
        row, col, meta = aligned(pos)
        h_row, c_row = h_row_all[row, :], c_row_all[row, :]
        parts, total = [], None
        for k in range(TILE_J // LANES):
            at = pl.ds(pl.multiple_of(meta + k * LANES, LANES), LANES)
            arg = jnp.minimum(prod[:, k * LANES:(k + 1) * LANES] * (2.0 * scale) - h_row - cols[1:2, at], 0.0)
            w = jnp.exp2(arg) * c_row * cols[0:1, at]
            if cfg['stage'] == 0:
                off = pos[1] + k * LANES
                off = jnp.where(off < row_mate, off - pos[0], 1 << 20)
                w = jnp.where(lax.broadcasted_iota(jnp.int32, (TILE_I, LANES), 0) - lax.broadcasted_iota(jnp.int32, (TILE_I, LANES), 1) == off, 0.0, w)
            total = w if total is None else total + w
            parts.append(w.astype(jnp.bfloat16))
        sums[row, width:] += total
        sums[row, :width] += jnp.dot(jnp.concatenate(parts, axis=1), x_col[col, :], preferred_element_type=jnp.float32)

    @pl.when(units > 0)
    def _():
        first = decode(0)
        gram(first, gram_a)

        def step(p, pos):
            mid = decode(2 * p + 1)
            gram(mid, gram_b)
            weigh(pos, gram_a)
            nxt = decode(2 * p + 2)
            gram(nxt, gram_a)
            weigh(mid, gram_b)
            return nxt

        lax.fori_loop(0, pl.cdiv(units, 2), step, first)

    if cfg['split']:
        extra[0][...] = sums[pl.ds(row_mate, rows), :]
    if cfg['finish']:
        force, part = extra
        part[...] = jnp.zeros_like(part)

        def tile(i, carry):
            at = pl.ds(pl.multiple_of(i * TILE_I, TILE_I), TILE_I)
            live = lax.broadcasted_iota(jnp.int32, (TILE_I, LANES), 0) + i * TILE_I < count['own']
            lanes = jnp.where(live, sums[at, width:] + incoming[at, width:], 0.0)
            x = x_row[at, :].astype(jnp.float32)
            value = (jnp.sum(lanes, axis=1, keepdims=True) * x - (sums[at, :width] + incoming[at, :width])) * cfg['inv_len2']
            force[at, :] = jnp.where(live[:, :1], value, 0.0)
            part[...] += jnp.sum(lanes.reshape(TILE_I // 8, 8, LANES), axis=0)
            return carry

        lax.fori_loop(0, rows // TILE_I, tile, 0)


def pair_call(stage, n, plan, modes, close, budget, metas, chunks, state, first=None, incoming=None, split=False):
    width = chunks[0].shape[1]
    rows = metas.shape[2]
    tall = 2 * rows + TILE_I
    null = up(sum(c[2] for s in plan for c in s), TILE_J) + (len(plan) + 1) * TILE_J
    cfg = dict(rows=rows, width=width, n=n, null=null, stage=stage, plan=plan, modes=modes, close=close, budget=budget, loads=chunks,
               finish=incoming is not None, split=split, scale=math.log2(math.e) * 0.5 / width, inv_len2=1.0 / width)
    args = [metas] + list(chunks)
    if stage == 0:
        args += list(first)
    if incoming is not None:
        args.append(incoming)
    aliases = {}
    if stage > 0:
        for k, a in enumerate(state):
            aliases[len(args)] = k
            args.append(a)
    out_shape = [pltpu.VMEM((tall, width), jnp.bfloat16), pltpu.VMEM((tall, LANES), jnp.float32), pltpu.VMEM((tall, LANES), jnp.float32),
                 pltpu.VMEM((null, width), jnp.bfloat16), pltpu.VMEM((2, null + TILE_J), jnp.float32), pltpu.VMEM((tall, width + LANES), jnp.float32)]
    if split:
        out_shape.append(jax.ShapeDtypeStruct((rows, width + LANES), jnp.float32))
    if incoming is not None:
        out_shape += [jax.ShapeDtypeStruct((rows, width), jnp.float32), pltpu.VMEM((8, LANES), jnp.float32)]
    outs = pl.pallas_call(
        functools.partial(pair_kernel, cfg),
        out_shape=out_shape,
        in_specs=[VMEM_SPEC] * len(args),
        out_specs=[VMEM_SPEC] * len(out_shape),
        input_output_aliases=aliases,
        scratch_shapes=[pltpu.VMEM((TILE_I, TILE_J), jnp.float32)] * 2,
        compiler_params=pltpu.CompilerParams(vmem_limit_bytes=18 << 20),
        cost_estimate=pl.CostEstimate(flops=1 << 30, bytes_accessed=1 << 20, transcendentals=0),
    )(*args)
    return list(outs[:6]), outs[6:]


def solution(mesh):
    n = mesh.shape['row']
    forth = [(p, (p + 2) % n if p % 2 == 0 else (p - 2) % n) for p in range(n)]
    back = [(b, a) for a, b in forth]
    swap = [(p, p ^ 1) for p in range(n)]

    def move(x, perm):
        return lax.ppermute(x, 'row', perm)

    def body(positions, charges, counts):
        block_rows, width = positions.shape
        half_rows = block_rows // 2
        scale = math.log2(math.e) * 0.5 / width

        live_q = jnp.where(jnp.arange(block_rows) < counts[0], charges, 0.0)
        pos_f32 = positions.astype(jnp.float32)
        half = jnp.sum(pos_f32 * pos_f32, axis=1) * scale
        meta = jnp.stack([live_q, half, jnp.broadcast_to(counts[0].astype(jnp.float32), live_q.shape), jnp.zeros_like(half)])
        metas = exchange(meta, n)
        mate = metas[lax.axis_index('row') ^ 1]

        top, bottom = positions[:half_rows], positions[half_rows:]
        mate_pos = move(positions, swap)
        near_a, next_a = move(top, forth), move(top, back)
        near_b, next_b = move(bottom, forth), move(bottom, back)
        far_a, far_b = move(near_a, forth), move(near_b, forth)
        away_a, away_b = move(far_a, swap), move(far_b, swap)

        def spread(k):
            return jnp.broadcast_to(jnp.concatenate([meta[k], mate[k]])[:, None], (2 * block_rows, LANES))

        def upper(name):
            return name, 0, half_rows

        def lower(name):
            return name, half_rows, block_rows - half_rows

        plan = [[('own', 0, block_rows)], [upper('near'), upper('next')], [lower('near'), lower('next')],
                [upper('far')], [lower('far'), upper('away')], [lower('away')]]
        arrays = [[positions], [near_a, next_a], [near_b, next_b], [far_a], [far_b, away_a], [away_b]]
        modes = ['both', 'both', 'both', 'own', 'own', 'own']
        close = [True, False, True, False, False, True]
        budget = [None, BUDGET, None, None, None, None]
        state = None
        for stage in range(len(plan)):
            state, out = pair_call(stage, n, plan, modes, close, budget, metas, arrays[stage], state,
                                   first=(mate_pos, spread(1), spread(0)) if stage == 0 else None,
                                   incoming=incoming if stage == len(plan) - 1 else None, split=stage == 2)
            if stage == 2:
                incoming = move(out[0], swap)
        forces, part = out
        return forces, total_energy(part, n)

    row_spec = P(('sys', 'row'), None)
    vec_spec = P(('sys', 'row'))
    step = jax.shard_map(body, mesh=mesh, in_specs=(row_spec, vec_spec, vec_spec), out_specs=(row_spec, P('sys')), check_vma=False)

    def program(positions, charges, counts):
        jax.eval_shape(step, positions, charges, counts)
        return step(positions, charges, counts)

    return program
```

time: 354 us -> 159 us (0.45)
  matrix products: 103 us -> 0 us
  waiting for transfers between devices: 139 us -> 44.3 us
  Pallas kernels: 0 us -> 75.5 us
  blocking collectives: 73.3 us -> 0 us
  other arithmetic: 17.6 us -> 1.09 us
  starting transfers between devices: 4.84 us -> 15.7 us
  local copies, waits for them, and re-layouts: 11.1 us -> 18.2 us
    dot_general x14 -> x0, matrix products: 103 us -> none  [the longest x5 53.1 us: pair_weight(): jnp.einsum('id,jd->ij', row_pos, col_pos, preferred_element_type=jnp.floa...]
    ppermute x12 -> x10, waiting for transfers between devices: 139 us -> 44.3 us  [move(): return lax.ppermute(x, 'row', perm)]
    pallas_call x0 -> x8, Pallas kernels: none -> 75.5 us  [the longest x1 34.1 us: exchange(): pl.pallas_call(functools.partial(exchange_kernel, n), out_shape=jax.Shape...]
    psum x1 -> x0, blocking collectives: 73.3 us -> none  [per_device(): energy = lax.psum(energy, 'row')]
    unnamed x6 -> x18, local copies, waits for them, and re-layouts: 0.01 us -> 13.2 us
    ppermute x12 -> x10, starting transfers between devices: 4.84 us -> 15.7 us  [move(): return lax.ppermute(x, 'row', perm)]
    add x2 -> x0, other arithmetic: 9.46 us -> none  [the longest x1 5.41 us: per_device(): own_force = own_force + lax.ppermute(vis_react, 'row', home_perm)]
    reduce_sum x6 -> x1, other arithmetic: 7.43 us -> 0.38 us  [body(): half = jnp.sum(pos_f32 * pos_f32, axis=1) * scale]
  transfers between devices with their start and end apart: 12 -> 10, of which waited for: 3 -> 2; matrix products, arithmetic and copies ran while one was open for 11% -> 4% of each run, Pallas kernels for 0% -> 32%
where the time goes in v1:
time: 159 us; the launch traced here: 158 us
  Pallas kernels  75.5 us (47%)
  waiting for transfers between devices  44.3 us (28%)
  local copies, waits for them, and re-layouts  18.2 us (11%)
  starting transfers between devices  15.7 us (10%)
  between operations  3.33 us (2%)
    ppermute x10, waiting for transfers between devices, move(): return lax.ppermute(x, 'row', perm)  44.3 us
    pallas_call x1, Pallas kernels, exchange(): pl.pallas_call(functools.partial(exchange_kernel, n), out_shape=jax.Shape...  34.1 us
    pallas_call x6, Pallas kernels, pair_call(): pl.pallas_call(functools.partial(pair_kernel, cfg), out_shape=out_shape,...  30.1 us
    ppermute x10, starting transfers between devices, move(): return lax.ppermute(x, 'row', perm)  15.7 us
    unnamed x18, local copies, waits for them, and re-layouts  13.2 us
    pallas_call x1, Pallas kernels, total_energy(): pl.pallas_call(functools.partial(energy_kernel, n), out_shape=jax.ShapeDt...  11.3 us
  transfers between devices with their start and end apart: 10, of which 2 were waited for; matrix products, arithmetic and copies ran while one was open for 4% of the time, Pallas kernels for 32%

profile of v1, /device:TPU:112, one launch (start us, length us, event | category | flops | bytes accessed | tf_op | source)
XLA Modules:
  0.0 158.1 jit_solution(195585914927853683)
XLA Ops:
  0.6 0.0 copy-start.4
  0.7 0.1 collective-permute-start.6
  0.8 2.8 %fusion.1 = (bf16[1024,384]{1,0:T(8,128)(2,1)}, bf16[1024,384]{1,0:T(8,128)(2,1)}) fusion(bf16[2048,384]{1,0:T(8,128)(2,1)} %refs_1_.1), kind=kLoop, calls=%fused_computation.9 | loop fusion | bytes 3145728 | tf_op jit(solution)/shard_map/slice | solution.py:271
  3.5 2.3 %collective-permute-start.4 = (bf16[1024,384]{1,0:T(8,128)(2,1)}, bf16[1024,384]{1,0:T(8,128)(2,1)S(1)}, u32[]{:S(2)}, u32[]{:S(2)}) collective-permute-start(bf16[1024,384]{1,0:T(8,128)(2,1)} %get-tuple-element.68), channel_id=1, source_target_pairs={{0,2},{1,7},{2,4},{3,1},{4,6},{5,3},{6,0},{7,5},{8,10},{9,15},{10,... | collective-permute-start | bytes 2359304 | tf_op jit(solution)/shard_map/ppermute | solution.py:257
  5.9 1.5 collective-permute-start.5
  7.4 0.5 collective-permute-start
  7.9 2.8 %collective-permute-start.3 = (bf16[1024,384]{1,0:T(8,128)(2,1)}, bf16[1024,384]{1,0:T(8,128)(2,1)}, u32[]{:S(2)}, u32[]{:S(2)}) collective-permute-start(bf16[1024,384]{1,0:T(8,128)(2,1)} %get-tuple-element.69), channel_id=1, source_target_pairs={{2,0},{7,1},{4,2},{1,3},{6,4},{3,5},{0,6},{5,7},{10,8},{15,9},{12,... | collective-permute-start | bytes 2359304 | tf_op jit(solution)/shard_map/ppermute | solution.py:257
  11.3 0.1 pad.6.clone
  11.4 0.1 pad.7.clone
  11.4 0.4 multiply_reduce_fusion
  11.9 0.7 maximum_maximum_fusion.src_ref
  12.5 34.1 %exchange.1.refs_0_ = f32[8,4,2048]{2,1,0:T(4,128)} custom-call(f32[4,2048]{1,0:T(4,128)} %maximum_maximum_fusion.src_ref), custom_call_target="tpu_custom_call" | custom-call | bytes 8388608 | tf_op jit(solution)/shard_map/exchange/pallas_call | solution.py:74
  46.7 0.9 constant_dynamic-slice_fusion.1
  47.6 0.6 broadcast_in_dim.18.refs_4_
  48.2 0.6 broadcast_in_dim.9.refs_3_
  48.9 1.4 copy-done.5
  50.3 4.8 %shard_map.50 = (bf16[4608,384]{1,0:T(8,128)(2,1)S(1)}, f32[4608,128]{1,0:T(8,128)S(1)}, f32[4608,128]{1,0:T(8,128)S(1)}, bf16[13824,384]{1,0:T(8,128)(2,1)S(1)}...) custom-call(f32[8,4,2048]{2,1,0:T(4,128)S(1)} %copy-done.6, bf16[2048,384]{1,0:T(8,128)(2,1)S(1)} %copy-done.5, ...), custom_call_target="tpu_custom_call" | custom-call | flops 1073741824 | bytes 1048576 | tf_op jit(solution)/shard_map/pallas_call | solution.py:237
  55.1 3.7 %copy-done = f32[4608,512]{1,0:T(8,128)} copy-done((f32[4608,512]{1,0:T(8,128)}, f32[4608,512]{1,0:T(8,128)S(1)}, u32[]{:S(2)}) %copy-start) | copy-done | bytes 9437208
  58.7 1.9 %copy-done.2 = bf16[4608,384]{1,0:T(8,128)(2,1)} copy-done((bf16[4608,384]{1,0:T(8,128)(2,1)}, bf16[4608,384]{1,0:T(8,128)(2,1)S(1)}, u32[]{:S(2)}) %copy-start.2) | copy-done | bytes 3538968
  60.6 3.7 %copy-done.1 = f32[4608,512]{1,0:T(8,128)S(1)} copy-done((f32[4608,512]{1,0:T(8,128)S(1)}, f32[4608,512]{1,0:T(8,128)}, u32[]{:S(2)}) %copy-start.1) | copy-done | bytes 9437208
  64.3 2.0 %copy-done.3 = bf16[4608,384]{1,0:T(8,128)(2,1)S(1)} copy-done((bf16[4608,384]{1,0:T(8,128)(2,1)S(1)}, bf16[4608,384]{1,0:T(8,128)(2,1)}, u32[]{:S(2)}) %copy-start.3) | copy-done | bytes 3538968
  66.3 6.5 %shard_map.51 = (bf16[4608,384]{1,0:T(8,128)(2,1)S(1)}, f32[4608,128]{1,0:T(8,128)S(1)}, f32[4608,128]{1,0:T(8,128)S(1)}, bf16[13824,384]{1,0:T(8,128)(2,1)S(1)}...) custom-call(f32[8,4,2048]{2,1,0:T(4,128)S(1)} %copy-done.6, ...), custom_call_target="tpu_custom_call", output_to_operand_aliasing={{0}: (3, {}), {1}: (4, {}), {2}: (5, {}), {3}: (6, {}), {4}... | custom-call | flops 1073741824 | bytes 1048576 | tf_op jit(solution)/shard_map/pallas_call | solution.py:237
  72.8 9.0 %shard_map.52 = (bf16[4608,384]{1,0:T(8,128)(2,1)S(1)}, f32[4608,128]{1,0:T(8,128)S(1)}, f32[4608,128]{1,0:T(8,128)S(1)}, bf16[13824,384]{1,0:T(8,128)(2,1)S(1)}...) custom-call(f32[8,4,2048]{2,1,0:T(4,128)S(1)} %copy-done.6, ...), custom_call_target="tpu_custom_call", output_to_operand_aliasing={{0}: (3, {}), {1}: (4, {}), {2}: (5, {}), {3}: (6, {}), {4}... | custom-call | flops 1073741824 | bytes 1048576 | tf_op jit(solution)/shard_map/pallas_call | solution.py:237
  81.8 0.4 collective-permute-start.7
  82.2 8.1 %collective-permute-start.1 = (bf16[1024,384]{1,0:T(8,128)(2,1)}, bf16[1024,384]{1,0:T(8,128)(2,1)S(1)}, u32[]{:S(2)}, u32[]{:S(2)}) collective-permute-start(bf16[1024,384]{1,0:T(8,128)(2,1)} %collective-permute-done.refs_1_), channel_id=1, source_target_pairs={{0,2},{1,7},{2,4},{3,1},{4,6},{5,3},{6,0},{7,5},{8,10},{9,15},{10,... | collective-permute-start | bytes 2359304 | tf_op jit(solution)/shard_map/ppermute | solution.py:257
  90.3 35.8 %collective-permute-done.8.refs_1_ = bf16[1024,384]{1,0:T(8,128)(2,1)S(1)} collective-permute-done((bf16[1024,384]{1,0:T(8,128)(2,1)S(1)}, bf16[1024,384]{1,0:T(8,128)(2,1)S(1)}, u32[]{:S(2)}, u32[]{:S(2)}) %collective-permute-start.8) | collective-permute-done | bytes 786464 | tf_op jit(solution)/shard_map/ppermute | solution.py:257
  126.1 8.4 %collective-permute-done.1.refs_1_ = bf16[1024,384]{1,0:T(8,128)(2,1)S(1)} collective-permute-done((bf16[1024,384]{1,0:T(8,128)(2,1)}, bf16[1024,384]{1,0:T(8,128)(2,1)S(1)}, u32[]{:S(2)}, u32[]{:S(2)}) %collective-permute-start.1) | collective-permute-done | bytes 786464 | tf_op jit(solution)/shard_map/ppermute | solution.py:257
  134.5 2.4 %shard_map.53 = (bf16[4608,384]{1,0:T(8,128)(2,1)S(1)}, f32[4608,128]{1,0:T(8,128)S(1)}, f32[4608,128]{1,0:T(8,128)S(1)}, bf16[13824,384]{1,0:T(8,128)(2,1)S(1)}...) custom-call(f32[8,4,2048]{2,1,0:T(4,128)S(1)} %copy-done.6, ...), custom_call_target="tpu_custom_call", output_to_operand_aliasing={{0}: (2, {}), {1}: (3, {}), {2}: (4, {}), {3}: (5, {}), {4}... | custom-call | flops 1073741824 | bytes 1048576 | tf_op jit(solution)/shard_map/pallas_call | solution.py:237
  137.0 2.4 %shard_map.54 = (bf16[4608,384]{1,0:T(8,128)(2,1)S(1)}, f32[4608,128]{1,0:T(8,128)S(1)}, f32[4608,128]{1,0:T(8,128)S(1)}, bf16[13824,384]{1,0:T(8,128)(2,1)S(1)}...) custom-call(f32[8,4,2048]{2,1,0:T(4,128)S(1)} %copy-done.6, ...), custom_call_target="tpu_custom_call", output_to_operand_aliasing={{0}: (3, {}), {1}: (4, {}), {2}: (5, {}), {3}: (6, {}), {4}... | custom-call | flops 1073741824 | bytes 1048576 | tf_op jit(solution)/shard_map/pallas_call | solution.py:237
  139.4 5.0 %shard_map.55 = (bf16[4608,384]{1,0:T(8,128)(2,1)S(1)}, f32[4608,128]{1,0:T(8,128)S(1)}, f32[4608,128]{1,0:T(8,128)S(1)}, bf16[13824,384]{1,0:T(8,128)(2,1)S(1)}...) custom-call(f32[8,4,2048]{2,1,0:T(4,128)S(1)} %copy-done.6, ...), custom_call_target="tpu_custom_call", output_to_operand_aliasing={{0}: (3, {}), {1}: (4, {}), {2}: (5, {}), {3}: (6, {}), {4}... | custom-call | flops 1073741824 | bytes 1048576 | tf_op jit(solution)/shard_map/pallas_call | solution.py:237
  144.4 0.6 copy-done.7
  145.0 11.3 %energy.1 = f32[1]{0:T(128)} custom-call(f32[8,128]{1,0:T(8,128)} %copy-done.7), custom_call_target="tpu_custom_call" | custom-call | tf_op jit(solution)/shard_map/energy/pallas_call | solution.py:42
  (26 shorter events, 0.1 us)
Async XLA Ops:
  0.6 10.8 %copy-start.4 = (bf16[2048,384]{1,0:T(8,128)(2,1)S(1)}, bf16[2048,384]{1,0:T(8,128)(2,1)}, u32[]{:S(2)}) copy-start(bf16[2048,384]{1,0:T(8,128)(2,1)} %refs_1_.1) | copy-start | bytes 4718596
  0.6 11.2 %copy-start.8 = (f32[2048]{0:T(1024)S(1)}, f32[2048]{0:T(1024)}, u32[]{:S(2)}) copy-start(f32[2048]{0:T(1024)} %param.4) | copy-start | bytes 24580
  0.7 47.0 %collective-permute-start.6 = (bf16[2048,384]{1,0:T(8,128)(2,1)}, bf16[2048,384]{1,0:T(8,128)(2,1)}, u32[]{:S(2)}, u32[]{:S(2)}) collective-permute-start(bf16[2048,384]{1,0:T(8,128)(2,1)} %refs_1_.1), channel_id=1, source_target_pairs={{0,1},{1,0},{2,3},{3,2},{4,5},{5,4},{6,7},{7,6},{8,9},{9,8},{10,11... | collective-permute-start | bytes 4718600 | tf_op jit(solution)/shard_map/ppermute | solution.py:257
  3.5 57.1 %collective-permute-start.4 = (bf16[1024,384]{1,0:T(8,128)(2,1)}, bf16[1024,384]{1,0:T(8,128)(2,1)S(1)}, u32[]{:S(2)}, u32[]{:S(2)}) collective-permute-start(bf16[1024,384]{1,0:T(8,128)(2,1)} %get-tuple-element.68), channel_id=1, source_target_pairs={{0,2},{1,7},{2,4},{3,1},{4,6},{5,3},{6,0},{7,5},{8,10},{9,15},{10,... | collective-permute-start | bytes 2359304 | tf_op jit(solution)/shard_map/ppermute | solution.py:257
  5.9 54.7 %collective-permute-start.5 = (bf16[1024,384]{1,0:T(8,128)(2,1)}, bf16[1024,384]{1,0:T(8,128)(2,1)}, u32[]{:S(2)}, u32[]{:S(2)}) collective-permute-start(bf16[1024,384]{1,0:T(8,128)(2,1)} %get-tuple-element.68), channel_id=1, source_target_pairs={{2,0},{7,1},{4,2},{1,3},{6,4},{3,5},{0,6},{5,7},{10,8},{15,9},{12,... | collective-permute-start | bytes 2359304 | tf_op jit(solution)/shard_map/ppermute | solution.py:257
  7.4 65.4 %collective-permute-start = (bf16[1024,384]{1,0:T(8,128)(2,1)}, bf16[1024,384]{1,0:T(8,128)(2,1)}, u32[]{:S(2)}, u32[]{:S(2)}) collective-permute-start(bf16[1024,384]{1,0:T(8,128)(2,1)} %get-tuple-element.69), channel_id=1, source_target_pairs={{0,2},{1,7},{2,4},{3,1},{4,6},{5,3},{6,0},{7,5},{8,10},{9,15},{10,... | collective-permute-start | bytes 2359304 | tf_op jit(solution)/shard_map/ppermute | solution.py:257
  7.9 64.9 %collective-permute-start.3 = (bf16[1024,384]{1,0:T(8,128)(2,1)}, bf16[1024,384]{1,0:T(8,128)(2,1)}, u32[]{:S(2)}, u32[]{:S(2)}) collective-permute-start(bf16[1024,384]{1,0:T(8,128)(2,1)} %get-tuple-element.69), channel_id=1, source_target_pairs={{2,0},{7,1},{4,2},{1,3},{6,4},{3,5},{0,6},{5,7},{10,8},{15,9},{12,... | collective-permute-start | bytes 2359304 | tf_op jit(solution)/shard_map/ppermute | solution.py:257
  46.7 2.2 %copy-start.6 = (f32[8,4,2048]{2,1,0:T(4,128)S(1)}, f32[8,4,2048]{2,1,0:T(4,128)}, u32[]{:S(2)}) copy-start(f32[8,4,2048]{2,1,0:T(4,128)} %exchange.1.refs_0_) | copy-start | bytes 786436
  48.8 1.4 copy-start.5
  55.1 3.7 %copy-start = (f32[4608,512]{1,0:T(8,128)}, f32[4608,512]{1,0:T(8,128)S(1)}, u32[]{:S(2)}) copy-start(f32[4608,512]{1,0:T(8,128)S(1)} %get-tuple-element.40.refs_8_) | copy-start | bytes 28311556
  58.7 1.9 %copy-start.2 = (bf16[4608,384]{1,0:T(8,128)(2,1)}, bf16[4608,384]{1,0:T(8,128)(2,1)S(1)}, u32[]{:S(2)}) copy-start(bf16[4608,384]{1,0:T(8,128)(2,1)S(1)} %get-tuple-element.35.refs_3_) | copy-start | bytes 10616836
  60.6 3.7 %copy-start.1 = (f32[4608,512]{1,0:T(8,128)S(1)}, f32[4608,512]{1,0:T(8,128)}, u32[]{:S(2)}) copy-start(f32[4608,512]{1,0:T(8,128)} %copy-done) | copy-start | bytes 28311556
  64.3 2.0 %copy-start.3 = (bf16[4608,384]{1,0:T(8,128)(2,1)S(1)}, bf16[4608,384]{1,0:T(8,128)(2,1)}, u32[]{:S(2)}) copy-start(bf16[4608,384]{1,0:T(8,128)(2,1)} %copy-done.2) | copy-start | bytes 10616836
  81.8 57.6 %collective-permute-start.7 = (f32[2048,512]{1,0:T(8,128)}, f32[2048,512]{1,0:T(8,128)S(1)}, u32[]{:S(2)}, u32[]{:S(2)}) collective-permute-start(f32[2048,512]{1,0:T(8,128)} %get-tuple-element.47), channel_id=1, source_target_pairs={{0,1},{1,0},{2,3},{3,2},{4,5},{5,4},{6,7},{7,6},{8,9},{9,8},{10,11... | collective-permute-start | bytes 12582920 | tf_op jit(solution)/shard_map/ppermute | solution.py:257
  82.2 43.9 %collective-permute-start.8 = (bf16[1024,384]{1,0:T(8,128)(2,1)S(1)}, bf16[1024,384]{1,0:T(8,128)(2,1)S(1)}, u32[]{:S(2)}, u32[]{:S(2)}) collective-permute-start(bf16[1024,384]{1,0:T(8,128)(2,1)S(1)} %collective-permute-done.4.refs_1_), channel_id=1, source_target_pairs={{0,2},{1,7},{2,4},{3,1},{4,6},{5,3},{6,0},{7,5},{8,10},{9,15},{10,... | collective-permute-start | bytes 2359304 | tf_op jit(solution)/shard_map/ppermute | solution.py:257
  82.2 52.3 %collective-permute-start.1 = (bf16[1024,384]{1,0:T(8,128)(2,1)}, bf16[1024,384]{1,0:T(8,128)(2,1)S(1)}, u32[]{:S(2)}, u32[]{:S(2)}) collective-permute-start(bf16[1024,384]{1,0:T(8,128)(2,1)} %collective-permute-done.refs_1_), channel_id=1, source_target_pairs={{0,2},{1,7},{2,4},{3,1},{4,6},{5,3},{6,0},{7,5},{8,10},{9,15},{10,... | collective-permute-start | bytes 2359304 | tf_op jit(solution)/shard_map/ppermute | solution.py:257
  126.1 10.9 %collective-permute-start.9 = (bf16[1024,384]{1,0:T(8,128)(2,1)S(1)}, bf16[1024,384]{1,0:T(8,128)(2,1)S(1)}, u32[]{:S(2)}, u32[]{:S(2)}) collective-permute-start(bf16[1024,384]{1,0:T(8,128)(2,1)S(1)} %collective-permute-done.8.refs_1_), channel_id=1, source_target_pairs={{0,1},{1,0},{2,3},{3,2},{4,5},{5,4},{6,7},{7,6},{8,9},{9,8},{10,11... | collective-permute-start | bytes 2359304 | tf_op jit(solution)/shard_map/ppermute | solution.py:257
  134.5 4.9 %collective-permute-start.2 = (bf16[1024,384]{1,0:T(8,128)(2,1)S(1)}, bf16[1024,384]{1,0:T(8,128)(2,1)S(1)}, u32[]{:S(2)}, u32[]{:S(2)}) collective-permute-start(bf16[1024,384]{1,0:T(8,128)(2,1)S(1)} %collective-permute-done.1.refs_1_), channel_id=1, source_target_pairs={{0,1},{1,0},{2,3},{3,2},{4,5},{5,4},{6,7},{7,6},{8,9},{9,8},{10,11... | collective-permute-start | bytes 2359304 | tf_op jit(solution)/shard_map/ppermute | solution.py:257
  144.4 0.6 copy-start.7

commit v2 on v1

--- a/solution.py
+++ b/solution.py
@@ -10,9 +10,11 @@
 
 
 LANES = 128
-TILE_I = 512
+TILE_I = 256
 TILE_J = 512
-BUDGET = 20
+UNROLL = 4
+BUDGET = 38
+VMEM_MB = (8, 6, 9, 6, 6, 12)
 MESH = pl.DeviceIdType.MESH
 VMEM_SPEC = pl.BlockSpec(memory_space=pltpu.VMEM)
 
@@ -50,37 +52,65 @@
     )(part)
 
 
-def exchange_kernel(n, src_ref, out_ref, send_sem, recv_sem, local_sem):
+def exchange_kernel(n, scale, pos_ref, q_ref, count_ref, top_ref, bottom_ref, mate_ref, meta_out, x_buf, meta, send_sem, recv_sem, local_sem, pos_sem):
+    rows, width = pos_ref.shape
     me = lax.axis_index('row')
+    mate = me + 1 - 2 * lax.rem(me, 2)
     barrier = pltpu.get_barrier_semaphore()
     for off in range(1, n):
         pl.semaphore_signal(barrier, inc=1, device_id={'row': lax.rem(me + off, n)}, device_id_type=MESH)
-    own = pltpu.make_async_copy(src_ref, out_ref.at[me], local_sem)
-    own.start()
+    load = pltpu.make_async_copy(pos_ref, x_buf, local_sem.at[0])
+    load.start()
+    load.wait()
+    halves = [pltpu.make_async_copy(x_buf.at[pl.ds(0, rows // 2), :], top_ref, local_sem.at[0]),
+              pltpu.make_async_copy(x_buf.at[pl.ds(rows // 2, rows // 2), :], bottom_ref, local_sem.at[1])]
+    for copy in halves:
+        copy.start()
+    lane = lax.broadcasted_iota(jnp.int32, (1, LANES), 1)
+    for b in range(rows // LANES):
+        x = x_buf[b * LANES:(b + 1) * LANES, :].astype(jnp.float32)
+        x = x * x
+        part = x[:, :LANES]
+        for k in range(1, width // LANES):
+            part = part + x[:, k * LANES:(k + 1) * LANES]
+        meta[1, b:b + 1, :] = jnp.sum(part.T, axis=0, keepdims=True) * scale
+        meta[0, b:b + 1, :] = jnp.where(lane + b * LANES < count_ref[0], q_ref[b:b + 1, :], 0.0)
+    meta[2] = jnp.full(meta.shape[1:], count_ref[0], jnp.int32).astype(jnp.float32)
+    for copy in halves:
+        copy.wait()
     pl.semaphore_wait(barrier, n - 1)
-    copies = []
+    copies = [pltpu.make_async_remote_copy(src_ref=x_buf, dst_ref=mate_ref, send_sem=pos_sem.at[0], recv_sem=pos_sem.at[1],
+                                           device_id={'row': mate}, device_id_type=MESH)]
     for off in range(1, n):
         copies.append(pltpu.make_async_remote_copy(
-            src_ref=src_ref, dst_ref=out_ref.at[me], send_sem=send_sem.at[off - 1], recv_sem=recv_sem.at[off - 1],
+            src_ref=meta, dst_ref=meta_out.at[me], send_sem=send_sem.at[off - 1], recv_sem=recv_sem.at[off - 1],
             device_id={'row': lax.rem(me + off, n)}, device_id_type=MESH))
     for copy in copies:
         copy.start()
+    own = pltpu.make_async_copy(meta, meta_out.at[me], local_sem.at[2])
+    own.start()
     own.wait()
     for copy in copies:
         copy.wait()
 
 
-def exchange(src, n):
+def exchange(positions, charges, counts, n):
+    rows, width = positions.shape
+    hbm = pl.BlockSpec(memory_space=pltpu.HBM)
+    groups = rows // LANES
+    half = jax.ShapeDtypeStruct((rows // 2, width), positions.dtype)
     return pl.pallas_call(
-        functools.partial(exchange_kernel, n),
-        out_shape=jax.ShapeDtypeStruct((n,) + src.shape, src.dtype),
-        in_specs=[pl.BlockSpec(memory_space=pltpu.HBM)],
-        out_specs=pl.BlockSpec(memory_space=pltpu.HBM),
-        scratch_shapes=[pltpu.SemaphoreType.DMA((n - 1,)), pltpu.SemaphoreType.DMA((n - 1,)), pltpu.SemaphoreType.DMA],
-        compiler_params=pltpu.CompilerParams(collective_id=1, has_side_effects=True),
+        functools.partial(exchange_kernel, n, math.log2(math.e) * 0.5 / width),
+        out_shape=[half, half, jax.ShapeDtypeStruct((rows, width), positions.dtype), jax.ShapeDtypeStruct((n, 3, groups, LANES), jnp.float32)],
+        in_specs=[hbm, VMEM_SPEC, pl.BlockSpec(memory_space=pltpu.SMEM)],
+        out_specs=[hbm] * 4,
+        scratch_shapes=[pltpu.VMEM((rows, width), positions.dtype), pltpu.VMEM((3, groups, LANES), jnp.float32),
+                        pltpu.SemaphoreType.DMA((n - 1,)), pltpu.SemaphoreType.DMA((n - 1,)), pltpu.SemaphoreType.DMA((3,)),
+                        pltpu.SemaphoreType.DMA((2,))],
+        compiler_params=pltpu.CompilerParams(collective_id=1, has_side_effects=True, vmem_limit_bytes=6 << 20),
         cost_estimate=pl.CostEstimate(flops=0, bytes_accessed=8 << 20, transcendentals=0),
         name='exchange',
-    )(src)
+    )(positions, charges.reshape(groups, LANES), counts)
 
 
 def up(value, step):
@@ -92,14 +122,14 @@
     metas, refs = refs[0], refs[1:]
     loads, refs = refs[:len(cfg['loads'])], refs[len(cfg['loads']):]
     if cfg['stage'] == 0:
-        partner_pos, spread_h, spread_c, refs = refs[0], refs[1], refs[2], refs[3:]
+        mate_pos, refs = refs[0], refs[1:]
     if cfg['finish']:
         incoming, refs = refs[0], refs[1:]
     if cfg['stage'] > 0:
-        refs = refs[6:]
-    x_row, h_row_all, c_row_all, x_col, cols, sums = refs[:6]
+        refs = refs[7:]
+    x_row, h_row_all, c_row_all, x_col, cols, pulls, sums = refs[:7]
     gram_a, gram_b = refs[-2:]
-    extra = refs[6:-2]
+    extra = refs[7:-2]
 
     me = lax.axis_index('row')
     ahead = jnp.where(lax.rem(me, 2) == 0, n - 2, 2)
@@ -109,7 +139,7 @@
     names = []
     for stage in cfg['plan'][:cfg['stage'] + 1]:
         names += [c[0] for c in stage]
-    count = {k: jnp.max(metas[block_of[k], 2:3, 0:LANES]).astype(jnp.int32) for k in ['mate'] + sorted(set(names))}
+    count = {k: jnp.max(metas[block_of[k], 2, 0:1, :]).astype(jnp.int32) for k in ['mate'] + sorted(set(names))}
     tiles_own = pl.cdiv(count['own'], TILE_I)
     row_mate = pl.multiple_of(up(count['own'], LANES), LANES)
     tiles_both = pl.cdiv(row_mate + count['mate'], TILE_I)
@@ -123,7 +153,9 @@
                 at = pl.multiple_of(end, LANES)
                 x_col[pl.ds(at, size), :] = loads[k][...]
                 x_col[pl.ds(pl.multiple_of(at + size, LANES), TILE_J), :] = jnp.zeros((TILE_J, width), x_col.dtype)
-                cols[:, pl.ds(at, size)] = metas[block_of[name], 0:2, start:start + size]
+                for g in range(size // LANES):
+                    for m in range(2):
+                        cols[m:m + 1, pl.ds(pl.multiple_of(at + g * LANES, LANES), LANES)] = metas[block_of[name], m, pl.ds(start // LANES + g, 1), :]
                 cols[:, pl.ds(pl.multiple_of(at + size, LANES), TILE_J)] = jnp.zeros((2, TILE_J), jnp.float32)
             end = end + up(jnp.clip(count[name] - start, 0, size), LANES)
         tiles = tiles_own if mode == 'own' else tiles_both
@@ -139,12 +171,13 @@
 
     if cfg['stage'] == 0:
         sums[...] = jnp.zeros_like(sums)
-        x_row[0:rows, :] = loads[0][...]
-        h_row_all[0:rows, :] = spread_h[0:rows, :]
-        c_row_all[0:rows, :] = spread_c[0:rows, :]
-        x_row[pl.ds(row_mate, rows), :] = partner_pos[...]
-        h_row_all[pl.ds(row_mate, rows), :] = spread_h[rows:, :]
-        c_row_all[pl.ds(row_mate, rows), :] = spread_c[rows:, :]
+        pulls[...] = jnp.zeros_like(pulls)
+        for name, row0, src in (('own', 0, loads[0]), ('mate', row_mate, mate_pos)):
+            x_row[pl.ds(row0, rows), :] = src[...]
+            for g in range(rows // LANES):
+                at = pl.ds(pl.multiple_of(row0 + g * LANES, LANES), LANES)
+                c_row_all[at, :] = jnp.broadcast_to(metas[block_of[name], 0, g:g + 1, :], (LANES, LANES)).T
+                h_row_all[at, :] = jnp.broadcast_to(metas[block_of[name], 1, g:g + 1, :], (LANES, LANES)).T
 
     def decode(unit):
         at = jnp.minimum(unit, units - 1)
@@ -173,8 +206,9 @@
                 w = jnp.where(lax.broadcasted_iota(jnp.int32, (TILE_I, LANES), 0) - lax.broadcasted_iota(jnp.int32, (TILE_I, LANES), 1) == off, 0.0, w)
             total = w if total is None else total + w
             parts.append(w.astype(jnp.bfloat16))
-        sums[row, width:] += total
-        sums[row, :width] += jnp.dot(jnp.concatenate(parts, axis=1), x_col[col, :], preferred_element_type=jnp.float32)
+        sums[row, :] += total
+        pulls[:width, row] += lax.dot_general(x_col[col, :], jnp.concatenate(parts, axis=1), (((0,), (1,)), ((), ())),
+                                              preferred_element_type=jnp.float32)
 
     @pl.when(units > 0)
     def _():
@@ -182,38 +216,43 @@
         gram(first, gram_a)
 
         def step(p, pos):
-            mid = decode(2 * p + 1)
-            gram(mid, gram_b)
-            weigh(pos, gram_a)
-            nxt = decode(2 * p + 2)
-            gram(nxt, gram_a)
-            weigh(mid, gram_b)
-            return nxt
-
-        lax.fori_loop(0, pl.cdiv(units, 2), step, first)
+            for k in range(UNROLL):
+                nxt = decode(UNROLL * p + k + 1)
+                gram(nxt, (gram_a, gram_b)[(k + 1) % 2])
+                weigh(pos, (gram_a, gram_b)[k % 2])
+                pos = nxt
+            return pos
+
+        lax.fori_loop(0, pl.cdiv(units, UNROLL), step, first)
 
     if cfg['split']:
-        extra[0][...] = sums[pl.ds(row_mate, rows), :]
+        for g in range(rows // LANES):
+            at = pl.ds(pl.multiple_of(row_mate + g * LANES, LANES), LANES)
+            pulls[width:, at] = jnp.sum(sums[at, :].T.reshape(LANES // 8, 8, LANES), axis=0)
+        extra[0][...] = pulls[:, pl.ds(row_mate, rows)]
     if cfg['finish']:
         force, part = extra
         part[...] = jnp.zeros_like(part)
 
         def tile(i, carry):
-            at = pl.ds(pl.multiple_of(i * TILE_I, TILE_I), TILE_I)
-            live = lax.broadcasted_iota(jnp.int32, (TILE_I, LANES), 0) + i * TILE_I < count['own']
-            lanes = jnp.where(live, sums[at, width:] + incoming[at, width:], 0.0)
-            x = x_row[at, :].astype(jnp.float32)
-            value = (jnp.sum(lanes, axis=1, keepdims=True) * x - (sums[at, :width] + incoming[at, :width])) * cfg['inv_len2']
-            force[at, :] = jnp.where(live[:, :1], value, 0.0)
-            part[...] += jnp.sum(lanes.reshape(TILE_I // 8, 8, LANES), axis=0)
+            at = pl.ds(pl.multiple_of(i * LANES, LANES), LANES)
+            live = lax.broadcasted_iota(jnp.int32, (LANES, LANES), 0) + i * LANES < count['own']
+            lanes = jnp.where(live, sums[at, :], 0.0)
+            inc = jnp.where(lax.broadcasted_iota(jnp.int32, (8, LANES), 1) + i * LANES < count['own'], incoming[width:, at], 0.0)
+            total = jnp.sum(lanes, axis=1, keepdims=True) + jnp.broadcast_to(jnp.sum(inc, axis=0, keepdims=True), (LANES, LANES)).T
+            for k in range(width // LANES):
+                d = pl.ds(k * LANES, LANES)
+                value = total * x_row[at, d].astype(jnp.float32) - (pulls[d, at] + incoming[d, at]).T
+                force[at, d] = jnp.where(live, value * cfg['inv_len2'], 0.0)
+            part[...] += jnp.sum(lanes.reshape(LANES // 8, 8, LANES), axis=0) + inc
             return carry
 
-        lax.fori_loop(0, rows // TILE_I, tile, 0)
+        lax.fori_loop(0, rows // LANES, tile, 0)
 
 
 def pair_call(stage, n, plan, modes, close, budget, metas, chunks, state, first=None, incoming=None, split=False):
     width = chunks[0].shape[1]
-    rows = metas.shape[2]
+    rows = metas.shape[2] * metas.shape[3]
     tall = 2 * rows + TILE_I
     null = up(sum(c[2] for s in plan for c in s), TILE_J) + (len(plan) + 1) * TILE_J
     cfg = dict(rows=rows, width=width, n=n, null=null, stage=stage, plan=plan, modes=modes, close=close, budget=budget, loads=chunks,
@@ -229,9 +268,10 @@
             aliases[len(args)] = k
             args.append(a)
     out_shape = [pltpu.VMEM((tall, width), jnp.bfloat16), pltpu.VMEM((tall, LANES), jnp.float32), pltpu.VMEM((tall, LANES), jnp.float32),
-                 pltpu.VMEM((null, width), jnp.bfloat16), pltpu.VMEM((2, null + TILE_J), jnp.float32), pltpu.VMEM((tall, width + LANES), jnp.float32)]
+                 pltpu.VMEM((null, width), jnp.bfloat16), pltpu.VMEM((2, null + TILE_J), jnp.float32), pltpu.VMEM((width + 8, tall), jnp.float32),
+                 pltpu.VMEM((tall, LANES), jnp.float32)]
     if split:
-        out_shape.append(jax.ShapeDtypeStruct((rows, width + LANES), jnp.float32))
+        out_shape.append(jax.ShapeDtypeStruct((width + 8, rows), jnp.float32))
     if incoming is not None:
         out_shape += [jax.ShapeDtypeStruct((rows, width), jnp.float32), pltpu.VMEM((8, LANES), jnp.float32)]
     outs = pl.pallas_call(
@@ -241,10 +281,10 @@
         out_specs=[VMEM_SPEC] * len(out_shape),
         input_output_aliases=aliases,
         scratch_shapes=[pltpu.VMEM((TILE_I, TILE_J), jnp.float32)] * 2,
-        compiler_params=pltpu.CompilerParams(vmem_limit_bytes=18 << 20),
+        compiler_params=pltpu.CompilerParams(vmem_limit_bytes=(VMEM_MB[stage]) << 20),
         cost_estimate=pl.CostEstimate(flops=1 << 30, bytes_accessed=1 << 20, transcendentals=0),
     )(*args)
-    return list(outs[:6]), outs[6:]
+    return list(outs[:7]), outs[7:]
 
 
 def solution(mesh):
@@ -257,26 +297,14 @@
         return lax.ppermute(x, 'row', perm)
 
     def body(positions, charges, counts):
-        block_rows, width = positions.shape
+        block_rows, _ = positions.shape
         half_rows = block_rows // 2
-        scale = math.log2(math.e) * 0.5 / width
-
-        live_q = jnp.where(jnp.arange(block_rows) < counts[0], charges, 0.0)
-        pos_f32 = positions.astype(jnp.float32)
-        half = jnp.sum(pos_f32 * pos_f32, axis=1) * scale
-        meta = jnp.stack([live_q, half, jnp.broadcast_to(counts[0].astype(jnp.float32), live_q.shape), jnp.zeros_like(half)])
-        metas = exchange(meta, n)
-        mate = metas[lax.axis_index('row') ^ 1]
-
-        top, bottom = positions[:half_rows], positions[half_rows:]
-        mate_pos = move(positions, swap)
+
+        top, bottom, mate_pos, metas = exchange(positions, charges, counts, n)
         near_a, next_a = move(top, forth), move(top, back)
         near_b, next_b = move(bottom, forth), move(bottom, back)
         far_a, far_b = move(near_a, forth), move(near_b, forth)
         away_a, away_b = move(far_a, swap), move(far_b, swap)
-
-        def spread(k):
-            return jnp.broadcast_to(jnp.concatenate([meta[k], mate[k]])[:, None], (2 * block_rows, LANES))
 
         def upper(name):
             return name, 0, half_rows
@@ -293,7 +321,7 @@
         state = None
         for stage in range(len(plan)):
             state, out = pair_call(stage, n, plan, modes, close, budget, metas, arrays[stage], state,
-                                   first=(mate_pos, spread(1), spread(0)) if stage == 0 else None,
+                                   first=(mate_pos,) if stage == 0 else None,
                                    incoming=incoming if stage == len(plan) - 1 else None, split=stage == 2)
             if stage == 2:
                 incoming = move(out[0], swap)

time: 159 us -> 107 us (0.67)
  the two profiles are of different devices: /device:TPU:112 before, /device:TPU:121 now
where the time goes in v2:
time: 107 us
  Pallas kernels  55.3 us (52%)
  waiting for transfers between devices  35.2 us (33%)
  starting transfers between devices  9.6 us (9%)
  local copies, waits for them, and re-layouts  4.1 us (4%)
  between operations  3.08 us (3%)
    ppermute x9, waiting for transfers between devices, move(): return lax.ppermute(x, 'row', perm)  35.2 us
    pallas_call x6, Pallas kernels, pair_call(): pl.pallas_call(functools.partial(pair_kernel, cfg), out_shape=out_shape,...  34.3 us
    pallas_call x1, Pallas kernels, total_energy(): pl.pallas_call(functools.partial(energy_kernel, n), out_shape=jax.ShapeDt...  13.1 us
    ppermute x9, starting transfers between devices, move(): return lax.ppermute(x, 'row', perm)  9.6 us
    pallas_call x1, Pallas kernels, exchange(): pl.pallas_call(functools.partial(exchange_kernel, n, math.log2(math.e) *...  7.83 us
    unnamed x8, local copies, waits for them, and re-layouts  4.1 us
  transfers between devices with their start and end apart: 9, of which 6 were waited for; matrix products, arithmetic and copies ran while one was open for 0% of the time, Pallas kernels for 17%

profile of v2, /device:TPU:121, one launch (start us, length us, event | category | flops | bytes accessed | tf_op | source)
XLA Modules:
  0.0 107.2 jit_solution(5195365707690169427)
XLA Ops:
  1.3 0.0 copy-start
  1.3 1.4 %copy-done = bf16[2048,384]{1,0:T(8,128)(2,1)S(1)} copy-done((bf16[2048,384]{1,0:T(8,128)(2,1)S(1)}, bf16[2048,384]{1,0:T(8,128)(2,1)}, u32[]{:S(2)}) %copy-start) | copy-done | bytes 1572888
  2.7 0.0 copy-start.2
  2.7 0.7 copy-done.2
  3.4 7.8 %exchange.1 = (bf16[1024,384]{1,0:T(8,128)(2,1)S(1)}, bf16[1024,384]{1,0:T(8,128)(2,1)S(1)}, bf16[2048,384]{1,0:T(8,128)(2,1)S(1)}, f32[8,3,16,128]{3,2,1,0:T(8,128)S(1)}) custom-call(bf16[2048,384]{1,0:T(8,128)(2,1)S(1)} %copy-done, f32[16,128]{1,0:T(8,128)S(1)} %bitcast.1, s32[1]{0:T(128)S(6)} %copy.76.count_ref), custom_call_target="tpu_custom_call" | custom-call | bytes 8388608 | tf_op jit(solution)/shard_map/exchange/pallas_call | solution.py:102
  11.2 1.7 %collective-permute-start.4 = (bf16[1024,384]{1,0:T(8,128)(2,1)S(1)}, bf16[1024,384]{1,0:T(8,128)(2,1)S(1)}, u32[]{:S(2)}, u32[]{:S(2)}) collective-permute-start(bf16[1024,384]{1,0:T(8,128)(2,1)S(1)} %get-tuple-element.46), channel_id=1, source_target_pairs={{0,2},{1,7},{2,4},{3,1},{4,6},{5,3},{6,0},{7,5},{8,10},{9,15},{10,... | collective-permute-start | bytes 2359304 | tf_op jit(solution)/shard_map/ppermute | solution.py:297
  12.9 0.0 collective-permute-start.5
  12.9 2.7 %collective-permute-start = (bf16[1024,384]{1,0:T(8,128)(2,1)S(1)}, bf16[1024,384]{1,0:T(8,128)(2,1)S(1)}, u32[]{:S(2)}, u32[]{:S(2)}) collective-permute-start(bf16[1024,384]{1,0:T(8,128)(2,1)S(1)} %get-tuple-element.45), channel_id=1, source_target_pairs={{0,2},{1,7},{2,4},{3,1},{4,6},{5,3},{6,0},{7,5},{8,10},{9,15},{10,... | collective-permute-start | bytes 2359304 | tf_op jit(solution)/shard_map/ppermute | solution.py:297
  15.6 0.0 collective-permute-start.3
  15.6 1.4 %copy-done.1 = bf16[2048,384]{1,0:T(8,128)(2,1)S(1)} copy-done((bf16[2048,384]{1,0:T(8,128)(2,1)S(1)}, bf16[2048,384]{1,0:T(8,128)(2,1)}, u32[]{:S(2)}) %copy-start.1) | copy-done | bytes 1572888
  17.0 8.1 %shard_map.50 = (bf16[4352,384]{1,0:T(8,128)(2,1)S(1)}, f32[4352,128]{1,0:T(8,128)S(1)}, f32[4352,128]{1,0:T(8,128)S(1)}, bf16[13824,384]{1,0:T(8,128)(2,1)S(1)}...) custom-call(f32[8,3,16,128]{3,2,1,0:T(8,128)S(1)} %get-tuple-element.44.refs_0_, ...), custom_call_target="tpu_custom_call" | custom-call | flops 1073741824 | bytes 1048576 | tf_op jit(solution)/shard_map/pallas_call | solution.py:277
  25.1 4.7 %collective-permute-done.4.refs_1_ = bf16[1024,384]{1,0:T(8,128)(2,1)S(1)} collective-permute-done((bf16[1024,384]{1,0:T(8,128)(2,1)S(1)}, bf16[1024,384]{1,0:T(8,128)(2,1)S(1)}, u32[]{:S(2)}, u32[]{:S(2)}) %collective-permute-start.4) | collective-permute-done | bytes 786464 | tf_op jit(solution)/shard_map/ppermute | solution.py:297
  29.9 3.8 %collective-permute-done.5.refs_2_ = bf16[1024,384]{1,0:T(8,128)(2,1)S(1)} collective-permute-done((bf16[1024,384]{1,0:T(8,128)(2,1)S(1)}, bf16[1024,384]{1,0:T(8,128)(2,1)S(1)}, u32[]{:S(2)}, u32[]{:S(2)}) %collective-permute-start.5) | collective-permute-done | bytes 786464 | tf_op jit(solution)/shard_map/ppermute | solution.py:297
  33.7 6.1 %shard_map.51 = (bf16[4352,384]{1,0:T(8,128)(2,1)S(1)}, f32[4352,128]{1,0:T(8,128)S(1)}, f32[4352,128]{1,0:T(8,128)S(1)}, bf16[13824,384]{1,0:T(8,128)(2,1)S(1)}...) custom-call(f32[8,3,16,128]{3,2,1,0:T(8,128)S(1)} %get-tuple-element, ...), custom_call_target="tpu_custom_call", output_to_operand_aliasing={{0}: (3, {}), {1}: (4, {}), {2}: (5, {}), {3}: (6, {}), {4}... | custom-call | flops 1073741824 | bytes 1048576 | tf_op jit(solution)/shard_map/pallas_call | solution.py:277
  39.8 6.9 %collective-permute-done.refs_1_ = bf16[1024,384]{1,0:T(8,128)(2,1)S(1)} collective-permute-done((bf16[1024,384]{1,0:T(8,128)(2,1)S(1)}, bf16[1024,384]{1,0:T(8,128)(2,1)S(1)}, u32[]{:S(2)}, u32[]{:S(2)}) %collective-permute-start) | collective-permute-done | bytes 786464 | tf_op jit(solution)/shard_map/ppermute | solution.py:297
  46.7 2.8 %collective-permute-done.3.refs_2_ = bf16[1024,384]{1,0:T(8,128)(2,1)S(1)} collective-permute-done((bf16[1024,384]{1,0:T(8,128)(2,1)S(1)}, bf16[1024,384]{1,0:T(8,128)(2,1)S(1)}, u32[]{:S(2)}, u32[]{:S(2)}) %collective-permute-start.3) | collective-permute-done | bytes 786464 | tf_op jit(solution)/shard_map/ppermute | solution.py:297
  49.5 9.3 %shard_map.52 = (bf16[4352,384]{1,0:T(8,128)(2,1)S(1)}, f32[4352,128]{1,0:T(8,128)S(1)}, f32[4352,128]{1,0:T(8,128)S(1)}, bf16[13824,384]{1,0:T(8,128)(2,1)S(1)}...) custom-call(f32[8,3,16,128]{3,2,1,0:T(8,128)S(1)} %get-tuple-element, ...), custom_call_target="tpu_custom_call", output_to_operand_aliasing={{0}: (3, {}), {1}: (4, {}), {2}: (5, {}), {3}: (6, {}), {4}... | custom-call | flops 1073741824 | bytes 1048576 | tf_op jit(solution)/shard_map/pallas_call | solution.py:277
  58.8 0.1 collective-permute-start.6
  58.9 0.1 collective-permute-start.7
  59.0 0.1 collective-permute-start.1
  59.1 11.0 %collective-permute-done.7.refs_1_ = bf16[1024,384]{1,0:T(8,128)(2,1)S(1)} collective-permute-done((bf16[1024,384]{1,0:T(8,128)(2,1)S(1)}, bf16[1024,384]{1,0:T(8,128)(2,1)S(1)}, u32[]{:S(2)}, u32[]{:S(2)}) %collective-permute-start.7) | collective-permute-done | bytes 786464 | tf_op jit(solution)/shard_map/ppermute | solution.py:297
  70.1 2.5 %collective-permute-start.8 = (bf16[1024,384]{1,0:T(8,128)(2,1)S(1)}, bf16[1024,384]{1,0:T(8,128)(2,1)S(1)}, u32[]{:S(2)}, u32[]{:S(2)}) collective-permute-start(bf16[1024,384]{1,0:T(8,128)(2,1)S(1)} %collective-permute-done.7.refs_1_), channel_id=1, source_target_pairs={{0,1},{1,0},{2,3},{3,2},{4,5},{5,4},{6,7},{7,6},{8,9},{9,8},{10,11... | collective-permute-start | bytes 2359304 | tf_op jit(solution)/shard_map/ppermute | solution.py:297
  72.6 6.0 %collective-permute-done.1.refs_1_ = bf16[1024,384]{1,0:T(8,128)(2,1)S(1)} collective-permute-done((bf16[1024,384]{1,0:T(8,128)(2,1)S(1)}, bf16[1024,384]{1,0:T(8,128)(2,1)S(1)}, u32[]{:S(2)}, u32[]{:S(2)}) %collective-permute-start.1) | collective-permute-done | bytes 786464 | tf_op jit(solution)/shard_map/ppermute | solution.py:297
  78.6 2.5 %collective-permute-start.2 = (bf16[1024,384]{1,0:T(8,128)(2,1)S(1)}, bf16[1024,384]{1,0:T(8,128)(2,1)S(1)}, u32[]{:S(2)}, u32[]{:S(2)}) collective-permute-start(bf16[1024,384]{1,0:T(8,128)(2,1)S(1)} %collective-permute-done.1.refs_1_), channel_id=1, source_target_pairs={{0,1},{1,0},{2,3},{3,2},{4,5},{5,4},{6,7},{7,6},{8,9},{9,8},{10,11... | collective-permute-start | bytes 2359304 | tf_op jit(solution)/shard_map/ppermute | solution.py:297
  81.0 2.0 %shard_map.53 = (bf16[4352,384]{1,0:T(8,128)(2,1)S(1)}, f32[4352,128]{1,0:T(8,128)S(1)}, f32[4352,128]{1,0:T(8,128)S(1)}, bf16[13824,384]{1,0:T(8,128)(2,1)S(1)}...) custom-call(f32[8,3,16,128]{3,2,1,0:T(8,128)S(1)} %get-tuple-element, ...), custom_call_target="tpu_custom_call", output_to_operand_aliasing={{0}: (2, {}), {1}: (3, {}), {2}: (4, {}), {3}: (5, {}), {4}... | custom-call | flops 1073741824 | bytes 1048576 | tf_op jit(solution)/shard_map/pallas_call | solution.py:277
  83.0 0.0 collective-permute-done.8.refs_2_
  83.0 2.1 %shard_map.54 = (bf16[4352,384]{1,0:T(8,128)(2,1)S(1)}, f32[4352,128]{1,0:T(8,128)S(1)}, f32[4352,128]{1,0:T(8,128)S(1)}, bf16[13824,384]{1,0:T(8,128)(2,1)S(1)}...) custom-call(f32[8,3,16,128]{3,2,1,0:T(8,128)S(1)} %get-tuple-element, ...), custom_call_target="tpu_custom_call", output_to_operand_aliasing={{0}: (3, {}), {1}: (4, {}), {2}: (5, {}), {3}: (6, {}), {4}... | custom-call | flops 1073741824 | bytes 1048576 | tf_op jit(solution)/shard_map/pallas_call | solution.py:277
  85.1 0.0 collective-permute-done.2.refs_1_
  85.1 0.0 collective-permute-done.6.refs_2_
  85.1 6.6 %shard_map.55 = (bf16[4352,384]{1,0:T(8,128)(2,1)S(1)}, f32[4352,128]{1,0:T(8,128)S(1)}, f32[4352,128]{1,0:T(8,128)S(1)}, bf16[13824,384]{1,0:T(8,128)(2,1)S(1)}...) custom-call(f32[8,3,16,128]{3,2,1,0:T(8,128)S(1)} %get-tuple-element, ...), custom_call_target="tpu_custom_call", output_to_operand_aliasing={{0}: (3, {}), {1}: (4, {}), {2}: (5, {}), {3}: (6, {}), {4}... | custom-call | flops 1073741824 | bytes 1048576 | tf_op jit(solution)/shard_map/pallas_call | solution.py:277
  91.8 0.6 copy-done.3
  92.4 13.1 %energy.1 = f32[1]{0:T(128)} custom-call(f32[8,128]{1,0:T(8,128)} %copy-done.3), custom_call_target="tpu_custom_call" | custom-call | tf_op jit(solution)/shard_map/energy/pallas_call | solution.py:44
  (2 shorter events, 0.0 us)
Async XLA Ops:
  1.3 1.4 %copy-start = (bf16[2048,384]{1,0:T(8,128)(2,1)S(1)}, bf16[2048,384]{1,0:T(8,128)(2,1)}, u32[]{:S(2)}) copy-start(bf16[2048,384]{1,0:T(8,128)(2,1)} %refs_1_.1) | copy-start | bytes 4718596
  2.7 0.7 copy-start.2
  11.2 18.6 %collective-permute-start.4 = (bf16[1024,384]{1,0:T(8,128)(2,1)S(1)}, bf16[1024,384]{1,0:T(8,128)(2,1)S(1)}, u32[]{:S(2)}, u32[]{:S(2)}) collective-permute-start(bf16[1024,384]{1,0:T(8,128)(2,1)S(1)} %get-tuple-element.46), channel_id=1, source_target_pairs={{0,2},{1,7},{2,4},{3,1},{4,6},{5,3},{6,0},{7,5},{8,10},{9,15},{10,... | collective-permute-start | bytes 2359304 | tf_op jit(solution)/shard_map/ppermute | solution.py:297
  12.9 20.8 %collective-permute-start.5 = (bf16[1024,384]{1,0:T(8,128)(2,1)S(1)}, bf16[1024,384]{1,0:T(8,128)(2,1)S(1)}, u32[]{:S(2)}, u32[]{:S(2)}) collective-permute-start(bf16[1024,384]{1,0:T(8,128)(2,1)S(1)} %get-tuple-element.46), channel_id=1, source_target_pairs={{2,0},{7,1},{4,2},{1,3},{6,4},{3,5},{0,6},{5,7},{10,8},{15,9},{12,... | collective-permute-start | bytes 2359304 | tf_op jit(solution)/shard_map/ppermute | solution.py:297
  12.9 33.8 %collective-permute-start = (bf16[1024,384]{1,0:T(8,128)(2,1)S(1)}, bf16[1024,384]{1,0:T(8,128)(2,1)S(1)}, u32[]{:S(2)}, u32[]{:S(2)}) collective-permute-start(bf16[1024,384]{1,0:T(8,128)(2,1)S(1)} %get-tuple-element.45), channel_id=1, source_target_pairs={{0,2},{1,7},{2,4},{3,1},{4,6},{5,3},{6,0},{7,5},{8,10},{9,15},{10,... | collective-permute-start | bytes 2359304 | tf_op jit(solution)/shard_map/ppermute | solution.py:297
  15.6 33.9 %collective-permute-start.3 = (bf16[1024,384]{1,0:T(8,128)(2,1)S(1)}, bf16[1024,384]{1,0:T(8,128)(2,1)S(1)}, u32[]{:S(2)}, u32[]{:S(2)}) collective-permute-start(bf16[1024,384]{1,0:T(8,128)(2,1)S(1)} %get-tuple-element.45), channel_id=1, source_target_pairs={{2,0},{7,1},{4,2},{1,3},{6,4},{3,5},{0,6},{5,7},{10,8},{15,9},{12,... | collective-permute-start | bytes 2359304 | tf_op jit(solution)/shard_map/ppermute | solution.py:297
  15.6 1.4 %copy-start.1 = (bf16[2048,384]{1,0:T(8,128)(2,1)S(1)}, bf16[2048,384]{1,0:T(8,128)(2,1)}, u32[]{:S(2)}) copy-start(bf16[2048,384]{1,0:T(8,128)(2,1)} %refs_1_.1) | copy-start | bytes 4718596
  58.8 26.3 %collective-permute-start.6 = (f32[392,2048]{1,0:T(8,128)S(1)}, f32[392,2048]{1,0:T(8,128)S(1)}, u32[]{:S(2)}, u32[]{:S(2)}) collective-permute-start(f32[392,2048]{1,0:T(8,128)S(1)} %get-tuple-element.62), channel_id=1, source_target_pairs={{0,1},{1,0},{2,3},{3,2},{4,5},{5,4},{6,7},{7,6},{8,9},{9,8},{10,11... | collective-permute-start | bytes 9633800 | tf_op jit(solution)/shard_map/ppermute | solution.py:297
  58.9 11.2 %collective-permute-start.7 = (bf16[1024,384]{1,0:T(8,128)(2,1)S(1)}, bf16[1024,384]{1,0:T(8,128)(2,1)S(1)}, u32[]{:S(2)}, u32[]{:S(2)}) collective-permute-start(bf16[1024,384]{1,0:T(8,128)(2,1)S(1)} %collective-permute-done.4.refs_1_), channel_id=1, source_target_pairs={{0,2},{1,7},{2,4},{3,1},{4,6},{5,3},{6,0},{7,5},{8,10},{9,15},{10,... | collective-permute-start | bytes 2359304 | tf_op jit(solution)/shard_map/ppermute | solution.py:297
  59.0 19.5 %collective-permute-start.1 = (bf16[1024,384]{1,0:T(8,128)(2,1)S(1)}, bf16[1024,384]{1,0:T(8,128)(2,1)S(1)}, u32[]{:S(2)}, u32[]{:S(2)}) collective-permute-start(bf16[1024,384]{1,0:T(8,128)(2,1)S(1)} %collective-permute-done.refs_1_), channel_id=1, source_target_pairs={{0,2},{1,7},{2,4},{3,1},{4,6},{5,3},{6,0},{7,5},{8,10},{9,15},{10,... | collective-permute-start | bytes 2359304 | tf_op jit(solution)/shard_map/ppermute | solution.py:297
  70.1 12.9 %collective-permute-start.8 = (bf16[1024,384]{1,0:T(8,128)(2,1)S(1)}, bf16[1024,384]{1,0:T(8,128)(2,1)S(1)}, u32[]{:S(2)}, u32[]{:S(2)}) collective-permute-start(bf16[1024,384]{1,0:T(8,128)(2,1)S(1)} %collective-permute-done.7.refs_1_), channel_id=1, source_target_pairs={{0,1},{1,0},{2,3},{3,2},{4,5},{5,4},{6,7},{7,6},{8,9},{9,8},{10,11... | collective-permute-start | bytes 2359304 | tf_op jit(solution)/shard_map/ppermute | solution.py:297
  78.6 6.6 %collective-permute-start.2 = (bf16[1024,384]{1,0:T(8,128)(2,1)S(1)}, bf16[1024,384]{1,0:T(8,128)(2,1)S(1)}, u32[]{:S(2)}, u32[]{:S(2)}) collective-permute-start(bf16[1024,384]{1,0:T(8,128)(2,1)S(1)} %collective-permute-done.1.refs_1_), channel_id=1, source_target_pairs={{0,1},{1,0},{2,3},{3,2},{4,5},{5,4},{6,7},{7,6},{8,9},{9,8},{10,11... | collective-permute-start | bytes 2359304 | tf_op jit(solution)/shard_map/ppermute | solution.py:297
  91.8 0.6 copy-start.3

commit v3 on v2

--- a/solution.py
+++ b/solution.py
@@ -14,16 +14,19 @@
 TILE_J = 512
 UNROLL = 4
 BUDGET = 38
-VMEM_MB = (8, 6, 9, 6, 6, 12)
+VMEM_MB = (5, 6, 9, 5, 5, 5, 11)
 MESH = pl.DeviceIdType.MESH
 VMEM_SPEC = pl.BlockSpec(memory_space=pltpu.VMEM)
 
 
-def energy_kernel(n, part_ref, out_ref, seen, send_sem, recv_sem):
+def energy_kernel(n, part_hbm, out_ref, seen, part_ref, send_sem, recv_sem, local_sem):
     me = lax.axis_index('row')
     barrier = pltpu.get_barrier_semaphore()
     for off in range(1, n):
         pl.semaphore_signal(barrier, inc=1, device_id={'row': lax.rem(me + off, n)}, device_id_type=MESH)
+    load = pltpu.make_async_copy(part_hbm, part_ref, local_sem)
+    load.start()
+    load.wait()
     pl.semaphore_wait(barrier, n - 1)
     copies = []
     for off in range(1, n):
@@ -34,7 +37,7 @@
         copy.start()
     for copy in copies:
         copy.wait()
-    total = jnp.zeros_like(part_ref)
+    total = jnp.zeros(part_ref.shape, jnp.float32)
     for k in range(n):
         total += jnp.where(me == k, part_ref[...], seen[k])
     out_ref[0] = 0.5 * jnp.sum(total)
@@ -44,18 +47,18 @@
     return pl.pallas_call(
         functools.partial(energy_kernel, n),
         out_shape=jax.ShapeDtypeStruct((1,), jnp.float32),
-        in_specs=[VMEM_SPEC],
+        in_specs=[pl.BlockSpec(memory_space=pltpu.HBM)],
         out_specs=pl.BlockSpec(memory_space=pltpu.SMEM),
-        scratch_shapes=[pltpu.VMEM((n,) + part.shape, jnp.float32), pltpu.SemaphoreType.DMA((n - 1,)), pltpu.SemaphoreType.DMA((n - 1,))],
+        scratch_shapes=[pltpu.VMEM((n,) + part.shape, jnp.float32), pltpu.VMEM(part.shape, jnp.float32), pltpu.SemaphoreType.DMA((n - 1,)),
+                        pltpu.SemaphoreType.DMA((n - 1,)), pltpu.SemaphoreType.DMA],
         compiler_params=pltpu.CompilerParams(collective_id=0, has_side_effects=True),
         name='energy',
     )(part)
 
 
-def exchange_kernel(n, scale, pos_ref, q_ref, count_ref, top_ref, bottom_ref, mate_ref, meta_out, x_buf, meta, send_sem, recv_sem, local_sem, pos_sem):
+def exchange_kernel(n, scale, pos_ref, q_ref, count_ref, top_ref, bottom_ref, meta_out, x_buf, meta, send_sem, recv_sem, local_sem):
     rows, width = pos_ref.shape
     me = lax.axis_index('row')
-    mate = me + 1 - 2 * lax.rem(me, 2)
     barrier = pltpu.get_barrier_semaphore()
     for off in range(1, n):
         pl.semaphore_signal(barrier, inc=1, device_id={'row': lax.rem(me + off, n)}, device_id_type=MESH)
@@ -76,11 +79,8 @@
         meta[1, b:b + 1, :] = jnp.sum(part.T, axis=0, keepdims=True) * scale
         meta[0, b:b + 1, :] = jnp.where(lane + b * LANES < count_ref[0], q_ref[b:b + 1, :], 0.0)
     meta[2] = jnp.full(meta.shape[1:], count_ref[0], jnp.int32).astype(jnp.float32)
-    for copy in halves:
-        copy.wait()
     pl.semaphore_wait(barrier, n - 1)
-    copies = [pltpu.make_async_remote_copy(src_ref=x_buf, dst_ref=mate_ref, send_sem=pos_sem.at[0], recv_sem=pos_sem.at[1],
-                                           device_id={'row': mate}, device_id_type=MESH)]
+    copies = []
     for off in range(1, n):
         copies.append(pltpu.make_async_remote_copy(
             src_ref=meta, dst_ref=meta_out.at[me], send_sem=send_sem.at[off - 1], recv_sem=recv_sem.at[off - 1],
@@ -90,7 +90,7 @@
     own = pltpu.make_async_copy(meta, meta_out.at[me], local_sem.at[2])
     own.start()
     own.wait()
-    for copy in copies:
+    for copy in halves + copies:
         copy.wait()
 
 
@@ -101,12 +101,11 @@
     half = jax.ShapeDtypeStruct((rows // 2, width), positions.dtype)
     return pl.pallas_call(
         functools.partial(exchange_kernel, n, math.log2(math.e) * 0.5 / width),
-        out_shape=[half, half, jax.ShapeDtypeStruct((rows, width), positions.dtype), jax.ShapeDtypeStruct((n, 3, groups, LANES), jnp.float32)],
+        out_shape=[half, half, jax.ShapeDtypeStruct((n, 3, groups, LANES), jnp.float32)],
         in_specs=[hbm, VMEM_SPEC, pl.BlockSpec(memory_space=pltpu.SMEM)],
-        out_specs=[hbm] * 4,
+        out_specs=[hbm] * 3,
         scratch_shapes=[pltpu.VMEM((rows, width), positions.dtype), pltpu.VMEM((3, groups, LANES), jnp.float32),
-                        pltpu.SemaphoreType.DMA((n - 1,)), pltpu.SemaphoreType.DMA((n - 1,)), pltpu.SemaphoreType.DMA((3,)),
-                        pltpu.SemaphoreType.DMA((2,))],
+                        pltpu.SemaphoreType.DMA((n - 1,)), pltpu.SemaphoreType.DMA((n - 1,)), pltpu.SemaphoreType.DMA((3,))],
         compiler_params=pltpu.CompilerParams(collective_id=1, has_side_effects=True, vmem_limit_bytes=6 << 20),
         cost_estimate=pl.CostEstimate(flops=0, bytes_accessed=8 << 20, transcendentals=0),
         name='exchange',
@@ -123,6 +122,8 @@
     loads, refs = refs[:len(cfg['loads'])], refs[len(cfg['loads']):]
     if cfg['stage'] == 0:
         mate_pos, refs = refs[0], refs[1:]
+        copy_sem = refs[-3]
+        refs = refs[:-3] + refs[-2:]
     if cfg['finish']:
         incoming, refs = refs[0], refs[1:]
     if cfg['stage'] > 0:
@@ -151,7 +152,8 @@
         for k, (name, start, size) in enumerate(chunks):
             if stage == cfg['stage']:
                 at = pl.multiple_of(end, LANES)
-                x_col[pl.ds(at, size), :] = loads[k][...]
+                if stage > 0:
+                    x_col[pl.ds(at, size), :] = loads[k][...]
                 x_col[pl.ds(pl.multiple_of(at + size, LANES), TILE_J), :] = jnp.zeros((TILE_J, width), x_col.dtype)
                 for g in range(size // LANES):
                     for m in range(2):
@@ -170,14 +172,22 @@
     units = n_j * tiles
 
     if cfg['stage'] == 0:
+        copies = [pltpu.make_async_copy(loads[0], x_row.at[pl.ds(0, rows), :], copy_sem.at[0]),
+                  pltpu.make_async_copy(loads[0], x_col.at[pl.ds(0, rows), :], copy_sem.at[1]),
+                  pltpu.make_async_copy(mate_pos, x_row.at[pl.ds(row_mate, rows), :], copy_sem.at[2])]
+        for copy in copies[:2]:
+            copy.start()
         sums[...] = jnp.zeros_like(sums)
         pulls[...] = jnp.zeros_like(pulls)
-        for name, row0, src in (('own', 0, loads[0]), ('mate', row_mate, mate_pos)):
-            x_row[pl.ds(row0, rows), :] = src[...]
+        for name, row0 in (('own', 0), ('mate', row_mate)):
             for g in range(rows // LANES):
                 at = pl.ds(pl.multiple_of(row0 + g * LANES, LANES), LANES)
                 c_row_all[at, :] = jnp.broadcast_to(metas[block_of[name], 0, g:g + 1, :], (LANES, LANES)).T
                 h_row_all[at, :] = jnp.broadcast_to(metas[block_of[name], 1, g:g + 1, :], (LANES, LANES)).T
+        copies[0].wait()
+        copies[2].start()
+        copies[1].wait()
+        copies[2].wait()
 
     def decode(unit):
         at = jnp.minimum(unit, units - 1)
@@ -247,7 +257,7 @@
             part[...] += jnp.sum(lanes.reshape(LANES // 8, 8, LANES), axis=0) + inc
             return carry
 
-        lax.fori_loop(0, rows // LANES, tile, 0)
+        lax.fori_loop(0, rows // LANES, tile, 0, unroll=4)
 
 
 def pair_call(stage, n, plan, modes, close, budget, metas, chunks, state, first=None, incoming=None, split=False):
@@ -273,14 +283,14 @@
     if split:
         out_shape.append(jax.ShapeDtypeStruct((width + 8, rows), jnp.float32))
     if incoming is not None:
-        out_shape += [jax.ShapeDtypeStruct((rows, width), jnp.float32), pltpu.VMEM((8, LANES), jnp.float32)]
+        out_shape += [jax.ShapeDtypeStruct((rows, width), jnp.float32), jax.ShapeDtypeStruct((8, LANES), jnp.float32)]
     outs = pl.pallas_call(
         functools.partial(pair_kernel, cfg),
         out_shape=out_shape,
-        in_specs=[VMEM_SPEC] * len(args),
+        in_specs=[VMEM_SPEC] + [VMEM_SPEC if stage else pl.BlockSpec(memory_space=pltpu.HBM)] * (len(args) - 1),
         out_specs=[VMEM_SPEC] * len(out_shape),
         input_output_aliases=aliases,
-        scratch_shapes=[pltpu.VMEM((TILE_I, TILE_J), jnp.float32)] * 2,
+        scratch_shapes=([] if stage else [pltpu.SemaphoreType.DMA((3,))]) + [pltpu.VMEM((TILE_I, TILE_J), jnp.float32)] * 2,
         compiler_params=pltpu.CompilerParams(vmem_limit_bytes=(VMEM_MB[stage]) << 20),
         cost_estimate=pl.CostEstimate(flops=1 << 30, bytes_accessed=1 << 20, transcendentals=0),
     )(*args)
@@ -300,7 +310,8 @@
         block_rows, _ = positions.shape
         half_rows = block_rows // 2
 
-        top, bottom, mate_pos, metas = exchange(positions, charges, counts, n)
+        mate_pos = move(positions, swap)
+        top, bottom, metas = exchange(positions, charges, counts, n)
         near_a, next_a = move(top, forth), move(top, back)
         near_b, next_b = move(bottom, forth), move(bottom, back)
         far_a, far_b = move(near_a, forth), move(near_b, forth)
@@ -313,11 +324,11 @@
             return name, half_rows, block_rows - half_rows
 
         plan = [[('own', 0, block_rows)], [upper('near'), upper('next')], [lower('near'), lower('next')],
-                [upper('far')], [lower('far'), upper('away')], [lower('away')]]
-        arrays = [[positions], [near_a, next_a], [near_b, next_b], [far_a], [far_b, away_a], [away_b]]
-        modes = ['both', 'both', 'both', 'own', 'own', 'own']
-        close = [True, False, True, False, False, True]
-        budget = [None, BUDGET, None, None, None, None]
+                [upper('far')], [upper('away')], [lower('far')], [lower('away')]]
+        arrays = [[positions], [near_a, next_a], [near_b, next_b], [far_a], [away_a], [far_b], [away_b]]
+        modes = ['both', 'both', 'both', 'own', 'own', 'own', 'own']
+        close = [True, False, True, False, False, False, True]
+        budget = [None, BUDGET, None, None, None, None, None]
         state = None
         for stage in range(len(plan)):
             state, out = pair_call(stage, n, plan, modes, close, budget, metas, arrays[stage], state,

time: 107 us -> 106 us (level)
  Pallas kernels: 55.3 us -> 52.4 us
    pallas_call x6 -> x7, Pallas kernels: 34.3 us -> 32.9 us  [pair_call(): pl.pallas_call(functools.partial(pair_kernel, cfg), out_shape=out_shape,...]
    ppermute x9 -> x10, starting transfers between devices: 9.6 us -> 10.3 us  [move(): return lax.ppermute(x, 'row', perm)]
    ppermute x9 -> x10, waiting for transfers between devices: 35.2 us -> 35.4 us  [move(): return lax.ppermute(x, 'row', perm)]
  transfers between devices with their start and end apart: 9 -> 10, of which waited for: 6 -> 6; matrix products, arithmetic and copies ran while one was open for 0% -> 0% of each run, Pallas kernels for 17% -> 24%
where the time goes in v3:
time: 106 us; the launch traced here: 105 us
  Pallas kernels  52.4 us (49%)
  waiting for transfers between devices  35.4 us (33%)
  starting transfers between devices  10.3 us (10%)
  local copies, waits for them, and re-layouts  4.09 us (4%)
  between operations  3.17 us (3%)
    ppermute x10, waiting for transfers between devices, move(): return lax.ppermute(x, 'row', perm)  35.4 us
    pallas_call x7, Pallas kernels, pair_call(): pl.pallas_call(functools.partial(pair_kernel, cfg), out_shape=out_shape,...  32.9 us
    pallas_call x1, Pallas kernels, total_energy(): pl.pallas_call(functools.partial(energy_kernel, n), out_shape=jax.ShapeDt...  12.2 us
    ppermute x10, starting transfers between devices, move(): return lax.ppermute(x, 'row', perm)  10.3 us
    pallas_call x1, Pallas kernels, exchange(): pl.pallas_call(functools.partial(exchange_kernel, n, math.log2(math.e) *...  7.31 us
    unnamed x8, local copies, waits for them, and re-layouts  4.09 us
  transfers between devices with their start and end apart: 10, of which 6 were waited for; matrix products, arithmetic and copies ran while one was open for 0% of the time, Pallas kernels for 24%

profile of v3, /device:TPU:121, one launch (start us, length us, event | category | flops | bytes accessed | tf_op | source)
XLA Modules:
  0.0 105.3 jit_solution(5392274268343273474)
XLA Ops:
  0.6 0.7 collective-permute-start.6
  2.0 1.4 %copy-done = bf16[2048,384]{1,0:T(8,128)(2,1)S(1)} copy-done((bf16[2048,384]{1,0:T(8,128)(2,1)S(1)}, bf16[2048,384]{1,0:T(8,128)(2,1)}, u32[]{:S(2)}) %copy-start) | copy-done | bytes 1572888
  3.4 0.7 copy-done.2
  4.1 7.3 %exchange.1 = (bf16[1024,384]{1,0:T(8,128)(2,1)S(1)}, bf16[1024,384]{1,0:T(8,128)(2,1)S(1)}, f32[8,3,16,128]{3,2,1,0:T(8,128)S(1)}) custom-call(bf16[2048,384]{1,0:T(8,128)(2,1)S(1)} %copy-done, f32[16,128]{1,0:T(8,128)S(1)} %bitcast.1, s32[1]{0:T(128)S(6)} %copy.90.count_ref), custom_call_target="tpu_custom_call" | custom-call | bytes 8388608 | tf_op jit(solution)/shard_map/exchange/pallas_call | solution.py:102
  11.4 1.7 %collective-permute-start.4 = (bf16[1024,384]{1,0:T(8,128)(2,1)S(1)}, bf16[1024,384]{1,0:T(8,128)(2,1)S(1)}, u32[]{:S(2)}, u32[]{:S(2)}) collective-permute-start(bf16[1024,384]{1,0:T(8,128)(2,1)S(1)} %get-tuple-element.52), channel_id=1, source_target_pairs={{0,2},{1,7},{2,4},{3,1},{4,6},{5,3},{6,0},{7,5},{8,10},{9,15},{10,... | collective-permute-start | bytes 2359304 | tf_op jit(solution)/shard_map/ppermute | solution.py:307
  13.1 0.0 collective-permute-start.5
  13.1 2.7 %collective-permute-start = (bf16[1024,384]{1,0:T(8,128)(2,1)S(1)}, bf16[1024,384]{1,0:T(8,128)(2,1)S(1)}, u32[]{:S(2)}, u32[]{:S(2)}) collective-permute-start(bf16[1024,384]{1,0:T(8,128)(2,1)S(1)} %get-tuple-element.51), channel_id=1, source_target_pairs={{0,2},{1,7},{2,4},{3,1},{4,6},{5,3},{6,0},{7,5},{8,10},{9,15},{10,... | collective-permute-start | bytes 2359304 | tf_op jit(solution)/shard_map/ppermute | solution.py:307
  15.8 0.0 collective-permute-start.3
  15.8 0.0 collective-permute-done.6.refs_2_
  15.8 1.4 %copy-done.1 = bf16[2048,384]{1,0:T(8,128)(2,1)S(1)} copy-done((bf16[2048,384]{1,0:T(8,128)(2,1)S(1)}, bf16[2048,384]{1,0:T(8,128)(2,1)}, u32[]{:S(2)}) %copy-start.1) | copy-done | bytes 1572888
  17.2 8.1 %shard_map.50 = (bf16[4352,384]{1,0:T(8,128)(2,1)S(1)}, f32[4352,128]{1,0:T(8,128)S(1)}, f32[4352,128]{1,0:T(8,128)S(1)}, bf16[14336,384]{1,0:T(8,128)(2,1)S(1)}...) custom-call(f32[8,3,16,128]{3,2,1,0:T(8,128)S(1)} %get-tuple-element.50.refs_0_, ...), custom_call_target="tpu_custom_call" | custom-call | flops 1073741824 | bytes 1048576 | tf_op jit(solution)/shard_map/pallas_call | solution.py:287
  25.2 4.8 %collective-permute-done.4.refs_1_ = bf16[1024,384]{1,0:T(8,128)(2,1)S(1)} collective-permute-done((bf16[1024,384]{1,0:T(8,128)(2,1)S(1)}, bf16[1024,384]{1,0:T(8,128)(2,1)S(1)}, u32[]{:S(2)}, u32[]{:S(2)}) %collective-permute-start.4) | collective-permute-done | bytes 786464 | tf_op jit(solution)/shard_map/ppermute | solution.py:307
  30.0 3.8 %collective-permute-done.5.refs_2_ = bf16[1024,384]{1,0:T(8,128)(2,1)S(1)} collective-permute-done((bf16[1024,384]{1,0:T(8,128)(2,1)S(1)}, bf16[1024,384]{1,0:T(8,128)(2,1)S(1)}, u32[]{:S(2)}, u32[]{:S(2)}) %collective-permute-start.5) | collective-permute-done | bytes 786464 | tf_op jit(solution)/shard_map/ppermute | solution.py:307
  33.9 5.9 %shard_map.51 = (bf16[4352,384]{1,0:T(8,128)(2,1)S(1)}, f32[4352,128]{1,0:T(8,128)S(1)}, f32[4352,128]{1,0:T(8,128)S(1)}, bf16[14336,384]{1,0:T(8,128)(2,1)S(1)}...) custom-call(f32[8,3,16,128]{3,2,1,0:T(8,128)S(1)} %get-tuple-element, ...), custom_call_target="tpu_custom_call", output_to_operand_aliasing={{0}: (3, {}), {1}: (4, {}), {2}: (5, {}), {3}: (6, {}), {4}... | custom-call | flops 1073741824 | bytes 1048576 | tf_op jit(solution)/shard_map/pallas_call | solution.py:287
  39.8 7.1 %collective-permute-done.refs_1_ = bf16[1024,384]{1,0:T(8,128)(2,1)S(1)} collective-permute-done((bf16[1024,384]{1,0:T(8,128)(2,1)S(1)}, bf16[1024,384]{1,0:T(8,128)(2,1)S(1)}, u32[]{:S(2)}, u32[]{:S(2)}) %collective-permute-start) | collective-permute-done | bytes 786464 | tf_op jit(solution)/shard_map/ppermute | solution.py:307
  46.9 2.8 %collective-permute-done.3.refs_2_ = bf16[1024,384]{1,0:T(8,128)(2,1)S(1)} collective-permute-done((bf16[1024,384]{1,0:T(8,128)(2,1)S(1)}, bf16[1024,384]{1,0:T(8,128)(2,1)S(1)}, u32[]{:S(2)}, u32[]{:S(2)}) %collective-permute-start.3) | collective-permute-done | bytes 786464 | tf_op jit(solution)/shard_map/ppermute | solution.py:307
  49.7 9.1 %shard_map.52 = (bf16[4352,384]{1,0:T(8,128)(2,1)S(1)}, f32[4352,128]{1,0:T(8,128)S(1)}, f32[4352,128]{1,0:T(8,128)S(1)}, bf16[14336,384]{1,0:T(8,128)(2,1)S(1)}...) custom-call(f32[8,3,16,128]{3,2,1,0:T(8,128)S(1)} %get-tuple-element, ...), custom_call_target="tpu_custom_call", output_to_operand_aliasing={{0}: (3, {}), {1}: (4, {}), {2}: (5, {}), {3}: (6, {}), {4}... | custom-call | flops 1073741824 | bytes 1048576 | tf_op jit(solution)/shard_map/pallas_call | solution.py:287
  58.7 0.1 collective-permute-start.7
  58.8 0.1 collective-permute-start.8
  58.9 0.1 collective-permute-start.1
  59.0 11.0 %collective-permute-done.8.refs_1_ = bf16[1024,384]{1,0:T(8,128)(2,1)S(1)} collective-permute-done((bf16[1024,384]{1,0:T(8,128)(2,1)S(1)}, bf16[1024,384]{1,0:T(8,128)(2,1)S(1)}, u32[]{:S(2)}, u32[]{:S(2)}) %collective-permute-start.8) | collective-permute-done | bytes 786464 | tf_op jit(solution)/shard_map/ppermute | solution.py:307
  70.0 2.5 %collective-permute-start.9 = (bf16[1024,384]{1,0:T(8,128)(2,1)S(1)}, bf16[1024,384]{1,0:T(8,128)(2,1)S(1)}, u32[]{:S(2)}, u32[]{:S(2)}) collective-permute-start(bf16[1024,384]{1,0:T(8,128)(2,1)S(1)} %collective-permute-done.8.refs_1_), channel_id=1, source_target_pairs={{0,1},{1,0},{2,3},{3,2},{4,5},{5,4},{6,7},{7,6},{8,9},{9,8},{10,11... | collective-permute-start | bytes 2359304 | tf_op jit(solution)/shard_map/ppermute | solution.py:307
  72.5 6.0 %collective-permute-done.1.refs_1_ = bf16[1024,384]{1,0:T(8,128)(2,1)S(1)} collective-permute-done((bf16[1024,384]{1,0:T(8,128)(2,1)S(1)}, bf16[1024,384]{1,0:T(8,128)(2,1)S(1)}, u32[]{:S(2)}, u32[]{:S(2)}) %collective-permute-start.1) | collective-permute-done | bytes 786464 | tf_op jit(solution)/shard_map/ppermute | solution.py:307
  78.5 2.5 %collective-permute-start.2 = (bf16[1024,384]{1,0:T(8,128)(2,1)S(1)}, bf16[1024,384]{1,0:T(8,128)(2,1)S(1)}, u32[]{:S(2)}, u32[]{:S(2)}) collective-permute-start(bf16[1024,384]{1,0:T(8,128)(2,1)S(1)} %collective-permute-done.1.refs_1_), channel_id=1, source_target_pairs={{0,1},{1,0},{2,3},{3,2},{4,5},{5,4},{6,7},{7,6},{8,9},{9,8},{10,11... | collective-permute-start | bytes 2359304 | tf_op jit(solution)/shard_map/ppermute | solution.py:307
  80.9 1.9 %shard_map.53 = (bf16[4352,384]{1,0:T(8,128)(2,1)S(1)}, f32[4352,128]{1,0:T(8,128)S(1)}, f32[4352,128]{1,0:T(8,128)S(1)}, bf16[14336,384]{1,0:T(8,128)(2,1)S(1)}...) custom-call(f32[8,3,16,128]{3,2,1,0:T(8,128)S(1)} %get-tuple-element, ...), custom_call_target="tpu_custom_call", output_to_operand_aliasing={{0}: (2, {}), {1}: (3, {}), {2}: (4, {}), {3}: (5, {}), {4}... | custom-call | flops 1073741824 | bytes 1048576 | tf_op jit(solution)/shard_map/pallas_call | solution.py:287
  82.9 0.0 collective-permute-done.9.refs_1_
  82.9 2.1 %shard_map.54 = (bf16[4352,384]{1,0:T(8,128)(2,1)S(1)}, f32[4352,128]{1,0:T(8,128)S(1)}, f32[4352,128]{1,0:T(8,128)S(1)}, bf16[14336,384]{1,0:T(8,128)(2,1)S(1)}...) custom-call(f32[8,3,16,128]{3,2,1,0:T(8,128)S(1)} %get-tuple-element, ...), custom_call_target="tpu_custom_call", output_to_operand_aliasing={{0}: (2, {}), {1}: (3, {}), {2}: (4, {}), {3}: (5, {}), {4}... | custom-call | flops 1073741824 | bytes 1048576 | tf_op jit(solution)/shard_map/pallas_call | solution.py:287
  85.0 0.3 shard_map.55
  85.3 0.0 collective-permute-done.7.refs_2_
  85.3 5.5 %shard_map.56 = (bf16[4352,384]{1,0:T(8,128)(2,1)S(1)}, f32[4352,128]{1,0:T(8,128)S(1)}, f32[4352,128]{1,0:T(8,128)S(1)}, bf16[14336,384]{1,0:T(8,128)(2,1)S(1)}...) custom-call(f32[8,3,16,128]{3,2,1,0:T(8,128)S(1)} %get-tuple-element, ...), custom_call_target="tpu_custom_call", output_to_operand_aliasing={{0}: (3, {}), {1}: (4, {}), {2}: (5, {}), {3}: (6, {}), {4}... | custom-call | flops 1073741824 | bytes 1048576 | tf_op jit(solution)/shard_map/pallas_call | solution.py:287
  90.8 0.6 copy-done.3
  91.4 12.2 %energy.1 = f32[1]{0:T(128)} custom-call(f32[8,128]{1,0:T(8,128)} %copy-done.3), custom_call_target="tpu_custom_call" | custom-call | tf_op jit(solution)/shard_map/energy/pallas_call | solution.py:47
  (5 shorter events, 0.0 us)
Async XLA Ops:
  0.6 15.1 %collective-permute-start.6 = (bf16[2048,384]{1,0:T(8,128)(2,1)}, bf16[2048,384]{1,0:T(8,128)(2,1)S(1)}, u32[]{:S(2)}, u32[]{:S(2)}) collective-permute-start(bf16[2048,384]{1,0:T(8,128)(2,1)} %refs_1_.1), channel_id=1, source_target_pairs={{0,1},{1,0},{2,3},{3,2},{4,5},{5,4},{6,7},{7,6},{8,9},{9,8},{10,11... | collective-permute-start | bytes 4718600 | tf_op jit(solution)/shard_map/ppermute | solution.py:307
  2.0 1.4 %copy-start = (bf16[2048,384]{1,0:T(8,128)(2,1)S(1)}, bf16[2048,384]{1,0:T(8,128)(2,1)}, u32[]{:S(2)}) copy-start(bf16[2048,384]{1,0:T(8,128)(2,1)} %refs_1_.1) | copy-start | bytes 4718596
  3.4 0.7 copy-start.2
  11.4 18.6 %collective-permute-start.4 = (bf16[1024,384]{1,0:T(8,128)(2,1)S(1)}, bf16[1024,384]{1,0:T(8,128)(2,1)S(1)}, u32[]{:S(2)}, u32[]{:S(2)}) collective-permute-start(bf16[1024,384]{1,0:T(8,128)(2,1)S(1)} %get-tuple-element.52), channel_id=1, source_target_pairs={{0,2},{1,7},{2,4},{3,1},{4,6},{5,3},{6,0},{7,5},{8,10},{9,15},{10,... | collective-permute-start | bytes 2359304 | tf_op jit(solution)/shard_map/ppermute | solution.py:307
  13.1 20.8 %collective-permute-start.5 = (bf16[1024,384]{1,0:T(8,128)(2,1)S(1)}, bf16[1024,384]{1,0:T(8,128)(2,1)S(1)}, u32[]{:S(2)}, u32[]{:S(2)}) collective-permute-start(bf16[1024,384]{1,0:T(8,128)(2,1)S(1)} %get-tuple-element.52), channel_id=1, source_target_pairs={{2,0},{7,1},{4,2},{1,3},{6,4},{3,5},{0,6},{5,7},{10,8},{15,9},{12,... | collective-permute-start | bytes 2359304 | tf_op jit(solution)/shard_map/ppermute | solution.py:307
  13.1 33.8 %collective-permute-start = (bf16[1024,384]{1,0:T(8,128)(2,1)S(1)}, bf16[1024,384]{1,0:T(8,128)(2,1)S(1)}, u32[]{:S(2)}, u32[]{:S(2)}) collective-permute-start(bf16[1024,384]{1,0:T(8,128)(2,1)S(1)} %get-tuple-element.51), channel_id=1, source_target_pairs={{0,2},{1,7},{2,4},{3,1},{4,6},{5,3},{6,0},{7,5},{8,10},{9,15},{10,... | collective-permute-start | bytes 2359304 | tf_op jit(solution)/shard_map/ppermute | solution.py:307
  15.8 33.9 %collective-permute-start.3 = (bf16[1024,384]{1,0:T(8,128)(2,1)S(1)}, bf16[1024,384]{1,0:T(8,128)(2,1)S(1)}, u32[]{:S(2)}, u32[]{:S(2)}) collective-permute-start(bf16[1024,384]{1,0:T(8,128)(2,1)S(1)} %get-tuple-element.51), channel_id=1, source_target_pairs={{2,0},{7,1},{4,2},{1,3},{6,4},{3,5},{0,6},{5,7},{10,8},{15,9},{12,... | collective-permute-start | bytes 2359304 | tf_op jit(solution)/shard_map/ppermute | solution.py:307
  15.8 1.4 %copy-start.1 = (bf16[2048,384]{1,0:T(8,128)(2,1)S(1)}, bf16[2048,384]{1,0:T(8,128)(2,1)}, u32[]{:S(2)}) copy-start(bf16[2048,384]{1,0:T(8,128)(2,1)} %refs_1_.1) | copy-start | bytes 4718596
  58.7 26.6 %collective-permute-start.7 = (f32[392,2048]{1,0:T(8,128)S(1)}, f32[392,2048]{1,0:T(8,128)S(1)}, u32[]{:S(2)}, u32[]{:S(2)}) collective-permute-start(f32[392,2048]{1,0:T(8,128)S(1)} %get-tuple-element.67), channel_id=1, source_target_pairs={{0,1},{1,0},{2,3},{3,2},{4,5},{5,4},{6,7},{7,6},{8,9},{9,8},{10,11... | collective-permute-start | bytes 9633800 | tf_op jit(solution)/shard_map/ppermute | solution.py:307
  58.8 11.2 %collective-permute-start.8 = (bf16[1024,384]{1,0:T(8,128)(2,1)S(1)}, bf16[1024,384]{1,0:T(8,128)(2,1)S(1)}, u32[]{:S(2)}, u32[]{:S(2)}) collective-permute-start(bf16[1024,384]{1,0:T(8,128)(2,1)S(1)} %collective-permute-done.4.refs_1_), channel_id=1, source_target_pairs={{0,2},{1,7},{2,4},{3,1},{4,6},{5,3},{6,0},{7,5},{8,10},{9,15},{10,... | collective-permute-start | bytes 2359304 | tf_op jit(solution)/shard_map/ppermute | solution.py:307
  58.9 19.5 %collective-permute-start.1 = (bf16[1024,384]{1,0:T(8,128)(2,1)S(1)}, bf16[1024,384]{1,0:T(8,128)(2,1)S(1)}, u32[]{:S(2)}, u32[]{:S(2)}) collective-permute-start(bf16[1024,384]{1,0:T(8,128)(2,1)S(1)} %collective-permute-done.refs_1_), channel_id=1, source_target_pairs={{0,2},{1,7},{2,4},{3,1},{4,6},{5,3},{6,0},{7,5},{8,10},{9,15},{10,... | collective-permute-start | bytes 2359304 | tf_op jit(solution)/shard_map/ppermute | solution.py:307
  70.0 12.8 %collective-permute-start.9 = (bf16[1024,384]{1,0:T(8,128)(2,1)S(1)}, bf16[1024,384]{1,0:T(8,128)(2,1)S(1)}, u32[]{:S(2)}, u32[]{:S(2)}) collective-permute-start(bf16[1024,384]{1,0:T(8,128)(2,1)S(1)} %collective-permute-done.8.refs_1_), channel_id=1, source_target_pairs={{0,1},{1,0},{2,3},{3,2},{4,5},{5,4},{6,7},{7,6},{8,9},{9,8},{10,11... | collective-permute-start | bytes 2359304 | tf_op jit(solution)/shard_map/ppermute | solution.py:307
  78.5 6.8 %collective-permute-start.2 = (bf16[1024,384]{1,0:T(8,128)(2,1)S(1)}, bf16[1024,384]{1,0:T(8,128)(2,1)S(1)}, u32[]{:S(2)}, u32[]{:S(2)}) collective-permute-start(bf16[1024,384]{1,0:T(8,128)(2,1)S(1)} %collective-permute-done.1.refs_1_), channel_id=1, source_target_pairs={{0,1},{1,0},{2,3},{3,2},{4,5},{5,4},{6,7},{7,6},{8,9},{9,8},{10,11... | collective-permute-start | bytes 2359304 | tf_op jit(solution)/shard_map/ppermute | solution.py:307
  90.8 0.6 copy-start.3

commit v4 on v3

v4 whole, which is shorter than its diff:
```python
import functools
import math

import jax
import jax.numpy as jnp
from jax import lax
from jax.experimental import pallas as pl
from jax.experimental.pallas import tpu as pltpu
from jax.sharding import PartitionSpec as P


LANES = 128
TILE_I = 256
TILE_J = 512
UNROLL = 4
BUDGET = 38
VMEM_MB = (5, 6, 9, 5, 8, 5, 9)
MESH = pl.DeviceIdType.MESH
VMEM_SPEC = pl.BlockSpec(memory_space=pltpu.VMEM)


def energy_kernel(n, part_hbm, out_ref, seen, part_ref, send_sem, recv_sem, local_sem):
    me = lax.axis_index('row')
    barrier = pltpu.get_barrier_semaphore()
    for off in range(1, n):
        pl.semaphore_signal(barrier, inc=1, device_id={'row': lax.rem(me + off, n)}, device_id_type=MESH)
    load = pltpu.make_async_copy(part_hbm, part_ref, local_sem)
    load.start()
    load.wait()
    pl.semaphore_wait(barrier, n - 1)
    copies = []
    for off in range(1, n):
        copies.append(pltpu.make_async_remote_copy(
            src_ref=part_ref, dst_ref=seen.at[me], send_sem=send_sem.at[off - 1], recv_sem=recv_sem.at[off - 1],
            device_id={'row': lax.rem(me + off, n)}, device_id_type=MESH))
    for copy in copies:
        copy.start()
    for copy in copies:
        copy.wait()
    total = jnp.zeros(part_ref.shape, jnp.float32)
    for k in range(n):
        total += jnp.where(me == k, part_ref[...], seen[k])
    out_ref[0] = 0.5 * jnp.sum(total)


def total_energy(part, n):
    return pl.pallas_call(
        functools.partial(energy_kernel, n),
        out_shape=jax.ShapeDtypeStruct((1,), jnp.float32),
        in_specs=[pl.BlockSpec(memory_space=pltpu.HBM)],
        out_specs=pl.BlockSpec(memory_space=pltpu.SMEM),
        scratch_shapes=[pltpu.VMEM((n,) + part.shape, jnp.float32), pltpu.VMEM(part.shape, jnp.float32), pltpu.SemaphoreType.DMA((n - 1,)),
                        pltpu.SemaphoreType.DMA((n - 1,)), pltpu.SemaphoreType.DMA],
        compiler_params=pltpu.CompilerParams(collective_id=0, has_side_effects=True),
        name='energy',
    )(part)


def up(value, step):
    return pl.cdiv(value, step) * step


def spread(meta, h_rows, c_rows, row0):
    groups = meta.shape[1]
    table = jnp.concatenate([meta[0], meta[1], jnp.zeros((LANES - 2 * groups, LANES), jnp.float32)], axis=0).T
    for g in range(groups):
        at = pl.ds(pl.multiple_of(row0 + g * LANES, LANES), LANES)
        c_rows[at, :] = jnp.broadcast_to(table[:, g:g + 1], (LANES, LANES))
        h_rows[at, :] = jnp.broadcast_to(table[:, groups + g:groups + g + 1], (LANES, LANES))


def append(meta, cols, at, start, size):
    for g in range(size // LANES):
        for m in range(2):
            cols[m:m + 1, pl.ds(pl.multiple_of(at + g * LANES, LANES), LANES)] = meta[m, start // LANES + g:start // LANES + g + 1, :]
    cols[:, pl.ds(pl.multiple_of(at + size, LANES), TILE_J)] = jnp.zeros((2, TILE_J), jnp.float32)


def begin_kernel(scale, pos_ref, q_ref, count_ref, meta, x_row, h_rows, c_rows, x_col, cols, pulls, sums):
    rows, width = pos_ref.shape
    lane = lax.broadcasted_iota(jnp.int32, (LANES, LANES), 1)
    table = jnp.zeros((LANES, LANES), jnp.float32)
    for b in range(rows // LANES):
        x = pos_ref[b * LANES:(b + 1) * LANES, :].astype(jnp.float32)
        table = jnp.where(lane == b, jnp.sum(x * x, axis=1, keepdims=True), table)
        meta[0, b:b + 1, :] = jnp.where(lane[:1] + b * LANES < count_ref[0], q_ref[b:b + 1, :], 0.0)
    meta[1] = table.T[:rows // LANES, :] * scale
    meta[2] = jnp.full(meta.shape[1:], count_ref[0], jnp.int32).astype(jnp.float32)
    sums[...] = jnp.zeros_like(sums)
    pulls[...] = jnp.zeros_like(pulls)
    x_row[:rows, :] = pos_ref[...]
    x_col[:rows, :] = pos_ref[...]
    x_col[rows:rows + TILE_J, :] = jnp.zeros((TILE_J, width), x_col.dtype)
    spread(meta, h_rows, c_rows, 0)
    append(meta, cols, 0, 0, rows)
    cols[:, cols.shape[1] - TILE_J:] = jnp.zeros((2, TILE_J), jnp.float32)


def state_shapes(rows, width, null, dtype):
    tall = 2 * rows + TILE_I
    return [pltpu.VMEM((tall, width), dtype), pltpu.VMEM((tall, LANES), jnp.float32), pltpu.VMEM((tall, LANES), jnp.float32),
            pltpu.VMEM((null, width), dtype), pltpu.VMEM((2, null + TILE_J), jnp.float32), pltpu.VMEM((width + 8, tall), jnp.float32),
            pltpu.VMEM((tall, LANES), jnp.float32)]


def begin(positions, charges, counts, null):
    rows, width = positions.shape
    groups = rows // LANES
    outs = pl.pallas_call(
        functools.partial(begin_kernel, math.log2(math.e) * 0.5 / width),
        out_shape=[jax.ShapeDtypeStruct((3, groups, LANES), jnp.float32)] + state_shapes(rows, width, null, positions.dtype),
        in_specs=[VMEM_SPEC, VMEM_SPEC, pl.BlockSpec(memory_space=pltpu.SMEM)],
        out_specs=[VMEM_SPEC] * 8,
        compiler_params=pltpu.CompilerParams(vmem_limit_bytes=4 << 20),
        cost_estimate=pl.CostEstimate(flops=1 << 30, bytes_accessed=1 << 20, transcendentals=0),
        name='begin',
    )(positions, charges.reshape(groups, LANES), counts)
    return outs[0], list(outs[1:])


def pair_kernel(cfg, *refs):
    rows, width, scale, this = cfg['rows'], cfg['width'], cfg['scale'], cfg['stage']
    refs = list(refs)
    metas = {k: refs.pop(0) for k in cfg['names']}
    loads = [refs.pop(0) for _ in range(cfg['loads'])]
    mate_pos = refs.pop(0) if this == 0 else None
    incoming = refs.pop(0) if this == cfg['turn'] else None
    n_state = 8 if this > cfg['turn'] else 7
    del refs[:n_state]
    x_row, h_rows, c_rows, x_col, cols, pulls, sums = refs[:7]
    turned = refs[7] if this >= cfg['turn'] else None
    gram_a, gram_b = refs[-2:]
    extra = refs[8 if this >= cfg['turn'] else 7:-2]

    count = {k: jnp.max(metas[k][2, 0:1, :]).astype(jnp.int32) for k in cfg['names']}
    tiles_own = pl.cdiv(count['own'], TILE_I)
    row_mate = pl.multiple_of(up(count['own'], LANES), LANES)
    tiles_both = pl.cdiv(row_mate + count['mate'], TILE_I)

    end = jnp.int32(0)
    lo = jnp.int32(0)
    for stage, chunks in enumerate(cfg['plan'][:this + 1]):
        for k, (name, start, size) in enumerate(chunks):
            if 0 < stage == this:
                at = pl.multiple_of(end, LANES)
                x_col[pl.ds(at, size), :] = loads[k][...]
                x_col[pl.ds(pl.multiple_of(at + size, LANES), TILE_J), :] = jnp.zeros((TILE_J, width), x_col.dtype)
                append(metas[name], cols, at, start, size)
            end = end + up(jnp.clip(count[name] - start, 0, size), LANES)
        tiles = tiles_own if cfg['modes'][stage] == 'own' else tiles_both
        have = pl.cdiv(end, TILE_J) if cfg['close'][stage] else end // TILE_J
        budget = cfg['budget'][stage]
        hi = have if budget is None else jnp.minimum(have, lo + budget // jnp.maximum(tiles, 1))
        if stage < this:
            lo = hi
        if cfg['close'][stage]:
            end = up(end, TILE_J)
    units = (hi - lo) * tiles

    if this == 0:
        x_row[pl.ds(row_mate, rows), :] = mate_pos[...]
        spread(metas['mate'], h_rows, c_rows, row_mate)
    if incoming is not None:
        table = jnp.zeros((LANES, LANES), jnp.float32)
        sub = lax.broadcasted_iota(jnp.int32, (LANES, LANES), 0)
        for g in range(rows // LANES):
            table = jnp.where(sub == g, incoming[width:width + 1, g * LANES:(g + 1) * LANES], table)
        table = table.T
        lane = lax.broadcasted_iota(jnp.int32, (LANES, LANES), 1)
        for g in range(rows // LANES):
            at = slice(g * LANES, (g + 1) * LANES)
            sums[at, :] += jnp.where(lane == 0, table[:, g:g + 1], 0.0)
            for k in range(width // LANES):
                d = slice(k * LANES, (k + 1) * LANES)
                turned[at, d] = (pulls[d, at] + incoming[d, at]).T

    def decode(unit):
        at = jnp.minimum(unit, units - 1)
        j = at // tiles
        return (at - j * tiles) * TILE_I, (j + lo) * TILE_J, jnp.where(unit < units, (j + lo) * TILE_J, cfg['null'])

    def aligned(pos):
        row, col, meta = pos
        return (pl.ds(pl.multiple_of(row, TILE_I), TILE_I), pl.ds(pl.multiple_of(col, TILE_J), TILE_J), pl.multiple_of(meta, TILE_J))

    def gram(pos, out):
        row, col, _ = aligned(pos)
        out[...] = lax.dot_general(x_row[row, :], x_col[col, :], (((1,), (1,)), ((), ())), preferred_element_type=jnp.float32)

    def weigh(pos, prod):
        row, col, meta = aligned(pos)
        h_row, c_row = h_rows[row, :], c_rows[row, :]
        parts, total = [], None
        for k in range(TILE_J // LANES):
            at = pl.ds(pl.multiple_of(meta + k * LANES, LANES), LANES)
            arg = jnp.minimum(prod[:, k * LANES:(k + 1) * LANES] * (2.0 * scale) - h_row - cols[1:2, at], 0.0)
            w = jnp.exp2(arg) * c_row * cols[0:1, at]
            if this == 0:
                off = pos[1] + k * LANES
                off = jnp.where(off < row_mate, off - pos[0], 1 << 20)
                w = jnp.where(lax.broadcasted_iota(jnp.int32, (TILE_I, LANES), 0) - lax.broadcasted_iota(jnp.int32, (TILE_I, LANES), 1) == off, 0.0, w)
            total = w if total is None else total + w
            parts.append(w.astype(jnp.bfloat16))
        sums[row, :] += total
        low = jnp.concatenate(parts, axis=1)
        if turned is None:
            pulls[:width, row] += lax.dot_general(x_col[col, :], low, (((0,), (1,)), ((), ())), preferred_element_type=jnp.float32)
        else:
            turned[row, :] += jnp.dot(low, x_col[col, :], preferred_element_type=jnp.float32)

    @pl.when(units > 0)
    def _():
        first = decode(0)
        gram(first, gram_a)

        def step(p, pos):
            for k in range(UNROLL):
                nxt = decode(UNROLL * p + k + 1)
                gram(nxt, (gram_a, gram_b)[(k + 1) % 2])
                weigh(pos, (gram_a, gram_b)[k % 2])
                pos = nxt
            return pos

        lax.fori_loop(0, pl.cdiv(units, UNROLL), step, first)

    if this == cfg['split']:
        lane = lax.broadcasted_iota(jnp.int32, (LANES, LANES), 1)
        table = jnp.zeros((LANES, LANES), jnp.float32)
        for g in range(rows // LANES):
            at = pl.ds(pl.multiple_of(row_mate + g * LANES, LANES), LANES)
            table = jnp.where(lane == g, jnp.sum(sums[at, :], axis=1, keepdims=True), table)
        table = table.T
        extra[0][:width, :] = pulls[:width, pl.ds(row_mate, rows)]
        for g in range(rows // LANES):
            extra[0][width:, g * LANES:(g + 1) * LANES] = jnp.broadcast_to(table[g:g + 1, :], (8, LANES))
    if this == len(cfg['plan']) - 1:
        force, part = extra
        part[...] = jnp.zeros_like(part)

        def tile(i, carry):
            at = pl.ds(pl.multiple_of(i * LANES, LANES), LANES)
            live = lax.broadcasted_iota(jnp.int32, (LANES, LANES), 0) + i * LANES < count['own']
            lanes = jnp.where(live, sums[at, :], 0.0)
            total = jnp.sum(lanes, axis=1, keepdims=True)
            for k in range(width // LANES):
                d = pl.ds(k * LANES, LANES)
                value = total * x_row[at, d].astype(jnp.float32) - turned[at, d]
                force[at, d] = jnp.where(live, value * cfg['inv_len2'], 0.0)
            part[...] += jnp.sum(lanes.reshape(LANES // 8, 8, LANES), axis=0)
            return carry

        lax.fori_loop(0, rows // LANES, tile, 0, unroll=4)


def pair_call(cfg, stage, metas, chunks, state, mate_pos=None, incoming=None):
    rows, width = cfg['rows'], cfg['width']
    names = ['own', 'mate']
    for chunk in cfg['plan'][:stage + 1]:
        names += [c[0] for c in chunk if c[0] not in names]
    final = stage == len(cfg['plan']) - 1
    cfg = dict(cfg, stage=stage, names=names, loads=len(chunks) if stage else 0)
    args = [metas[k] for k in names] + (list(chunks) if stage else [mate_pos])
    if incoming is not None:
        args.append(incoming)
    aliases = {}
    for k, a in enumerate(state):
        aliases[len(args)] = k
        args.append(a)
    out_shape = state_shapes(rows, width, cfg['null'], jnp.bfloat16)
    if stage >= cfg['turn']:
        out_shape.append(pltpu.VMEM((rows, width), jnp.float32))
    n_state = len(out_shape)
    if stage == cfg['split']:
        out_shape.append(jax.ShapeDtypeStruct((width + 8, rows), jnp.float32))
    if final:
        out_shape += [jax.ShapeDtypeStruct((rows, width), jnp.float32), jax.ShapeDtypeStruct((8, LANES), jnp.float32)]
    outs = pl.pallas_call(
        functools.partial(pair_kernel, cfg),
        out_shape=out_shape,
        in_specs=[VMEM_SPEC] * len(args),
        out_specs=[VMEM_SPEC] * len(out_shape),
        input_output_aliases=aliases,
        scratch_shapes=[pltpu.VMEM((TILE_I, TILE_J), jnp.float32)] * 2,
        compiler_params=pltpu.CompilerParams(vmem_limit_bytes=VMEM_MB[stage] << 20),
        cost_estimate=pl.CostEstimate(flops=1 << 30, bytes_accessed=1 << 20, transcendentals=0),
    )(*args)
    return list(outs[:n_state]), outs[n_state:]


def solution(mesh):
    n = mesh.shape['row']
    forth = [(p, (p + 2) % n if p % 2 == 0 else (p - 2) % n) for p in range(n)]
    back = [(b, a) for a, b in forth]
    twice = [(p, (p + n // 2) % n) for p in range(n)]
    swap = [(p, p ^ 1) for p in range(n)]

    def move(x, perm):
        return lax.ppermute(x, 'row', perm)

    def body(positions, charges, counts):
        block_rows, width = positions.shape
        half_rows = block_rows // 2

        def upper(name):
            return name, 0, half_rows

        def lower(name):
            return name, half_rows, block_rows - half_rows

        plan = [[('own', 0, block_rows)], [upper('near'), upper('next')], [lower('near'), lower('next')],
                [upper('far')], [upper('away')], [lower('far')], [lower('away')]]
        null = up(sum(c[2] for stage in plan for c in stage), TILE_J) + 8 * TILE_J
        cfg = dict(rows=block_rows, width=width, null=null, plan=plan, modes=['both'] * 3 + ['own'] * 4,
                   close=[True, False, True, False, False, False, True], budget=[None, BUDGET, None, None, None, None, None],
                   split=2, turn=4, scale=math.log2(math.e) * 0.5 / width, inv_len2=1.0 / width)

        mate_pos = move(positions, swap)
        top, bottom = positions[:half_rows], positions[half_rows:]
        meta, state = begin(positions, charges, counts, null)
        near_a, next_a = move(top, forth), move(top, back)
        near_b, next_b = move(bottom, forth), move(bottom, back)
        far_a, far_b = move(near_a, forth), move(near_b, forth)
        away_a, away_b = move(far_a, swap), move(far_b, swap)
        far_meta = move(meta, twice)
        metas = {'own': meta, 'mate': move(meta, swap), 'near': move(meta, forth), 'next': move(meta, back),
                 'far': far_meta, 'away': move(far_meta, swap)}
        arrays = [[positions], [near_a, next_a], [near_b, next_b], [far_a], [away_a], [far_b], [away_b]]
        incoming = None
        for stage in range(len(plan)):
            state, out = pair_call(cfg, stage, metas, arrays[stage], state, mate_pos=mate_pos if stage == 0 else None,
                                   incoming=incoming if stage == cfg['turn'] else None)
            if stage == cfg['split']:
                incoming = move(out[0], swap)
        forces, part = out
        return forces, total_energy(part, n)

    row_spec = P(('sys', 'row'), None)
    vec_spec = P(('sys', 'row'))
    step = jax.shard_map(body, mesh=mesh, in_specs=(row_spec, vec_spec, vec_spec), out_specs=(row_spec, P('sys')), check_vma=False)

    def program(positions, charges, counts):
        jax.eval_shape(step, positions, charges, counts)
        return step(positions, charges, counts)

    return program
```

time: 106 us -> 119 us (1.12)
  the two profiles are of different devices: /device:TPU:121 before, /device:TPU:112 now
where the time goes in v4:
time: 119 us
  waiting for transfers between devices  58.3 us (49%)
  Pallas kernels  38 us (32%)
  starting transfers between devices  17.2 us (14%)
  between operations  3.26 us (3%)
  local copies, waits for them, and re-layouts  2.23 us (2%)
    ppermute x15, waiting for transfers between devices, move(): return lax.ppermute(x, 'row', perm)  58.3 us
    pallas_call x7, Pallas kernels, pair_call(): pl.pallas_call(functools.partial(pair_kernel, cfg), out_shape=out_shape,...  23.6 us
    ppermute x15, starting transfers between devices, move(): return lax.ppermute(x, 'row', perm)  17.2 us
    pallas_call x1, Pallas kernels, total_energy(): pl.pallas_call(functools.partial(energy_kernel, n), out_shape=jax.ShapeDt...  12.5 us
  transfers between devices with their start and end apart: 15, of which 5 were waited for; matrix products, arithmetic and copies ran while one was open for 1% of the time, Pallas kernels for 13%

profile of v4, /device:TPU:112, one launch (start us, length us, event | category | flops | bytes accessed | tf_op | source)
XLA Modules:
  0.0 119.0 jit_solution(18362283367864238322)
XLA Ops:
  0.6 0.1 collective-permute-start.13
  0.7 1.6 %fusion = (bf16[1024,384]{1,0:T(8,128)(2,1)S(1)}, bf16[1024,384]{1,0:T(8,128)(2,1)S(1)}) fusion(bf16[2048,384]{1,0:T(8,128)(2,1)} %pos_ref.1), kind=kLoop, calls=%fused_computation | loop fusion | bytes 3145728 | tf_op jit(solution)/shard_map/slice | solution.py:318
  2.4 4.0 %collective-permute-start.12 = (bf16[1024,384]{1,0:T(8,128)(2,1)S(1)}, bf16[1024,384]{1,0:T(8,128)(2,1)S(1)}, u32[]{:S(2)}, u32[]{:S(2)}) collective-permute-start(bf16[1024,384]{1,0:T(8,128)(2,1)S(1)} %get-tuple-element.112), channel_id=1, source_target_pairs={{2,0},{7,1},{4,2},{1,3},{6,4},{3,5},{0,6},{5,7},{10,8},{15,9},{12,... | collective-permute-start | bytes 2359304 | tf_op jit(solution)/shard_map/ppermute | solution.py:298
  6.3 0.0 collective-permute-start.8
  7.0 1.9 %begin.1 = (f32[3,16,128]{2,1,0:T(8,128)S(1)}, bf16[4352,384]{1,0:T(8,128)(2,1)S(1)}, f32[4352,128]{1,0:T(8,128)S(1)}, f32[4352,128]{1,0:T(8,128)S(1)}, bf16[143...) custom-call(bf16[2048,384]{1,0:T(8,128)(2,1)S(1)} %copy-done, ...), custom_call_target="tpu_custom_call" | custom-call | flops 1073741824 | bytes 1048576 | tf_op jit(solution)/shard_map/begin/pallas_call | solution.py:109
  8.9 3.3 %collective-permute-start.2 = (f32[3,16,128]{2,1,0:T(8,128)S(1)}, f32[3,16,128]{2,1,0:T(8,128)S(1)}, u32[]{:S(2)}, u32[]{:S(2)}) collective-permute-start(f32[3,16,128]{2,1,0:T(8,128)S(1)} %get-tuple-element.57.refs_0_), channel_id=1, source_target_pairs={{2,0},{7,1},{4,2},{1,3},{6,4},{3,5},{0,6},{5,7},{10,8},{15,9},{12,... | collective-permute-start | bytes 73736 | tf_op jit(solution)/shard_map/ppermute | solution.py:298
  12.3 0.0 collective-permute-start
  12.3 11.8 %collective-permute-done.2.refs_3_ = f32[3,16,128]{2,1,0:T(8,128)S(1)} collective-permute-done((f32[3,16,128]{2,1,0:T(8,128)S(1)}, f32[3,16,128]{2,1,0:T(8,128)S(1)}, u32[]{:S(2)}, u32[]{:S(2)}) %collective-permute-start.2) | collective-permute-done | bytes 24608 | tf_op jit(solution)/shard_map/ppermute | solution.py:298
  24.1 3.7 %collective-permute-start.11 = (bf16[1024,384]{1,0:T(8,128)(2,1)S(1)}, bf16[1024,384]{1,0:T(8,128)(2,1)S(1)}, u32[]{:S(2)}, u32[]{:S(2)}) collective-permute-start(bf16[1024,384]{1,0:T(8,128)(2,1)S(1)} %get-tuple-element.113), channel_id=1, source_target_pairs={{2,0},{7,1},{4,2},{1,3},{6,4},{3,5},{0,6},{5,7},{10,8},{15,9},{12,... | collective-permute-start | bytes 2359304 | tf_op jit(solution)/shard_map/ppermute | solution.py:298
  27.7 0.0 collective-permute-done.refs_1_
  27.8 0.1 collective-permute-start.1
  27.9 2.7 %shard_map.50 = (bf16[4352,384]{1,0:T(8,128)(2,1)S(1)}, f32[4352,128]{1,0:T(8,128)S(1)}, f32[4352,128]{1,0:T(8,128)S(1)}, bf16[14336,384]{1,0:T(8,128)(2,1)S(1)}...) custom-call(f32[3,16,128]{2,1,0:T(8,128)S(1)} %get-tuple-element.57., ...), custom_call_target="tpu_custom_call", output_to_operand_aliasing={{0}: (3, {}), {1}: (4, {}), {2}: (5, {}), {3}: (6, {}), {4}... | custom-call | flops 1073741824 | bytes 1048576 | tf_op jit(solution)/shard_map/pallas_call | solution.py:277
  30.6 12.9 %collective-permute-done.1.refs_2_ = f32[3,16,128]{2,1,0:T(8,128)S(1)} collective-permute-done((f32[3,16,128]{2,1,0:T(8,128)S(1)}, f32[3,16,128]{2,1,0:T(8,128)S(1)}, u32[]{:S(2)}, u32[]{:S(2)}) %collective-permute-start.1) | collective-permute-done | bytes 24608 | tf_op jit(solution)/shard_map/ppermute | solution.py:298
  43.5 4.9 %shard_map.51 = (bf16[4352,384]{1,0:T(8,128)(2,1)S(1)}, f32[4352,128]{1,0:T(8,128)S(1)}, f32[4352,128]{1,0:T(8,128)S(1)}, bf16[14336,384]{1,0:T(8,128)(2,1)S(1)}...) custom-call(f32[3,16,128]{2,1,0:T(8,128)S(1)} %get-tuple-element.57., ...), custom_call_target="tpu_custom_call", output_to_operand_aliasing={{0}: (6, {}), {1}: (7, {}), {2}: (8, {}), {3}: (9, {}), {4}... | custom-call | flops 1073741824 | bytes 1048576 | tf_op jit(solution)/shard_map/pallas_call | solution.py:277
  48.4 0.0 collective-permute-done.11.refs_5_
  48.4 5.4 %shard_map.52 = (bf16[4352,384]{1,0:T(8,128)(2,1)S(1)}, f32[4352,128]{1,0:T(8,128)S(1)}, f32[4352,128]{1,0:T(8,128)S(1)}, bf16[14336,384]{1,0:T(8,128)(2,1)S(1)}...) custom-call(f32[3,16,128]{2,1,0:T(8,128)S(1)} %get-tuple-element.57., ...), custom_call_target="tpu_custom_call", output_to_operand_aliasing={{0}: (6, {}), {1}: (7, {}), {2}: (8, {}), {3}: (9, {}), {4}... | custom-call | flops 1073741824 | bytes 1048576 | tf_op jit(solution)/shard_map/pallas_call | solution.py:277
  53.8 0.1 collective-permute-start.14
  53.9 0.5 collective-permute-start.9
  54.4 4.4 %collective-permute-start.6 = (bf16[1024,384]{1,0:T(8,128)(2,1)S(1)}, bf16[1024,384]{1,0:T(8,128)(2,1)S(1)}, u32[]{:S(2)}, u32[]{:S(2)}) collective-permute-start(bf16[1024,384]{1,0:T(8,128)(2,1)S(1)} %collective-permute-done.5.refs_4_), channel_id=1, source_target_pairs={{0,2},{1,7},{2,4},{3,1},{4,6},{5,3},{6,0},{7,5},{8,10},{9,15},{10,... | collective-permute-start | bytes 2359304 | tf_op jit(solution)/shard_map/ppermute | solution.py:298
  58.8 20.8 %collective-permute-done.9.refs_5_ = bf16[1024,384]{1,0:T(8,128)(2,1)S(1)} collective-permute-done((bf16[1024,384]{1,0:T(8,128)(2,1)S(1)}, bf16[1024,384]{1,0:T(8,128)(2,1)S(1)}, u32[]{:S(2)}, u32[]{:S(2)}) %collective-permute-start.9) | collective-permute-done | bytes 786464 | tf_op jit(solution)/shard_map/ppermute | solution.py:298
  79.7 0.0 collective-permute-start.10
  79.7 8.4 %collective-permute-done.6.refs_6_ = bf16[1024,384]{1,0:T(8,128)(2,1)S(1)} collective-permute-done((bf16[1024,384]{1,0:T(8,128)(2,1)S(1)}, bf16[1024,384]{1,0:T(8,128)(2,1)S(1)}, u32[]{:S(2)}, u32[]{:S(2)}) %collective-permute-start.6) | collective-permute-done | bytes 786464 | tf_op jit(solution)/shard_map/ppermute | solution.py:298
  88.1 1.0 collective-permute-start.3
  89.1 4.3 %collective-permute-done.3.refs_4_ = f32[3,16,128]{2,1,0:T(8,128)S(1)} collective-permute-done((f32[3,16,128]{2,1,0:T(8,128)S(1)}, f32[3,16,128]{2,1,0:T(8,128)S(1)}, u32[]{:S(2)}, u32[]{:S(2)}) %collective-permute-start.3) | collective-permute-done | bytes 24608 | tf_op jit(solution)/shard_map/ppermute | solution.py:298
  93.4 2.2 %shard_map.53 = (bf16[4352,384]{1,0:T(8,128)(2,1)S(1)}, f32[4352,128]{1,0:T(8,128)S(1)}, f32[4352,128]{1,0:T(8,128)S(1)}, bf16[14336,384]{1,0:T(8,128)(2,1)S(1)}...) custom-call(f32[3,16,128]{2,1,0:T(8,128)S(1)} %get-tuple-element.57., ...), custom_call_target="tpu_custom_call", output_to_operand_aliasing={{0}: (6, {}), {1}: (7, {}), {2}: (8, {}), {3}: (9, {}), {4}... | custom-call | flops 1073741824 | bytes 1048576 | tf_op jit(solution)/shard_map/pallas_call | solution.py:277
  95.6 0.0 collective-permute-done.4.refs_5_
  95.6 3.4 %shard_map.54 = (bf16[4352,384]{1,0:T(8,128)(2,1)S(1)}, f32[4352,128]{1,0:T(8,128)S(1)}, f32[4352,128]{1,0:T(8,128)S(1)}, bf16[14336,384]{1,0:T(8,128)(2,1)S(1)}...) custom-call(f32[3,16,128]{2,1,0:T(8,128)S(1)} %get-tuple-element.57., ...), custom_call_target="tpu_custom_call", output_to_operand_aliasing={{0}: (8, {}), {1}: (9, {}), {2}: (10, {}), {3}: (11, {}), {... | custom-call | flops 1073741824 | bytes 1048576 | tf_op jit(solution)/shard_map/pallas_call | solution.py:277
  99.0 0.3 shard_map.55
  99.3 0.0 collective-permute-done.7.refs_6_
  99.3 4.8 %shard_map.56 = (bf16[4352,384]{1,0:T(8,128)(2,1)S(1)}, f32[4352,128]{1,0:T(8,128)S(1)}, f32[4352,128]{1,0:T(8,128)S(1)}, bf16[14336,384]{1,0:T(8,128)(2,1)S(1)}...) custom-call(f32[3,16,128]{2,1,0:T(8,128)S(1)} %get-tuple-element.57., ...), custom_call_target="tpu_custom_call", output_to_operand_aliasing={{0}: (7, {}), {1}: (8, {}), {2}: (9, {}), {3}: (10, {}), {4... | custom-call | flops 1073741824 | bytes 1048576 | tf_op jit(solution)/shard_map/pallas_call | solution.py:277
  104.1 0.6 copy-done.1
  104.7 12.5 %energy.1 = f32[1]{0:T(128)} custom-call(f32[8,128]{1,0:T(8,128)} %copy-done.1), custom_call_target="tpu_custom_call" | custom-call | tf_op jit(solution)/shard_map/energy/pallas_call | solution.py:47
  (14 shorter events, 0.0 us)
Async XLA Ops:
  0.6 6.4 %copy-start = (bf16[2048,384]{1,0:T(8,128)(2,1)S(1)}, bf16[2048,384]{1,0:T(8,128)(2,1)}, u32[]{:S(2)}) copy-start(bf16[2048,384]{1,0:T(8,128)(2,1)} %pos_ref.1) | copy-start | bytes 4718596
  0.6 6.4 %copy-start.2 = (f32[2048]{0:T(1024)S(1)}, f32[2048]{0:T(1024)}, u32[]{:S(2)}) copy-start(f32[2048]{0:T(1024)} %param.4) | copy-start | bytes 24580
  0.6 27.1 %collective-permute-start.13 = (bf16[2048,384]{1,0:T(8,128)(2,1)}, bf16[2048,384]{1,0:T(8,128)(2,1)S(1)}, u32[]{:S(2)}, u32[]{:S(2)}) collective-permute-start(bf16[2048,384]{1,0:T(8,128)(2,1)} %pos_ref.1), channel_id=1, source_target_pairs={{0,1},{1,0},{2,3},{3,2},{4,5},{5,4},{6,7},{7,6},{8,9},{9,8},{10,11... | collective-permute-start | bytes 4718600 | tf_op jit(solution)/shard_map/ppermute | solution.py:298
  2.4 41.1 %collective-permute-start.12 = (bf16[1024,384]{1,0:T(8,128)(2,1)S(1)}, bf16[1024,384]{1,0:T(8,128)(2,1)S(1)}, u32[]{:S(2)}, u32[]{:S(2)}) collective-permute-start(bf16[1024,384]{1,0:T(8,128)(2,1)S(1)} %get-tuple-element.112), channel_id=1, source_target_pairs={{2,0},{7,1},{4,2},{1,3},{6,4},{3,5},{0,6},{5,7},{10,8},{15,9},{12,... | collective-permute-start | bytes 2359304 | tf_op jit(solution)/shard_map/ppermute | solution.py:298
  6.3 37.2 %collective-permute-start.8 = (bf16[1024,384]{1,0:T(8,128)(2,1)S(1)}, bf16[1024,384]{1,0:T(8,128)(2,1)S(1)}, u32[]{:S(2)}, u32[]{:S(2)}) collective-permute-start(bf16[1024,384]{1,0:T(8,128)(2,1)S(1)} %get-tuple-element.112), channel_id=1, source_target_pairs={{0,2},{1,7},{2,4},{3,1},{4,6},{5,3},{6,0},{7,5},{8,10},{9,15},{10,... | collective-permute-start | bytes 2359304 | tf_op jit(solution)/shard_map/ppermute | solution.py:298
  8.9 15.1 %collective-permute-start.2 = (f32[3,16,128]{2,1,0:T(8,128)S(1)}, f32[3,16,128]{2,1,0:T(8,128)S(1)}, u32[]{:S(2)}, u32[]{:S(2)}) collective-permute-start(f32[3,16,128]{2,1,0:T(8,128)S(1)} %get-tuple-element.57.refs_0_), channel_id=1, source_target_pairs={{2,0},{7,1},{4,2},{1,3},{6,4},{3,5},{0,6},{5,7},{10,8},{15,9},{12,... | collective-permute-start | bytes 73736 | tf_op jit(solution)/shard_map/ppermute | solution.py:298
  12.3 15.5 %collective-permute-start = (f32[3,16,128]{2,1,0:T(8,128)S(1)}, f32[3,16,128]{2,1,0:T(8,128)S(1)}, u32[]{:S(2)}, u32[]{:S(2)}) collective-permute-start(f32[3,16,128]{2,1,0:T(8,128)S(1)} %get-tuple-element.57.refs_0_), channel_id=1, source_target_pairs={{0,1},{1,0},{2,3},{3,2},{4,5},{5,4},{6,7},{7,6},{8,9},{9,8},{10,11... | collective-permute-start | bytes 73736 | tf_op jit(solution)/shard_map/ppermute | solution.py:298
  24.1 24.3 %collective-permute-start.11 = (bf16[1024,384]{1,0:T(8,128)(2,1)S(1)}, bf16[1024,384]{1,0:T(8,128)(2,1)S(1)}, u32[]{:S(2)}, u32[]{:S(2)}) collective-permute-start(bf16[1024,384]{1,0:T(8,128)(2,1)S(1)} %get-tuple-element.113), channel_id=1, source_target_pairs={{2,0},{7,1},{4,2},{1,3},{6,4},{3,5},{0,6},{5,7},{10,8},{15,9},{12,... | collective-permute-start | bytes 2359304 | tf_op jit(solution)/shard_map/ppermute | solution.py:298
  27.8 20.6 %collective-permute-start.5 = (bf16[1024,384]{1,0:T(8,128)(2,1)S(1)}, bf16[1024,384]{1,0:T(8,128)(2,1)S(1)}, u32[]{:S(2)}, u32[]{:S(2)}) collective-permute-start(bf16[1024,384]{1,0:T(8,128)(2,1)S(1)} %get-tuple-element.113), channel_id=1, source_target_pairs={{0,2},{1,7},{2,4},{3,1},{4,6},{5,3},{6,0},{7,5},{8,10},{9,15},{10,... | collective-permute-start | bytes 2359304 | tf_op jit(solution)/shard_map/ppermute | solution.py:298
  27.8 15.7 %collective-permute-start.1 = (f32[3,16,128]{2,1,0:T(8,128)S(1)}, f32[3,16,128]{2,1,0:T(8,128)S(1)}, u32[]{:S(2)}, u32[]{:S(2)}) collective-permute-start(f32[3,16,128]{2,1,0:T(8,128)S(1)} %get-tuple-element.57.refs_0_), channel_id=1, source_target_pairs={{0,2},{1,7},{2,4},{3,1},{4,6},{5,3},{6,0},{7,5},{8,10},{9,15},{10,... | collective-permute-start | bytes 73736 | tf_op jit(solution)/shard_map/ppermute | solution.py:298
  53.8 41.8 %collective-permute-start.14 = (f32[392,2048]{1,0:T(8,128)S(1)}, f32[392,2048]{1,0:T(8,128)S(1)}, u32[]{:S(2)}, u32[]{:S(2)}) collective-permute-start(f32[392,2048]{1,0:T(8,128)S(1)} %get-tuple-element.79), channel_id=1, source_target_pairs={{0,1},{1,0},{2,3},{3,2},{4,5},{5,4},{6,7},{7,6},{8,9},{9,8},{10,11... | collective-permute-start | bytes 9633800 | tf_op jit(solution)/shard_map/ppermute | solution.py:298
  53.9 25.7 %collective-permute-start.9 = (bf16[1024,384]{1,0:T(8,128)(2,1)S(1)}, bf16[1024,384]{1,0:T(8,128)(2,1)S(1)}, u32[]{:S(2)}, u32[]{:S(2)}) collective-permute-start(bf16[1024,384]{1,0:T(8,128)(2,1)S(1)} %collective-permute-done.8.refs_4_), channel_id=1, source_target_pairs={{0,2},{1,7},{2,4},{3,1},{4,6},{5,3},{6,0},{7,5},{8,10},{9,15},{10,... | collective-permute-start | bytes 2359304 | tf_op jit(solution)/shard_map/ppermute | solution.py:298
  54.4 33.7 %collective-permute-start.6 = (bf16[1024,384]{1,0:T(8,128)(2,1)S(1)}, bf16[1024,384]{1,0:T(8,128)(2,1)S(1)}, u32[]{:S(2)}, u32[]{:S(2)}) collective-permute-start(bf16[1024,384]{1,0:T(8,128)(2,1)S(1)} %collective-permute-done.5.refs_4_), channel_id=1, source_target_pairs={{0,2},{1,7},{2,4},{3,1},{4,6},{5,3},{6,0},{7,5},{8,10},{9,15},{10,... | collective-permute-start | bytes 2359304 | tf_op jit(solution)/shard_map/ppermute | solution.py:298
  79.7 15.9 %collective-permute-start.10 = (bf16[1024,384]{1,0:T(8,128)(2,1)S(1)}, bf16[1024,384]{1,0:T(8,128)(2,1)S(1)}, u32[]{:S(2)}, u32[]{:S(2)}) collective-permute-start(bf16[1024,384]{1,0:T(8,128)(2,1)S(1)} %collective-permute-done.9.refs_5_), channel_id=1, source_target_pairs={{0,1},{1,0},{2,3},{3,2},{4,5},{5,4},{6,7},{7,6},{8,9},{9,8},{10,11... | collective-permute-start | bytes 2359304 | tf_op jit(solution)/shard_map/ppermute | solution.py:298
  88.1 11.2 %collective-permute-start.7 = (bf16[1024,384]{1,0:T(8,128)(2,1)S(1)}, bf16[1024,384]{1,0:T(8,128)(2,1)S(1)}, u32[]{:S(2)}, u32[]{:S(2)}) collective-permute-start(bf16[1024,384]{1,0:T(8,128)(2,1)S(1)} %collective-permute-done.6.refs_6_), channel_id=1, source_target_pairs={{0,1},{1,0},{2,3},{3,2},{4,5},{5,4},{6,7},{7,6},{8,9},{9,8},{10,11... | collective-permute-start | bytes 2359304 | tf_op jit(solution)/shard_map/ppermute | solution.py:298
  88.1 5.3 %collective-permute-start.3 = (f32[3,16,128]{2,1,0:T(8,128)S(1)}, f32[3,16,128]{2,1,0:T(8,128)S(1)}, u32[]{:S(2)}, u32[]{:S(2)}) collective-permute-start(f32[3,16,128]{2,1,0:T(8,128)S(1)} %get-tuple-element.57.refs_0_), channel_id=1, source_target_pairs={{0,4},{1,5},{2,6},{3,7},{4,0},{5,1},{6,2},{7,3},{8,12},{9,13},{10,... | collective-permute-start | bytes 73736 | tf_op jit(solution)/shard_map/ppermute | solution.py:298
  93.4 2.2 %collective-permute-start.4 = (f32[3,16,128]{2,1,0:T(8,128)S(1)}, f32[3,16,128]{2,1,0:T(8,128)S(1)}, u32[]{:S(2)}, u32[]{:S(2)}) collective-permute-start(f32[3,16,128]{2,1,0:T(8,128)S(1)} %collective-permute-done.3.refs_4_), channel_id=1, source_target_pairs={{0,1},{1,0},{2,3},{3,2},{4,5},{5,4},{6,7},{7,6},{8,9},{9,8},{10,11... | collective-permute-start | bytes 73736 | tf_op jit(solution)/shard_map/ppermute | solution.py:298
  104.1 0.6 copy-start.1

commit v5 on v4

--- a/solution.py
+++ b/solution.py
@@ -13,8 +13,9 @@
 TILE_I = 256
 TILE_J = 512
 UNROLL = 4
+FIRST_BUDGET = 22
 BUDGET = 38
-VMEM_MB = (5, 6, 9, 5, 8, 5, 9)
+VMEM_MB = (5, 4, 6, 9, 5, 5, 8, 5, 9)
 MESH = pl.DeviceIdType.MESH
 VMEM_SPEC = pl.BlockSpec(memory_space=pltpu.VMEM)
 
@@ -129,8 +130,10 @@
     del refs[:n_state]
     x_row, h_rows, c_rows, x_col, cols, pulls, sums = refs[:7]
     turned = refs[7] if this >= cfg['turn'] else None
-    gram_a, gram_b = refs[-2:]
-    extra = refs[8 if this >= cfg['turn'] else 7:-2]
+    refs = refs[8 if this >= cfg['turn'] else 7:]
+    n_out = (this == cfg['split']) + 2 * (this == len(cfg['plan']) - 1)
+    gram_a, gram_b = refs[n_out:n_out + 2]
+    extra = refs[:n_out] + refs[n_out + 2:]
 
     count = {k: jnp.max(metas[k][2, 0:1, :]).astype(jnp.int32) for k in cfg['names']}
     tiles_own = pl.cdiv(count['own'], TILE_I)
@@ -177,25 +180,24 @@
     def decode(unit):
         at = jnp.minimum(unit, units - 1)
         j = at // tiles
-        return (at - j * tiles) * TILE_I, (j + lo) * TILE_J, jnp.where(unit < units, (j + lo) * TILE_J, cfg['null'])
+        return (at - j * tiles) * TILE_I, (j + lo) * TILE_J
 
     def aligned(pos):
-        row, col, meta = pos
-        return (pl.ds(pl.multiple_of(row, TILE_I), TILE_I), pl.ds(pl.multiple_of(col, TILE_J), TILE_J), pl.multiple_of(meta, TILE_J))
+        return pl.ds(pl.multiple_of(pos[0], TILE_I), TILE_I), pl.ds(pl.multiple_of(pos[1], TILE_J), TILE_J)
 
     def gram(pos, out):
-        row, col, _ = aligned(pos)
+        row, col = aligned(pos)
         out[...] = lax.dot_general(x_row[row, :], x_col[col, :], (((1,), (1,)), ((), ())), preferred_element_type=jnp.float32)
 
     def weigh(pos, prod):
-        row, col, meta = aligned(pos)
+        row, col = aligned(pos)
         h_row, c_row = h_rows[row, :], c_rows[row, :]
         parts, total = [], None
         for k in range(TILE_J // LANES):
-            at = pl.ds(pl.multiple_of(meta + k * LANES, LANES), LANES)
+            at = pl.ds(pl.multiple_of(pos[1] + k * LANES, LANES), LANES)
             arg = jnp.minimum(prod[:, k * LANES:(k + 1) * LANES] * (2.0 * scale) - h_row - cols[1:2, at], 0.0)
             w = jnp.exp2(arg) * c_row * cols[0:1, at]
-            if this == 0:
+            if this < 2:
                 off = pos[1] + k * LANES
                 off = jnp.where(off < row_mate, off - pos[0], 1 << 20)
                 w = jnp.where(lax.broadcasted_iota(jnp.int32, (TILE_I, LANES), 0) - lax.broadcasted_iota(jnp.int32, (TILE_I, LANES), 1) == off, 0.0, w)
@@ -208,7 +210,7 @@
         else:
             turned[row, :] += jnp.dot(low, x_col[col, :], preferred_element_type=jnp.float32)
 
-    @pl.when(units > 0)
+    @pl.when((units > 0) if cfg['plan'][this] or this < 2 else False)
     def _():
         first = decode(0)
         gram(first, gram_a)
@@ -221,7 +223,14 @@
                 pos = nxt
             return pos
 
-        lax.fori_loop(0, pl.cdiv(units, UNROLL), step, first)
+        def single(unit, pos):
+            nxt = decode(unit + 1)
+            weigh(pos, gram_a)
+            gram(nxt, gram_a)
+            return nxt
+
+        whole = units // UNROLL
+        lax.fori_loop(whole * UNROLL, units, single, lax.fori_loop(0, whole, step, first))
 
     if this == cfg['split']:
         lane = lax.broadcasted_iota(jnp.int32, (LANES, LANES), 1)
@@ -234,8 +243,10 @@
         for g in range(rows // LANES):
             extra[0][width:, g * LANES:(g + 1) * LANES] = jnp.broadcast_to(table[g:g + 1, :], (8, LANES))
     if this == len(cfg['plan']) - 1:
-        force, part = extra
+        force, part = extra[:2]
+        staged, copy_sem = extra[2:]
         part[...] = jnp.zeros_like(part)
+        step = rows // copy_sem.shape[0]
 
         def tile(i, carry):
             at = pl.ds(pl.multiple_of(i * LANES, LANES), LANES)
@@ -245,11 +256,18 @@
             for k in range(width // LANES):
                 d = pl.ds(k * LANES, LANES)
                 value = total * x_row[at, d].astype(jnp.float32) - turned[at, d]
-                force[at, d] = jnp.where(live, value * cfg['inv_len2'], 0.0)
+                staged[at, d] = jnp.where(live, value * cfg['inv_len2'], 0.0)
             part[...] += jnp.sum(lanes.reshape(LANES // 8, 8, LANES), axis=0)
             return carry
 
-        lax.fori_loop(0, rows // LANES, tile, 0, unroll=4)
+        copies = []
+        for q in range(copy_sem.shape[0]):
+            lax.fori_loop(q * step // LANES, (q + 1) * step // LANES, tile, 0, unroll=True)
+            at = pl.ds(q * step, step)
+            copies.append(pltpu.make_async_copy(staged.at[at, :], force.at[at, :], copy_sem.at[q]))
+            copies[-1].start()
+        for copy in copies:
+            copy.wait()
 
 
 def pair_call(cfg, stage, metas, chunks, state, mate_pos=None, incoming=None):
@@ -274,13 +292,18 @@
         out_shape.append(jax.ShapeDtypeStruct((width + 8, rows), jnp.float32))
     if final:
         out_shape += [jax.ShapeDtypeStruct((rows, width), jnp.float32), jax.ShapeDtypeStruct((8, LANES), jnp.float32)]
+    out_specs = [VMEM_SPEC] * len(out_shape)
+    scratch = []
+    if final:
+        out_specs[n_state] = pl.BlockSpec(memory_space=pltpu.HBM)
+        scratch = [pltpu.VMEM((rows, width), jnp.float32), pltpu.SemaphoreType.DMA((4,))]
     outs = pl.pallas_call(
         functools.partial(pair_kernel, cfg),
         out_shape=out_shape,
         in_specs=[VMEM_SPEC] * len(args),
-        out_specs=[VMEM_SPEC] * len(out_shape),
+        out_specs=out_specs,
         input_output_aliases=aliases,
-        scratch_shapes=[pltpu.VMEM((TILE_I, TILE_J), jnp.float32)] * 2,
+        scratch_shapes=[pltpu.VMEM((TILE_I, TILE_J), jnp.float32)] * 2 + scratch,
         compiler_params=pltpu.CompilerParams(vmem_limit_bytes=VMEM_MB[stage] << 20),
         cost_estimate=pl.CostEstimate(flops=1 << 30, bytes_accessed=1 << 20, transcendentals=0),
     )(*args)
@@ -307,12 +330,13 @@
         def lower(name):
             return name, half_rows, block_rows - half_rows
 
-        plan = [[('own', 0, block_rows)], [upper('near'), upper('next')], [lower('near'), lower('next')],
-                [upper('far')], [upper('away')], [lower('far')], [lower('away')]]
+        plan = [[('own', 0, block_rows)], [], [upper('near'), upper('next')], [lower('near'), lower('next')],
+                [upper('far')], [upper('away')], [], [lower('far')], [lower('away')]]
         null = up(sum(c[2] for stage in plan for c in stage), TILE_J) + 8 * TILE_J
-        cfg = dict(rows=block_rows, width=width, null=null, plan=plan, modes=['both'] * 3 + ['own'] * 4,
-                   close=[True, False, True, False, False, False, True], budget=[None, BUDGET, None, None, None, None, None],
-                   split=2, turn=4, scale=math.log2(math.e) * 0.5 / width, inv_len2=1.0 / width)
+        cfg = dict(rows=block_rows, width=width, null=null, plan=plan, modes=['both'] * 4 + ['own'] * 5,
+                   close=[True, True, False, True, False, False, False, False, True],
+                   budget=[FIRST_BUDGET, None, BUDGET] + [None] * 6,
+                   split=3, turn=6, scale=math.log2(math.e) * 0.5 / width, inv_len2=1.0 / width)
 
         mate_pos = move(positions, swap)
         top, bottom = positions[:half_rows], positions[half_rows:]
@@ -324,7 +348,7 @@
         far_meta = move(meta, twice)
         metas = {'own': meta, 'mate': move(meta, swap), 'near': move(meta, forth), 'next': move(meta, back),
                  'far': far_meta, 'away': move(far_meta, swap)}
-        arrays = [[positions], [near_a, next_a], [near_b, next_b], [far_a], [away_a], [far_b], [away_b]]
+        arrays = [[positions], [], [near_a, next_a], [near_b, next_b], [far_a], [away_a], [], [far_b], [away_b]]
         incoming = None
         for stage in range(len(plan)):
             state, out = pair_call(cfg, stage, metas, arrays[stage], state, mate_pos=mate_pos if stage == 0 else None,

time: 119 us -> 128 us (1.076)
  waiting for transfers between devices: 58.3 us -> 67.5 us
    ppermute x15, waiting for transfers between devices: 58.3 us -> 67.5 us  [move(): return lax.ppermute(x, 'row', perm)]
    pallas_call x7 -> x9, Pallas kernels: 23.6 us -> 20.2 us  [pair_call(): pl.pallas_call(functools.partial(pair_kernel, cfg), out_shape=out_shape,...]
    pallas_call x1, Pallas kernels: 12.5 us -> 15.2 us  [total_energy(): pl.pallas_call(functools.partial(energy_kernel, n), out_shape=jax.ShapeDt...]
  transfers between devices with their start and end apart: 15 -> 15, of which waited for: 5 -> 6; matrix products, arithmetic and copies ran while one was open for 1% -> 1% of each run, Pallas kernels for 13% -> 11%
where the time goes in v5:
time: 128 us; the launch traced here: 127 us
  waiting for transfers between devices  67.5 us (53%)
  Pallas kernels  37.4 us (29%)
  starting transfers between devices  17 us (13%)
  between operations  3.23 us (3%)
  local copies, waits for them, and re-layouts  2.22 us (2%)
    ppermute x15, waiting for transfers between devices, move(): return lax.ppermute(x, 'row', perm)  67.5 us
    pallas_call x9, Pallas kernels, pair_call(): pl.pallas_call(functools.partial(pair_kernel, cfg), out_shape=out_shape,...  20.2 us
    ppermute x15, starting transfers between devices, move(): return lax.ppermute(x, 'row', perm)  17 us
    pallas_call x1, Pallas kernels, total_energy(): pl.pallas_call(functools.partial(energy_kernel, n), out_shape=jax.ShapeDt...  15.2 us
  transfers between devices with their start and end apart: 15, of which 6 were waited for; matrix products, arithmetic and copies ran while one was open for 1% of the time, Pallas kernels for 11%

profile of v5, /device:TPU:112, one launch (start us, length us, event | category | flops | bytes accessed | tf_op | source)
XLA Modules:
  0.0 127.3 jit_solution(15673367744162222276)
XLA Ops:
  0.6 0.1 collective-permute-start.11
  0.7 1.6 %fusion = (bf16[1024,384]{1,0:T(8,128)(2,1)S(1)}, bf16[1024,384]{1,0:T(8,128)(2,1)S(1)}) fusion(bf16[2048,384]{1,0:T(8,128)(2,1)} %pos_ref.1), kind=kLoop, calls=%fused_computation | loop fusion | bytes 3145728 | tf_op jit(solution)/shard_map/slice | solution.py:342
  2.4 4.0 %collective-permute-start.10 = (bf16[1024,384]{1,0:T(8,128)(2,1)S(1)}, bf16[1024,384]{1,0:T(8,128)(2,1)S(1)}, u32[]{:S(2)}, u32[]{:S(2)}) collective-permute-start(bf16[1024,384]{1,0:T(8,128)(2,1)S(1)} %get-tuple-element.140), channel_id=1, source_target_pairs={{2,0},{7,1},{4,2},{1,3},{6,4},{3,5},{0,6},{5,7},{10,8},{15,9},{12,... | collective-permute-start | bytes 2359304 | tf_op jit(solution)/shard_map/ppermute | solution.py:321
  6.3 0.0 collective-permute-start.9
  7.0 1.9 %begin.1 = (f32[3,16,128]{2,1,0:T(8,128)S(1)}, bf16[4352,384]{1,0:T(8,128)(2,1)S(1)}, f32[4352,128]{1,0:T(8,128)S(1)}, f32[4352,128]{1,0:T(8,128)S(1)}, bf16[143...) custom-call(bf16[2048,384]{1,0:T(8,128)(2,1)S(1)} %copy-done, ...), custom_call_target="tpu_custom_call" | custom-call | flops 1073741824 | bytes 1048576 | tf_op jit(solution)/shard_map/begin/pallas_call | solution.py:110
  8.9 0.3 collective-permute-start
  9.2 3.1 %collective-permute-start.8 = (bf16[1024,384]{1,0:T(8,128)(2,1)S(1)}, bf16[1024,384]{1,0:T(8,128)(2,1)S(1)}, u32[]{:S(2)}, u32[]{:S(2)}) collective-permute-start(bf16[1024,384]{1,0:T(8,128)(2,1)S(1)} %get-tuple-element.141), channel_id=1, source_target_pairs={{2,0},{7,1},{4,2},{1,3},{6,4},{3,5},{0,6},{5,7},{10,8},{15,9},{12,... | collective-permute-start | bytes 2359304 | tf_op jit(solution)/shard_map/ppermute | solution.py:321
  12.4 0.0 collective-permute-start.5
  12.4 0.0 collective-permute-done.11.refs_2_
  12.4 3.2 %collective-permute-start.2 = (f32[3,16,128]{2,1,0:T(8,128)S(1)}, f32[3,16,128]{2,1,0:T(8,128)S(1)}, u32[]{:S(2)}, u32[]{:S(2)}) collective-permute-start(f32[3,16,128]{2,1,0:T(8,128)S(1)} %get-tuple-element.71.refs_0_), channel_id=1, source_target_pairs={{2,0},{7,1},{4,2},{1,3},{6,4},{3,5},{0,6},{5,7},{10,8},{15,9},{12,... | collective-permute-start | bytes 73736 | tf_op jit(solution)/shard_map/ppermute | solution.py:321
  15.6 2.7 %shard_map.50 = (bf16[4352,384]{1,0:T(8,128)(2,1)S(1)}, f32[4352,128]{1,0:T(8,128)S(1)}, f32[4352,128]{1,0:T(8,128)S(1)}, bf16[14336,384]{1,0:T(8,128)(2,1)S(1)}...) custom-call(f32[3,16,128]{2,1,0:T(8,128)S(1)} %get-tuple-element.71., ...), custom_call_target="tpu_custom_call", output_to_operand_aliasing={{0}: (3, {}), {1}: (4, {}), {2}: (5, {}), {3}: (6, {}), {4}... | custom-call | flops 1073741824 | bytes 1048576 | tf_op jit(solution)/shard_map/pallas_call | solution.py:300
  18.3 22.6 %collective-permute-done.2.refs_3_ = f32[3,16,128]{2,1,0:T(8,128)S(1)} collective-permute-done((f32[3,16,128]{2,1,0:T(8,128)S(1)}, f32[3,16,128]{2,1,0:T(8,128)S(1)}, u32[]{:S(2)}, u32[]{:S(2)}) %collective-permute-start.2) | collective-permute-done | bytes 24608 | tf_op jit(solution)/shard_map/ppermute | solution.py:321
  40.9 0.9 collective-permute-start.1
  41.8 0.1 shard_map.51
  42.0 4.4 %collective-permute-done.1.refs_2_ = f32[3,16,128]{2,1,0:T(8,128)S(1)} collective-permute-done((f32[3,16,128]{2,1,0:T(8,128)S(1)}, f32[3,16,128]{2,1,0:T(8,128)S(1)}, u32[]{:S(2)}, u32[]{:S(2)}) %collective-permute-start.1) | collective-permute-done | bytes 24608 | tf_op jit(solution)/shard_map/ppermute | solution.py:321
  46.4 4.9 %shard_map.52 = (bf16[4352,384]{1,0:T(8,128)(2,1)S(1)}, f32[4352,128]{1,0:T(8,128)S(1)}, f32[4352,128]{1,0:T(8,128)S(1)}, bf16[14336,384]{1,0:T(8,128)(2,1)S(1)}...) custom-call(f32[3,16,128]{2,1,0:T(8,128)S(1)} %get-tuple-element.71., ...), custom_call_target="tpu_custom_call", output_to_operand_aliasing={{0}: (6, {}), {1}: (7, {}), {2}: (8, {}), {3}: (9, {}), {4}... | custom-call | flops 1073741824 | bytes 1048576 | tf_op jit(solution)/shard_map/pallas_call | solution.py:300
  51.3 5.6 %shard_map.53 = (bf16[4352,384]{1,0:T(8,128)(2,1)S(1)}, f32[4352,128]{1,0:T(8,128)S(1)}, f32[4352,128]{1,0:T(8,128)S(1)}, bf16[14336,384]{1,0:T(8,128)(2,1)S(1)}...) custom-call(f32[3,16,128]{2,1,0:T(8,128)S(1)} %get-tuple-element.71., ...), custom_call_target="tpu_custom_call", output_to_operand_aliasing={{0}: (6, {}), {1}: (7, {}), {2}: (8, {}), {3}: (9, {}), {4}... | custom-call | flops 1073741824 | bytes 1048576 | tf_op jit(solution)/shard_map/pallas_call | solution.py:300
  56.9 0.1 collective-permute-start.12
  57.0 0.1 collective-permute-start.13
  57.1 4.1 %collective-permute-start.6 = (bf16[1024,384]{1,0:T(8,128)(2,1)S(1)}, bf16[1024,384]{1,0:T(8,128)(2,1)S(1)}, u32[]{:S(2)}, u32[]{:S(2)}) collective-permute-start(bf16[1024,384]{1,0:T(8,128)(2,1)S(1)} %collective-permute-done.5.refs_4_), channel_id=1, source_target_pairs={{0,2},{1,7},{2,4},{3,1},{4,6},{5,3},{6,0},{7,5},{8,10},{9,15},{10,... | collective-permute-start | bytes 2359304 | tf_op jit(solution)/shard_map/ppermute | solution.py:321
  61.3 27.7 %collective-permute-done.13.refs_5_ = bf16[1024,384]{1,0:T(8,128)(2,1)S(1)} collective-permute-done((bf16[1024,384]{1,0:T(8,128)(2,1)S(1)}, bf16[1024,384]{1,0:T(8,128)(2,1)S(1)}, u32[]{:S(2)}, u32[]{:S(2)}) %collective-permute-start.13) | collective-permute-done | bytes 786464 | tf_op jit(solution)/shard_map/ppermute | solution.py:321
  88.9 8.4 %collective-permute-done.6.refs_6_ = bf16[1024,384]{1,0:T(8,128)(2,1)S(1)} collective-permute-done((bf16[1024,384]{1,0:T(8,128)(2,1)S(1)}, bf16[1024,384]{1,0:T(8,128)(2,1)S(1)}, u32[]{:S(2)}, u32[]{:S(2)}) %collective-permute-start.6) | collective-permute-done | bytes 786464 | tf_op jit(solution)/shard_map/ppermute | solution.py:321
  97.4 1.0 collective-permute-start.3
  98.4 4.3 %collective-permute-done.3.refs_4_ = f32[3,16,128]{2,1,0:T(8,128)S(1)} collective-permute-done((f32[3,16,128]{2,1,0:T(8,128)S(1)}, f32[3,16,128]{2,1,0:T(8,128)S(1)}, u32[]{:S(2)}, u32[]{:S(2)}) %collective-permute-start.3) | collective-permute-done | bytes 24608 | tf_op jit(solution)/shard_map/ppermute | solution.py:321
  102.7 1.1 shard_map.54
  103.8 0.1 collective-permute-done.4.refs_5_
  103.9 1.1 shard_map.55
  105.0 1.3 %shard_map.56 = (bf16[4352,384]{1,0:T(8,128)(2,1)S(1)}, f32[4352,128]{1,0:T(8,128)S(1)}, f32[4352,128]{1,0:T(8,128)S(1)}, bf16[14336,384]{1,0:T(8,128)(2,1)S(1)}...) custom-call(f32[3,16,128]{2,1,0:T(8,128)S(1)} %get-tuple-element.71., ...), custom_call_target="tpu_custom_call", output_to_operand_aliasing={{0}: (7, {}), {1}: (8, {}), {2}: (9, {}), {3}: (10, {}), {4... | custom-call | flops 1073741824 | bytes 1048576 | tf_op jit(solution)/shard_map/pallas_call | solution.py:300
  106.3 0.3 shard_map.57
  106.7 3.1 %shard_map.58 = (bf16[4352,384]{1,0:T(8,128)(2,1)S(1)}, f32[4352,128]{1,0:T(8,128)S(1)}, f32[4352,128]{1,0:T(8,128)S(1)}, bf16[14336,384]{1,0:T(8,128)(2,1)S(1)}...) custom-call(f32[3,16,128]{2,1,0:T(8,128)S(1)} %get-tuple-element.71., ...), custom_call_target="tpu_custom_call", output_to_operand_aliasing={{0}: (7, {}), {1}: (8, {}), {2}: (9, {}), {3}: (10, {}), {4... | custom-call | flops 1073741824 | bytes 1048576 | tf_op jit(solution)/shard_map/pallas_call | solution.py:300
  109.7 0.6 copy-done.1
  110.3 15.2 %energy.1 = f32[1]{0:T(128)} custom-call(f32[8,128]{1,0:T(8,128)} %copy-done.1), custom_call_target="tpu_custom_call" | custom-call | tf_op jit(solution)/shard_map/energy/pallas_call | solution.py:48
  (16 shorter events, 0.0 us)
Async XLA Ops:
  0.6 6.4 %copy-start = (bf16[2048,384]{1,0:T(8,128)(2,1)S(1)}, bf16[2048,384]{1,0:T(8,128)(2,1)}, u32[]{:S(2)}) copy-start(bf16[2048,384]{1,0:T(8,128)(2,1)} %pos_ref.1) | copy-start | bytes 4718596
  0.6 6.4 %copy-start.2 = (f32[2048]{0:T(1024)S(1)}, f32[2048]{0:T(1024)}, u32[]{:S(2)}) copy-start(f32[2048]{0:T(1024)} %param.4) | copy-start | bytes 24580
  0.6 11.7 %collective-permute-start.11 = (bf16[2048,384]{1,0:T(8,128)(2,1)}, bf16[2048,384]{1,0:T(8,128)(2,1)S(1)}, u32[]{:S(2)}, u32[]{:S(2)}) collective-permute-start(bf16[2048,384]{1,0:T(8,128)(2,1)} %pos_ref.1), channel_id=1, source_target_pairs={{0,1},{1,0},{2,3},{3,2},{4,5},{5,4},{6,7},{7,6},{8,9},{9,8},{10,11... | collective-permute-start | bytes 4718600 | tf_op jit(solution)/shard_map/ppermute | solution.py:321
  2.4 44.0 %collective-permute-start.10 = (bf16[1024,384]{1,0:T(8,128)(2,1)S(1)}, bf16[1024,384]{1,0:T(8,128)(2,1)S(1)}, u32[]{:S(2)}, u32[]{:S(2)}) collective-permute-start(bf16[1024,384]{1,0:T(8,128)(2,1)S(1)} %get-tuple-element.140), channel_id=1, source_target_pairs={{2,0},{7,1},{4,2},{1,3},{6,4},{3,5},{0,6},{5,7},{10,8},{15,9},{12,... | collective-permute-start | bytes 2359304 | tf_op jit(solution)/shard_map/ppermute | solution.py:321
  6.3 40.1 %collective-permute-start.9 = (bf16[1024,384]{1,0:T(8,128)(2,1)S(1)}, bf16[1024,384]{1,0:T(8,128)(2,1)S(1)}, u32[]{:S(2)}, u32[]{:S(2)}) collective-permute-start(bf16[1024,384]{1,0:T(8,128)(2,1)S(1)} %get-tuple-element.140), channel_id=1, source_target_pairs={{0,2},{1,7},{2,4},{3,1},{4,6},{5,3},{6,0},{7,5},{8,10},{9,15},{10,... | collective-permute-start | bytes 2359304 | tf_op jit(solution)/shard_map/ppermute | solution.py:321
  8.9 3.4 %collective-permute-start = (f32[3,16,128]{2,1,0:T(8,128)S(1)}, f32[3,16,128]{2,1,0:T(8,128)S(1)}, u32[]{:S(2)}, u32[]{:S(2)}) collective-permute-start(f32[3,16,128]{2,1,0:T(8,128)S(1)} %get-tuple-element.71.refs_0_), channel_id=1, source_target_pairs={{0,1},{1,0},{2,3},{3,2},{4,5},{5,4},{6,7},{7,6},{8,9},{9,8},{10,11... | collective-permute-start | bytes 73736 | tf_op jit(solution)/shard_map/ppermute | solution.py:321
  9.2 42.1 %collective-permute-start.8 = (bf16[1024,384]{1,0:T(8,128)(2,1)S(1)}, bf16[1024,384]{1,0:T(8,128)(2,1)S(1)}, u32[]{:S(2)}, u32[]{:S(2)}) collective-permute-start(bf16[1024,384]{1,0:T(8,128)(2,1)S(1)} %get-tuple-element.141), channel_id=1, source_target_pairs={{2,0},{7,1},{4,2},{1,3},{6,4},{3,5},{0,6},{5,7},{10,8},{15,9},{12,... | collective-permute-start | bytes 2359304 | tf_op jit(solution)/shard_map/ppermute | solution.py:321
  12.4 39.0 %collective-permute-start.5 = (bf16[1024,384]{1,0:T(8,128)(2,1)S(1)}, bf16[1024,384]{1,0:T(8,128)(2,1)S(1)}, u32[]{:S(2)}, u32[]{:S(2)}) collective-permute-start(bf16[1024,384]{1,0:T(8,128)(2,1)S(1)} %get-tuple-element.141), channel_id=1, source_target_pairs={{0,2},{1,7},{2,4},{3,1},{4,6},{5,3},{6,0},{7,5},{8,10},{9,15},{10,... | collective-permute-start | bytes 2359304 | tf_op jit(solution)/shard_map/ppermute | solution.py:321
  12.4 28.5 %collective-permute-start.2 = (f32[3,16,128]{2,1,0:T(8,128)S(1)}, f32[3,16,128]{2,1,0:T(8,128)S(1)}, u32[]{:S(2)}, u32[]{:S(2)}) collective-permute-start(f32[3,16,128]{2,1,0:T(8,128)S(1)} %get-tuple-element.71.refs_0_), channel_id=1, source_target_pairs={{2,0},{7,1},{4,2},{1,3},{6,4},{3,5},{0,6},{5,7},{10,8},{15,9},{12,... | collective-permute-start | bytes 73736 | tf_op jit(solution)/shard_map/ppermute | solution.py:321
  40.9 5.5 %collective-permute-start.1 = (f32[3,16,128]{2,1,0:T(8,128)S(1)}, f32[3,16,128]{2,1,0:T(8,128)S(1)}, u32[]{:S(2)}, u32[]{:S(2)}) collective-permute-start(f32[3,16,128]{2,1,0:T(8,128)S(1)} %get-tuple-element.71.refs_0_), channel_id=1, source_target_pairs={{0,2},{1,7},{2,4},{3,1},{4,6},{5,3},{6,0},{7,5},{8,10},{9,15},{10,... | collective-permute-start | bytes 73736 | tf_op jit(solution)/shard_map/ppermute | solution.py:321
  56.9 48.1 %collective-permute-start.12 = (f32[392,2048]{1,0:T(8,128)S(1)}, f32[392,2048]{1,0:T(8,128)S(1)}, u32[]{:S(2)}, u32[]{:S(2)}) collective-permute-start(f32[392,2048]{1,0:T(8,128)S(1)} %get-tuple-element.100), channel_id=1, source_target_pairs={{0,1},{1,0},{2,3},{3,2},{4,5},{5,4},{6,7},{7,6},{8,9},{9,8},{10,11... | collective-permute-start | bytes 9633800 | tf_op jit(solution)/shard_map/ppermute | solution.py:321
  57.0 31.9 %collective-permute-start.13 = (bf16[1024,384]{1,0:T(8,128)(2,1)S(1)}, bf16[1024,384]{1,0:T(8,128)(2,1)S(1)}, u32[]{:S(2)}, u32[]{:S(2)}) collective-permute-start(bf16[1024,384]{1,0:T(8,128)(2,1)S(1)} %collective-permute-done.9.refs_4_), channel_id=1, source_target_pairs={{0,2},{1,7},{2,4},{3,1},{4,6},{5,3},{6,0},{7,5},{8,10},{9,15},{10,... | collective-permute-start | bytes 2359304 | tf_op jit(solution)/shard_map/ppermute | solution.py:321
  57.1 40.2 %collective-permute-start.6 = (bf16[1024,384]{1,0:T(8,128)(2,1)S(1)}, bf16[1024,384]{1,0:T(8,128)(2,1)S(1)}, u32[]{:S(2)}, u32[]{:S(2)}) collective-permute-start(bf16[1024,384]{1,0:T(8,128)(2,1)S(1)} %collective-permute-done.5.refs_4_), channel_id=1, source_target_pairs={{0,2},{1,7},{2,4},{3,1},{4,6},{5,3},{6,0},{7,5},{8,10},{9,15},{10,... | collective-permute-start | bytes 2359304 | tf_op jit(solution)/shard_map/ppermute | solution.py:321
  88.9 15.0 %collective-permute-start.14 = (bf16[1024,384]{1,0:T(8,128)(2,1)S(1)}, bf16[1024,384]{1,0:T(8,128)(2,1)S(1)}, u32[]{:S(2)}, u32[]{:S(2)}) collective-permute-start(bf16[1024,384]{1,0:T(8,128)(2,1)S(1)} %collective-permute-done.13.refs_5_), channel_id=1, source_target_pairs={{0,1},{1,0},{2,3},{3,2},{4,5},{5,4},{6,7},{7,6},{8,9},{9,8},{10,11... | collective-permute-start | bytes 2359304 | tf_op jit(solution)/shard_map/ppermute | solution.py:321
  97.4 9.3 %collective-permute-start.7 = (bf16[1024,384]{1,0:T(8,128)(2,1)S(1)}, bf16[1024,384]{1,0:T(8,128)(2,1)S(1)}, u32[]{:S(2)}, u32[]{:S(2)}) collective-permute-start(bf16[1024,384]{1,0:T(8,128)(2,1)S(1)} %collective-permute-done.6.refs_6_), channel_id=1, source_target_pairs={{0,1},{1,0},{2,3},{3,2},{4,5},{5,4},{6,7},{7,6},{8,9},{9,8},{10,11... | collective-permute-start | bytes 2359304 | tf_op jit(solution)/shard_map/ppermute | solution.py:321
  97.4 5.3 %collective-permute-start.3 = (f32[3,16,128]{2,1,0:T(8,128)S(1)}, f32[3,16,128]{2,1,0:T(8,128)S(1)}, u32[]{:S(2)}, u32[]{:S(2)}) collective-permute-start(f32[3,16,128]{2,1,0:T(8,128)S(1)} %get-tuple-element.71.refs_0_), channel_id=1, source_target_pairs={{0,4},{1,5},{2,6},{3,7},{4,0},{5,1},{6,2},{7,3},{8,12},{9,13},{10,... | collective-permute-start | bytes 73736 | tf_op jit(solution)/shard_map/ppermute | solution.py:321
  102.7 1.2 collective-permute-start.4
  109.7 0.6 copy-start.1

commit v6 on v5

--- a/solution.py
+++ b/solution.py
@@ -13,9 +13,8 @@
 TILE_I = 256
 TILE_J = 512
 UNROLL = 4
-FIRST_BUDGET = 22
-BUDGET = 38
-VMEM_MB = (5, 4, 6, 9, 5, 5, 8, 5, 9)
+BUDGET = 74
+VMEM_MB = (5, 6, 9, 5, 5, 8, 5, 9)
 MESH = pl.DeviceIdType.MESH
 VMEM_SPEC = pl.BlockSpec(memory_space=pltpu.VMEM)
 
@@ -153,13 +152,11 @@
         tiles = tiles_own if cfg['modes'][stage] == 'own' else tiles_both
         have = pl.cdiv(end, TILE_J) if cfg['close'][stage] else end // TILE_J
         budget = cfg['budget'][stage]
-        hi = have if budget is None else jnp.minimum(have, lo + budget // jnp.maximum(tiles, 1))
+        hi = have if budget is None else jnp.minimum(have, jnp.maximum(lo, budget // jnp.maximum(tiles, 1)))
         if stage < this:
             lo = hi
         if cfg['close'][stage]:
             end = up(end, TILE_J)
-    units = (hi - lo) * tiles
-
     if this == 0:
         x_row[pl.ds(row_mate, rows), :] = mate_pos[...]
         spread(metas['mate'], h_rows, c_rows, row_mate)
@@ -177,11 +174,6 @@
                 d = slice(k * LANES, (k + 1) * LANES)
                 turned[at, d] = (pulls[d, at] + incoming[d, at]).T
 
-    def decode(unit):
-        at = jnp.minimum(unit, units - 1)
-        j = at // tiles
-        return (at - j * tiles) * TILE_I, (j + lo) * TILE_J
-
     def aligned(pos):
         return pl.ds(pl.multiple_of(pos[0], TILE_I), TILE_I), pl.ds(pl.multiple_of(pos[1], TILE_J), TILE_J)
 
@@ -189,7 +181,7 @@
         row, col = aligned(pos)
         out[...] = lax.dot_general(x_row[row, :], x_col[col, :], (((1,), (1,)), ((), ())), preferred_element_type=jnp.float32)
 
-    def weigh(pos, prod):
+    def weigh(pos, prod, diag):
         row, col = aligned(pos)
         h_row, c_row = h_rows[row, :], c_rows[row, :]
         parts, total = [], None
@@ -197,7 +189,7 @@
             at = pl.ds(pl.multiple_of(pos[1] + k * LANES, LANES), LANES)
             arg = jnp.minimum(prod[:, k * LANES:(k + 1) * LANES] * (2.0 * scale) - h_row - cols[1:2, at], 0.0)
             w = jnp.exp2(arg) * c_row * cols[0:1, at]
-            if this < 2:
+            if diag:
                 off = pos[1] + k * LANES
                 off = jnp.where(off < row_mate, off - pos[0], 1 << 20)
                 w = jnp.where(lax.broadcasted_iota(jnp.int32, (TILE_I, LANES), 0) - lax.broadcasted_iota(jnp.int32, (TILE_I, LANES), 1) == off, 0.0, w)
@@ -210,27 +202,48 @@
         else:
             turned[row, :] += jnp.dot(low, x_col[col, :], preferred_element_type=jnp.float32)
 
-    @pl.when((units > 0) if cfg['plan'][this] or this < 2 else False)
-    def _():
-        first = decode(0)
-        gram(first, gram_a)
-
-        def step(p, pos):
-            for k in range(UNROLL):
-                nxt = decode(UNROLL * p + k + 1)
-                gram(nxt, (gram_a, gram_b)[(k + 1) % 2])
-                weigh(pos, (gram_a, gram_b)[k % 2])
-                pos = nxt
-            return pos
-
-        def single(unit, pos):
-            nxt = decode(unit + 1)
-            weigh(pos, gram_a)
-            gram(nxt, gram_a)
-            return nxt
-
-        whole = units // UNROLL
-        lax.fori_loop(whole * UNROLL, units, single, lax.fori_loop(0, whole, step, first))
+    def run(units, decode, unroll, diag=False):
+        @pl.when(units > 0)
+        def _():
+            first = decode(0)
+            gram(first, gram_a)
+
+            def step(p, pos):
+                for k in range(unroll):
+                    nxt = decode(jnp.minimum(unroll * p + k + 1, units - 1))
+                    gram(nxt, (gram_a, gram_b)[(k + 1) % 2])
+                    weigh(pos, (gram_a, gram_b)[k % 2], diag)
+                    pos = nxt
+                return pos
+
+            def single(unit, pos):
+                nxt = decode(jnp.minimum(unit + 1, units - 1))
+                weigh(pos, gram_a, diag)
+                gram(nxt, gram_a)
+                return nxt
+
+            whole = units // unroll
+            last = lax.fori_loop(0, whole, step, first)
+            if not diag:
+                lax.fori_loop(whole * unroll, units, single, last)
+
+    if this == 0:
+        per_col = TILE_J // TILE_I
+        rest = jnp.maximum(tiles - per_col, per_col * hi - per_col)
+
+        def off_diag(unit):
+            j = unit // jnp.maximum(rest, 1)
+            i = unit - j * rest
+            return jnp.where(i < per_col * j, i, i + per_col) * TILE_I, j * TILE_J
+
+        run(per_col * hi, lambda unit: (unit * TILE_I, unit // per_col * TILE_J), per_col, diag=True)
+        run(jnp.where(rest > 0, rest * hi, 0), off_diag, UNROLL)
+    elif cfg['loads']:
+        def plain(unit):
+            j = unit // tiles
+            return (unit - j * tiles) * TILE_I, (j + lo) * TILE_J
+
+        run((hi - lo) * tiles, plain, UNROLL)
 
     if this == cfg['split']:
         lane = lax.broadcasted_iota(jnp.int32, (LANES, LANES), 1)
@@ -330,13 +343,13 @@
         def lower(name):
             return name, half_rows, block_rows - half_rows
 
-        plan = [[('own', 0, block_rows)], [], [upper('near'), upper('next')], [lower('near'), lower('next')],
+        plan = [[('own', 0, block_rows)], [upper('near'), upper('next')], [lower('near'), lower('next')],
                 [upper('far')], [upper('away')], [], [lower('far')], [lower('away')]]
         null = up(sum(c[2] for stage in plan for c in stage), TILE_J) + 8 * TILE_J
-        cfg = dict(rows=block_rows, width=width, null=null, plan=plan, modes=['both'] * 4 + ['own'] * 5,
-                   close=[True, True, False, True, False, False, False, False, True],
-                   budget=[FIRST_BUDGET, None, BUDGET] + [None] * 6,
-                   split=3, turn=6, scale=math.log2(math.e) * 0.5 / width, inv_len2=1.0 / width)
+        cfg = dict(rows=block_rows, width=width, null=null, plan=plan, modes=['both'] * 3 + ['own'] * 5,
+                   close=[True, False, True, False, False, False, False, True],
+                   budget=[None, BUDGET] + [None] * 6,
+                   split=2, turn=5, scale=math.log2(math.e) * 0.5 / width, inv_len2=1.0 / width)
 
         mate_pos = move(positions, swap)
         top, bottom = positions[:half_rows], positions[half_rows:]
@@ -348,7 +361,7 @@
         far_meta = move(meta, twice)
         metas = {'own': meta, 'mate': move(meta, swap), 'near': move(meta, forth), 'next': move(meta, back),
                  'far': far_meta, 'away': move(far_meta, swap)}
-        arrays = [[positions], [], [near_a, next_a], [near_b, next_b], [far_a], [away_a], [], [far_b], [away_b]]
+        arrays = [[positions], [near_a, next_a], [near_b, next_b], [far_a], [away_a], [], [far_b], [away_b]]
         incoming = None
         for stage in range(len(plan)):
             state, out = pair_call(cfg, stage, metas, arrays[stage], state, mate_pos=mate_pos if stage == 0 else None,

time: 128 us -> 116 us (0.906)
  waiting for transfers between devices: 67.5 us -> 54.8 us
    ppermute x15, waiting for transfers between devices: 67.5 us -> 54.8 us  [move(): return lax.ppermute(x, 'row', perm)]
    pallas_call x9 -> x8, Pallas kernels: 20.2 us -> 20.4 us  [pair_call(): pl.pallas_call(functools.partial(pair_kernel, cfg), out_shape=out_shape,...]
  transfers between devices with their start and end apart: 15 -> 15, of which waited for: 6 -> 5; matrix products, arithmetic and copies ran while one was open for 1% -> 1% of each run, Pallas kernels for 11% -> 12%
where the time goes in v6:
time: 116 us; the launch traced here: 115 us
  waiting for transfers between devices  54.8 us (47%)
  Pallas kernels  37.6 us (32%)
  starting transfers between devices  17.4 us (15%)
  between operations  3.3 us (3%)
  local copies, waits for them, and re-layouts  2.21 us (2%)
    ppermute x15, waiting for transfers between devices, move(): return lax.ppermute(x, 'row', perm)  54.8 us
    pallas_call x8, Pallas kernels, pair_call(): pl.pallas_call(functools.partial(pair_kernel, cfg), out_shape=out_shape,...  20.4 us
    ppermute x15, starting transfers between devices, move(): return lax.ppermute(x, 'row', perm)  17.4 us
    pallas_call x1, Pallas kernels, total_energy(): pl.pallas_call(functools.partial(energy_kernel, n), out_shape=jax.ShapeDt...  15.2 us
  transfers between devices with their start and end apart: 15, of which 5 were waited for; matrix products, arithmetic and copies ran while one was open for 1% of the time, Pallas kernels for 12%

profile of v6, /device:TPU:112, one launch (start us, length us, event | category | flops | bytes accessed | tf_op | source)
XLA Modules:
  0.0 115.2 jit_solution(12158845151241792415)
XLA Ops:
  0.6 0.1 collective-permute-start.11
  0.7 1.6 %fusion = (bf16[1024,384]{1,0:T(8,128)(2,1)S(1)}, bf16[1024,384]{1,0:T(8,128)(2,1)S(1)}) fusion(bf16[2048,384]{1,0:T(8,128)(2,1)} %pos_ref.1), kind=kLoop, calls=%fused_computation | loop fusion | bytes 3145728 | tf_op jit(solution)/shard_map/slice | solution.py:355
  2.4 4.0 %collective-permute-start.10 = (bf16[1024,384]{1,0:T(8,128)(2,1)S(1)}, bf16[1024,384]{1,0:T(8,128)(2,1)S(1)}, u32[]{:S(2)}, u32[]{:S(2)}) collective-permute-start(bf16[1024,384]{1,0:T(8,128)(2,1)S(1)} %get-tuple-element.126), channel_id=1, source_target_pairs={{2,0},{7,1},{4,2},{1,3},{6,4},{3,5},{0,6},{5,7},{10,8},{15,9},{12,... | collective-permute-start | bytes 2359304 | tf_op jit(solution)/shard_map/ppermute | solution.py:334
  6.3 0.0 collective-permute-start.9
  7.0 1.9 %begin.1 = (f32[3,16,128]{2,1,0:T(8,128)S(1)}, bf16[4352,384]{1,0:T(8,128)(2,1)S(1)}, f32[4352,128]{1,0:T(8,128)S(1)}, f32[4352,128]{1,0:T(8,128)S(1)}, bf16[143...) custom-call(bf16[2048,384]{1,0:T(8,128)(2,1)S(1)} %copy-done, ...), custom_call_target="tpu_custom_call" | custom-call | flops 1073741824 | bytes 1048576 | tf_op jit(solution)/shard_map/begin/pallas_call | solution.py:109
  8.9 3.3 %collective-permute-start.2 = (f32[3,16,128]{2,1,0:T(8,128)S(1)}, f32[3,16,128]{2,1,0:T(8,128)S(1)}, u32[]{:S(2)}, u32[]{:S(2)}) collective-permute-start(f32[3,16,128]{2,1,0:T(8,128)S(1)} %get-tuple-element.64.refs_0_), channel_id=1, source_target_pairs={{2,0},{7,1},{4,2},{1,3},{6,4},{3,5},{0,6},{5,7},{10,8},{15,9},{12,... | collective-permute-start | bytes 73736 | tf_op jit(solution)/shard_map/ppermute | solution.py:334
  12.3 0.0 collective-permute-start
  12.3 11.8 %collective-permute-done.2.refs_3_ = f32[3,16,128]{2,1,0:T(8,128)S(1)} collective-permute-done((f32[3,16,128]{2,1,0:T(8,128)S(1)}, f32[3,16,128]{2,1,0:T(8,128)S(1)}, u32[]{:S(2)}, u32[]{:S(2)}) %collective-permute-start.2) | collective-permute-done | bytes 24608 | tf_op jit(solution)/shard_map/ppermute | solution.py:334
  24.1 3.7 %collective-permute-start.8 = (bf16[1024,384]{1,0:T(8,128)(2,1)S(1)}, bf16[1024,384]{1,0:T(8,128)(2,1)S(1)}, u32[]{:S(2)}, u32[]{:S(2)}) collective-permute-start(bf16[1024,384]{1,0:T(8,128)(2,1)S(1)} %get-tuple-element.127), channel_id=1, source_target_pairs={{2,0},{7,1},{4,2},{1,3},{6,4},{3,5},{0,6},{5,7},{10,8},{15,9},{12,... | collective-permute-start | bytes 2359304 | tf_op jit(solution)/shard_map/ppermute | solution.py:334
  27.7 0.0 collective-permute-done.refs_1_
  27.8 0.0 collective-permute-start.5
  27.8 0.1 collective-permute-start.1
  27.9 3.3 %shard_map.50 = (bf16[4352,384]{1,0:T(8,128)(2,1)S(1)}, f32[4352,128]{1,0:T(8,128)S(1)}, f32[4352,128]{1,0:T(8,128)S(1)}, bf16[14336,384]{1,0:T(8,128)(2,1)S(1)}...) custom-call(f32[3,16,128]{2,1,0:T(8,128)S(1)} %get-tuple-element.64., ...), custom_call_target="tpu_custom_call", output_to_operand_aliasing={{0}: (3, {}), {1}: (4, {}), {2}: (5, {}), {3}: (6, {}), {4}... | custom-call | flops 1073741824 | bytes 1048576 | tf_op jit(solution)/shard_map/pallas_call | solution.py:313
  31.1 12.4 %collective-permute-done.1.refs_2_ = f32[3,16,128]{2,1,0:T(8,128)S(1)} collective-permute-done((f32[3,16,128]{2,1,0:T(8,128)S(1)}, f32[3,16,128]{2,1,0:T(8,128)S(1)}, u32[]{:S(2)}, u32[]{:S(2)}) %collective-permute-start.1) | collective-permute-done | bytes 24608 | tf_op jit(solution)/shard_map/ppermute | solution.py:334
  43.5 4.8 %shard_map.51 = (bf16[4352,384]{1,0:T(8,128)(2,1)S(1)}, f32[4352,128]{1,0:T(8,128)S(1)}, f32[4352,128]{1,0:T(8,128)S(1)}, bf16[14336,384]{1,0:T(8,128)(2,1)S(1)}...) custom-call(f32[3,16,128]{2,1,0:T(8,128)S(1)} %get-tuple-element.64., ...), custom_call_target="tpu_custom_call", output_to_operand_aliasing={{0}: (6, {}), {1}: (7, {}), {2}: (8, {}), {3}: (9, {}), {4}... | custom-call | flops 1073741824 | bytes 1048576 | tf_op jit(solution)/shard_map/pallas_call | solution.py:313
  48.3 0.0 collective-permute-done.8.refs_5_
  48.4 5.4 %shard_map.52 = (bf16[4352,384]{1,0:T(8,128)(2,1)S(1)}, f32[4352,128]{1,0:T(8,128)S(1)}, f32[4352,128]{1,0:T(8,128)S(1)}, bf16[14336,384]{1,0:T(8,128)(2,1)S(1)}...) custom-call(f32[3,16,128]{2,1,0:T(8,128)S(1)} %get-tuple-element.64., ...), custom_call_target="tpu_custom_call", output_to_operand_aliasing={{0}: (6, {}), {1}: (7, {}), {2}: (8, {}), {3}: (9, {}), {4}... | custom-call | flops 1073741824 | bytes 1048576 | tf_op jit(solution)/shard_map/pallas_call | solution.py:313
  53.7 0.1 collective-permute-start.12
  53.8 0.1 collective-permute-start.13
  54.0 5.0 %collective-permute-start.6 = (bf16[1024,384]{1,0:T(8,128)(2,1)S(1)}, bf16[1024,384]{1,0:T(8,128)(2,1)S(1)}, u32[]{:S(2)}, u32[]{:S(2)}) collective-permute-start(bf16[1024,384]{1,0:T(8,128)(2,1)S(1)} %collective-permute-done.5.refs_4_), channel_id=1, source_target_pairs={{0,2},{1,7},{2,4},{3,1},{4,6},{5,3},{6,0},{7,5},{8,10},{9,15},{10,... | collective-permute-start | bytes 2359304 | tf_op jit(solution)/shard_map/ppermute | solution.py:334
  58.9 17.8 %collective-permute-done.13.refs_5_ = bf16[1024,384]{1,0:T(8,128)(2,1)S(1)} collective-permute-done((bf16[1024,384]{1,0:T(8,128)(2,1)S(1)}, bf16[1024,384]{1,0:T(8,128)(2,1)S(1)}, u32[]{:S(2)}, u32[]{:S(2)}) %collective-permute-start.13) | collective-permute-done | bytes 786464 | tf_op jit(solution)/shard_map/ppermute | solution.py:334
  76.8 8.4 %collective-permute-done.6.refs_6_ = bf16[1024,384]{1,0:T(8,128)(2,1)S(1)} collective-permute-done((bf16[1024,384]{1,0:T(8,128)(2,1)S(1)}, bf16[1024,384]{1,0:T(8,128)(2,1)S(1)}, u32[]{:S(2)}, u32[]{:S(2)}) %collective-permute-start.6) | collective-permute-done | bytes 786464 | tf_op jit(solution)/shard_map/ppermute | solution.py:334
  85.2 1.0 collective-permute-start.3
  86.2 4.3 %collective-permute-done.3.refs_4_ = f32[3,16,128]{2,1,0:T(8,128)S(1)} collective-permute-done((f32[3,16,128]{2,1,0:T(8,128)S(1)}, f32[3,16,128]{2,1,0:T(8,128)S(1)}, u32[]{:S(2)}, u32[]{:S(2)}) %collective-permute-start.3) | collective-permute-done | bytes 24608 | tf_op jit(solution)/shard_map/ppermute | solution.py:334
  90.5 1.3 %shard_map.53 = (bf16[4352,384]{1,0:T(8,128)(2,1)S(1)}, f32[4352,128]{1,0:T(8,128)S(1)}, f32[4352,128]{1,0:T(8,128)S(1)}, bf16[14336,384]{1,0:T(8,128)(2,1)S(1)}...) custom-call(f32[3,16,128]{2,1,0:T(8,128)S(1)} %get-tuple-element.64., ...), custom_call_target="tpu_custom_call", output_to_operand_aliasing={{0}: (6, {}), {1}: (7, {}), {2}: (8, {}), {3}: (9, {}), {4}... | custom-call | flops 1073741824 | bytes 1048576 | tf_op jit(solution)/shard_map/pallas_call | solution.py:313
  91.8 0.0 collective-permute-done.14.refs_6_
  91.8 1.1 shard_map.54
  93.0 1.3 %shard_map.55 = (bf16[4352,384]{1,0:T(8,128)(2,1)S(1)}, f32[4352,128]{1,0:T(8,128)S(1)}, f32[4352,128]{1,0:T(8,128)S(1)}, bf16[14336,384]{1,0:T(8,128)(2,1)S(1)}...) custom-call(f32[3,16,128]{2,1,0:T(8,128)S(1)} %get-tuple-element.64., ...), custom_call_target="tpu_custom_call", output_to_operand_aliasing={{0}: (7, {}), {1}: (8, {}), {2}: (9, {}), {3}: (10, {}), {4... | custom-call | flops 1073741824 | bytes 1048576 | tf_op jit(solution)/shard_map/pallas_call | solution.py:313
  94.3 0.3 shard_map.56
  94.6 3.0 %shard_map.57 = (bf16[4352,384]{1,0:T(8,128)(2,1)S(1)}, f32[4352,128]{1,0:T(8,128)S(1)}, f32[4352,128]{1,0:T(8,128)S(1)}, bf16[14336,384]{1,0:T(8,128)(2,1)S(1)}...) custom-call(f32[3,16,128]{2,1,0:T(8,128)S(1)} %get-tuple-element.64., ...), custom_call_target="tpu_custom_call", output_to_operand_aliasing={{0}: (7, {}), {1}: (8, {}), {2}: (9, {}), {3}: (10, {}), {4... | custom-call | flops 1073741824 | bytes 1048576 | tf_op jit(solution)/shard_map/pallas_call | solution.py:313
  97.6 0.6 copy-done.1
  98.2 15.2 %energy.1 = f32[1]{0:T(128)} custom-call(f32[8,128]{1,0:T(8,128)} %copy-done.1), custom_call_target="tpu_custom_call" | custom-call | tf_op jit(solution)/shard_map/energy/pallas_call | solution.py:47
  (15 shorter events, 0.0 us)
Async XLA Ops:
  0.6 6.4 %copy-start = (bf16[2048,384]{1,0:T(8,128)(2,1)S(1)}, bf16[2048,384]{1,0:T(8,128)(2,1)}, u32[]{:S(2)}) copy-start(bf16[2048,384]{1,0:T(8,128)(2,1)} %pos_ref.1) | copy-start | bytes 4718596
  0.6 6.4 %copy-start.2 = (f32[2048]{0:T(1024)S(1)}, f32[2048]{0:T(1024)}, u32[]{:S(2)}) copy-start(f32[2048]{0:T(1024)} %param.4) | copy-start | bytes 24580
  0.6 27.1 %collective-permute-start.11 = (bf16[2048,384]{1,0:T(8,128)(2,1)}, bf16[2048,384]{1,0:T(8,128)(2,1)S(1)}, u32[]{:S(2)}, u32[]{:S(2)}) collective-permute-start(bf16[2048,384]{1,0:T(8,128)(2,1)} %pos_ref.1), channel_id=1, source_target_pairs={{0,1},{1,0},{2,3},{3,2},{4,5},{5,4},{6,7},{7,6},{8,9},{9,8},{10,11... | collective-permute-start | bytes 4718600 | tf_op jit(solution)/shard_map/ppermute | solution.py:334
  2.4 41.1 %collective-permute-start.10 = (bf16[1024,384]{1,0:T(8,128)(2,1)S(1)}, bf16[1024,384]{1,0:T(8,128)(2,1)S(1)}, u32[]{:S(2)}, u32[]{:S(2)}) collective-permute-start(bf16[1024,384]{1,0:T(8,128)(2,1)S(1)} %get-tuple-element.126), channel_id=1, source_target_pairs={{2,0},{7,1},{4,2},{1,3},{6,4},{3,5},{0,6},{5,7},{10,8},{15,9},{12,... | collective-permute-start | bytes 2359304 | tf_op jit(solution)/shard_map/ppermute | solution.py:334
  6.3 37.2 %collective-permute-start.9 = (bf16[1024,384]{1,0:T(8,128)(2,1)S(1)}, bf16[1024,384]{1,0:T(8,128)(2,1)S(1)}, u32[]{:S(2)}, u32[]{:S(2)}) collective-permute-start(bf16[1024,384]{1,0:T(8,128)(2,1)S(1)} %get-tuple-element.126), channel_id=1, source_target_pairs={{0,2},{1,7},{2,4},{3,1},{4,6},{5,3},{6,0},{7,5},{8,10},{9,15},{10,... | collective-permute-start | bytes 2359304 | tf_op jit(solution)/shard_map/ppermute | solution.py:334
  8.9 15.1 %collective-permute-start.2 = (f32[3,16,128]{2,1,0:T(8,128)S(1)}, f32[3,16,128]{2,1,0:T(8,128)S(1)}, u32[]{:S(2)}, u32[]{:S(2)}) collective-permute-start(f32[3,16,128]{2,1,0:T(8,128)S(1)} %get-tuple-element.64.refs_0_), channel_id=1, source_target_pairs={{2,0},{7,1},{4,2},{1,3},{6,4},{3,5},{0,6},{5,7},{10,8},{15,9},{12,... | collective-permute-start | bytes 73736 | tf_op jit(solution)/shard_map/ppermute | solution.py:334
  12.3 15.5 %collective-permute-start = (f32[3,16,128]{2,1,0:T(8,128)S(1)}, f32[3,16,128]{2,1,0:T(8,128)S(1)}, u32[]{:S(2)}, u32[]{:S(2)}) collective-permute-start(f32[3,16,128]{2,1,0:T(8,128)S(1)} %get-tuple-element.64.refs_0_), channel_id=1, source_target_pairs={{0,1},{1,0},{2,3},{3,2},{4,5},{5,4},{6,7},{7,6},{8,9},{9,8},{10,11... | collective-permute-start | bytes 73736 | tf_op jit(solution)/shard_map/ppermute | solution.py:334
  24.1 24.3 %collective-permute-start.8 = (bf16[1024,384]{1,0:T(8,128)(2,1)S(1)}, bf16[1024,384]{1,0:T(8,128)(2,1)S(1)}, u32[]{:S(2)}, u32[]{:S(2)}) collective-permute-start(bf16[1024,384]{1,0:T(8,128)(2,1)S(1)} %get-tuple-element.127), channel_id=1, source_target_pairs={{2,0},{7,1},{4,2},{1,3},{6,4},{3,5},{0,6},{5,7},{10,8},{15,9},{12,... | collective-permute-start | bytes 2359304 | tf_op jit(solution)/shard_map/ppermute | solution.py:334
  27.8 20.6 %collective-permute-start.5 = (bf16[1024,384]{1,0:T(8,128)(2,1)S(1)}, bf16[1024,384]{1,0:T(8,128)(2,1)S(1)}, u32[]{:S(2)}, u32[]{:S(2)}) collective-permute-start(bf16[1024,384]{1,0:T(8,128)(2,1)S(1)} %get-tuple-element.127), channel_id=1, source_target_pairs={{0,2},{1,7},{2,4},{3,1},{4,6},{5,3},{6,0},{7,5},{8,10},{9,15},{10,... | collective-permute-start | bytes 2359304 | tf_op jit(solution)/shard_map/ppermute | solution.py:334
  27.8 15.7 %collective-permute-start.1 = (f32[3,16,128]{2,1,0:T(8,128)S(1)}, f32[3,16,128]{2,1,0:T(8,128)S(1)}, u32[]{:S(2)}, u32[]{:S(2)}) collective-permute-start(f32[3,16,128]{2,1,0:T(8,128)S(1)} %get-tuple-element.64.refs_0_), channel_id=1, source_target_pairs={{0,2},{1,7},{2,4},{3,1},{4,6},{5,3},{6,0},{7,5},{8,10},{9,15},{10,... | collective-permute-start | bytes 73736 | tf_op jit(solution)/shard_map/ppermute | solution.py:334
  53.7 39.2 %collective-permute-start.12 = (f32[392,2048]{1,0:T(8,128)S(1)}, f32[392,2048]{1,0:T(8,128)S(1)}, u32[]{:S(2)}, u32[]{:S(2)}) collective-permute-start(f32[392,2048]{1,0:T(8,128)S(1)} %get-tuple-element.86), channel_id=1, source_target_pairs={{0,1},{1,0},{2,3},{3,2},{4,5},{5,4},{6,7},{7,6},{8,9},{9,8},{10,11... | collective-permute-start | bytes 9633800 | tf_op jit(solution)/shard_map/ppermute | solution.py:334
  53.8 22.9 %collective-permute-start.13 = (bf16[1024,384]{1,0:T(8,128)(2,1)S(1)}, bf16[1024,384]{1,0:T(8,128)(2,1)S(1)}, u32[]{:S(2)}, u32[]{:S(2)}) collective-permute-start(bf16[1024,384]{1,0:T(8,128)(2,1)S(1)} %collective-permute-done.9.refs_4_), channel_id=1, source_target_pairs={{0,2},{1,7},{2,4},{3,1},{4,6},{5,3},{6,0},{7,5},{8,10},{9,15},{10,... | collective-permute-start | bytes 2359304 | tf_op jit(solution)/shard_map/ppermute | solution.py:334
  54.0 31.2 %collective-permute-start.6 = (bf16[1024,384]{1,0:T(8,128)(2,1)S(1)}, bf16[1024,384]{1,0:T(8,128)(2,1)S(1)}, u32[]{:S(2)}, u32[]{:S(2)}) collective-permute-start(bf16[1024,384]{1,0:T(8,128)(2,1)S(1)} %collective-permute-done.5.refs_4_), channel_id=1, source_target_pairs={{0,2},{1,7},{2,4},{3,1},{4,6},{5,3},{6,0},{7,5},{8,10},{9,15},{10,... | collective-permute-start | bytes 2359304 | tf_op jit(solution)/shard_map/ppermute | solution.py:334
  76.8 15.1 %collective-permute-start.14 = (bf16[1024,384]{1,0:T(8,128)(2,1)S(1)}, bf16[1024,384]{1,0:T(8,128)(2,1)S(1)}, u32[]{:S(2)}, u32[]{:S(2)}) collective-permute-start(bf16[1024,384]{1,0:T(8,128)(2,1)S(1)} %collective-permute-done.13.refs_5_), channel_id=1, source_target_pairs={{0,1},{1,0},{2,3},{3,2},{4,5},{5,4},{6,7},{7,6},{8,9},{9,8},{10,11... | collective-permute-start | bytes 2359304 | tf_op jit(solution)/shard_map/ppermute | solution.py:334
  85.2 9.4 %collective-permute-start.7 = (bf16[1024,384]{1,0:T(8,128)(2,1)S(1)}, bf16[1024,384]{1,0:T(8,128)(2,1)S(1)}, u32[]{:S(2)}, u32[]{:S(2)}) collective-permute-start(bf16[1024,384]{1,0:T(8,128)(2,1)S(1)} %collective-permute-done.6.refs_6_), channel_id=1, source_target_pairs={{0,1},{1,0},{2,3},{3,2},{4,5},{5,4},{6,7},{7,6},{8,9},{9,8},{10,11... | collective-permute-start | bytes 2359304 | tf_op jit(solution)/shard_map/ppermute | solution.py:334
  85.2 5.3 %collective-permute-start.3 = (f32[3,16,128]{2,1,0:T(8,128)S(1)}, f32[3,16,128]{2,1,0:T(8,128)S(1)}, u32[]{:S(2)}, u32[]{:S(2)}) collective-permute-start(f32[3,16,128]{2,1,0:T(8,128)S(1)} %get-tuple-element.64.refs_0_), channel_id=1, source_target_pairs={{0,4},{1,5},{2,6},{3,7},{4,0},{5,1},{6,2},{7,3},{8,12},{9,13},{10,... | collective-permute-start | bytes 73736 | tf_op jit(solution)/shard_map/ppermute | solution.py:334
  90.5 1.3 %collective-permute-start.4 = (f32[3,16,128]{2,1,0:T(8,128)S(1)}, f32[3,16,128]{2,1,0:T(8,128)S(1)}, u32[]{:S(2)}, u32[]{:S(2)}) collective-permute-start(f32[3,16,128]{2,1,0:T(8,128)S(1)} %collective-permute-done.3.refs_4_), channel_id=1, source_target_pairs={{0,1},{1,0},{2,3},{3,2},{4,5},{5,4},{6,7},{7,6},{8,9},{9,8},{10,11... | collective-permute-start | bytes 73736 | tf_op jit(solution)/shard_map/ppermute | solution.py:334
  97.6 0.6 copy-start.1

commit v7 on v6

--- a/solution.py
+++ b/solution.py
@@ -14,7 +14,7 @@
 TILE_J = 512
 UNROLL = 4
 BUDGET = 74
-VMEM_MB = (5, 6, 9, 5, 5, 8, 5, 9)
+VMEM_MB = (5, 6, 6, 9, 5, 8, 9)
 MESH = pl.DeviceIdType.MESH
 VMEM_SPEC = pl.BlockSpec(memory_space=pltpu.VMEM)
 
@@ -344,12 +344,12 @@
             return name, half_rows, block_rows - half_rows
 
         plan = [[('own', 0, block_rows)], [upper('near'), upper('next')], [lower('near'), lower('next')],
-                [upper('far')], [upper('away')], [], [lower('far')], [lower('away')]]
+                [upper('far')], [lower('far')], [], [lower('away')]]
         null = up(sum(c[2] for stage in plan for c in stage), TILE_J) + 8 * TILE_J
-        cfg = dict(rows=block_rows, width=width, null=null, plan=plan, modes=['both'] * 3 + ['own'] * 5,
-                   close=[True, False, True, False, False, False, False, True],
-                   budget=[None, BUDGET] + [None] * 6,
-                   split=2, turn=5, scale=math.log2(math.e) * 0.5 / width, inv_len2=1.0 / width)
+        cfg = dict(rows=block_rows, width=width, null=null, plan=plan, modes=['both'] * 4 + ['own'] * 3,
+                   close=[True, False, False, True, False, False, True],
+                   budget=[None, BUDGET] + [None] * 5,
+                   split=3, turn=5, scale=math.log2(math.e) * 0.5 / width, inv_len2=1.0 / width)
 
         mate_pos = move(positions, swap)
         top, bottom = positions[:half_rows], positions[half_rows:]
@@ -357,11 +357,11 @@
         near_a, next_a = move(top, forth), move(top, back)
         near_b, next_b = move(bottom, forth), move(bottom, back)
         far_a, far_b = move(near_a, forth), move(near_b, forth)
-        away_a, away_b = move(far_a, swap), move(far_b, swap)
+        away_b = move(far_b, swap)
         far_meta = move(meta, twice)
         metas = {'own': meta, 'mate': move(meta, swap), 'near': move(meta, forth), 'next': move(meta, back),
                  'far': far_meta, 'away': move(far_meta, swap)}
-        arrays = [[positions], [near_a, next_a], [near_b, next_b], [far_a], [away_a], [], [far_b], [away_b]]
+        arrays = [[positions], [near_a, next_a], [near_b, next_b], [far_a], [far_b], [], [away_b]]
         incoming = None
         for stage in range(len(plan)):
             state, out = pair_call(cfg, stage, metas, arrays[stage], state, mate_pos=mate_pos if stage == 0 else None,

time: 116 us -> 106 us (0.914)
  the two profiles are of different devices: /device:TPU:112 before, /device:TPU:121 now
where the time goes in v7:
time: 106 us
  Pallas kernels  43.3 us (41%)
  waiting for transfers between devices  42.7 us (40%)
  starting transfers between devices  15 us (14%)
  between operations  3.15 us (3%)
  local copies, waits for them, and re-layouts  2.12 us (2%)
    ppermute x14, waiting for transfers between devices, move(): return lax.ppermute(x, 'row', perm)  42.7 us
    pallas_call x7, Pallas kernels, pair_call(): pl.pallas_call(functools.partial(pair_kernel, cfg), out_shape=out_shape,...  28.5 us
    ppermute x14, starting transfers between devices, move(): return lax.ppermute(x, 'row', perm)  15 us
    pallas_call x1, Pallas kernels, total_energy(): pl.pallas_call(functools.partial(energy_kernel, n), out_shape=jax.ShapeDt...  12.8 us
  transfers between devices with their start and end apart: 14, of which 4 were waited for; matrix products, arithmetic and copies ran while one was open for 1% of the time, Pallas kernels for 21%

profile of v7, /device:TPU:121, one launch (start us, length us, event | category | flops | bytes accessed | tf_op | source)
XLA Modules:
  0.0 106.3 jit_solution(5263036219843012594)
XLA Ops:
  0.6 0.7 collective-permute-start.12
  1.3 1.5 %fusion = (bf16[1024,384]{1,0:T(8,128)(2,1)S(1)}, bf16[1024,384]{1,0:T(8,128)(2,1)S(1)}) fusion(bf16[2048,384]{1,0:T(8,128)(2,1)} %pos_ref.1), kind=kLoop, calls=%fused_computation | loop fusion | bytes 3145728 | tf_op jit(solution)/shard_map/slice | solution.py:355
  2.9 3.0 %collective-permute-start.8 = (bf16[1024,384]{1,0:T(8,128)(2,1)S(1)}, bf16[1024,384]{1,0:T(8,128)(2,1)S(1)}, u32[]{:S(2)}, u32[]{:S(2)}) collective-permute-start(bf16[1024,384]{1,0:T(8,128)(2,1)S(1)} %get-tuple-element.110), channel_id=1, source_target_pairs={{0,2},{1,7},{2,4},{3,1},{4,6},{5,3},{6,0},{7,5},{8,10},{9,15},{10,... | collective-permute-start | bytes 2359304 | tf_op jit(solution)/shard_map/ppermute | solution.py:334
  6.5 1.9 %begin.1 = (f32[3,16,128]{2,1,0:T(8,128)S(1)}, bf16[4352,384]{1,0:T(8,128)(2,1)S(1)}, f32[4352,128]{1,0:T(8,128)S(1)}, f32[4352,128]{1,0:T(8,128)S(1)}, bf16[133...) custom-call(bf16[2048,384]{1,0:T(8,128)(2,1)S(1)} %copy-done, ...), custom_call_target="tpu_custom_call" | custom-call | flops 1073741824 | bytes 1048576 | tf_op jit(solution)/shard_map/begin/pallas_call | solution.py:109
  8.4 0.1 collective-permute-start.2
  8.5 2.4 %collective-permute-start = (f32[3,16,128]{2,1,0:T(8,128)S(1)}, f32[3,16,128]{2,1,0:T(8,128)S(1)}, u32[]{:S(2)}, u32[]{:S(2)}) collective-permute-start(f32[3,16,128]{2,1,0:T(8,128)S(1)} %get-tuple-element.56.refs_0_), channel_id=1, source_target_pairs={{0,1},{1,0},{2,3},{3,2},{4,5},{5,4},{6,7},{7,6},{8,9},{9,8},{10,11... | collective-permute-start | bytes 73736 | tf_op jit(solution)/shard_map/ppermute | solution.py:334
  10.9 13.3 %collective-permute-done.2.refs_3_ = f32[3,16,128]{2,1,0:T(8,128)S(1)} collective-permute-done((f32[3,16,128]{2,1,0:T(8,128)S(1)}, f32[3,16,128]{2,1,0:T(8,128)S(1)}, u32[]{:S(2)}, u32[]{:S(2)}) %collective-permute-start.2) | collective-permute-done | bytes 24608 | tf_op jit(solution)/shard_map/ppermute | solution.py:334
  24.3 0.1 collective-permute-start.10
  24.4 2.5 %collective-permute-start.5 = (bf16[1024,384]{1,0:T(8,128)(2,1)S(1)}, bf16[1024,384]{1,0:T(8,128)(2,1)S(1)}, u32[]{:S(2)}, u32[]{:S(2)}) collective-permute-start(bf16[1024,384]{1,0:T(8,128)(2,1)S(1)} %get-tuple-element.111), channel_id=1, source_target_pairs={{0,2},{1,7},{2,4},{3,1},{4,6},{5,3},{6,0},{7,5},{8,10},{9,15},{10,... | collective-permute-start | bytes 2359304 | tf_op jit(solution)/shard_map/ppermute | solution.py:334
  26.9 0.0 collective-permute-done.8.refs_4_
  26.9 0.6 collective-permute-start.9
  27.5 0.1 collective-permute-start.1
  27.6 6.7 %shard_map.50 = (bf16[4352,384]{1,0:T(8,128)(2,1)S(1)}, f32[4352,128]{1,0:T(8,128)S(1)}, f32[4352,128]{1,0:T(8,128)S(1)}, bf16[13312,384]{1,0:T(8,128)(2,1)S(1)}...) custom-call(f32[3,16,128]{2,1,0:T(8,128)S(1)} %get-tuple-element.56., ...), custom_call_target="tpu_custom_call", output_to_operand_aliasing={{0}: (3, {}), {1}: (4, {}), {2}: (5, {}), {3}: (6, {}), {4}... | custom-call | flops 1073741824 | bytes 1048576 | tf_op jit(solution)/shard_map/pallas_call | solution.py:313
  34.4 18.6 %collective-permute-done.1.refs_2_ = f32[3,16,128]{2,1,0:T(8,128)S(1)} collective-permute-done((f32[3,16,128]{2,1,0:T(8,128)S(1)}, f32[3,16,128]{2,1,0:T(8,128)S(1)}, u32[]{:S(2)}, u32[]{:S(2)}) %collective-permute-start.1) | collective-permute-done | bytes 24608 | tf_op jit(solution)/shard_map/ppermute | solution.py:334
  53.0 2.1 %collective-permute-start.3 = (f32[3,16,128]{2,1,0:T(8,128)S(1)}, f32[3,16,128]{2,1,0:T(8,128)S(1)}, u32[]{:S(2)}, u32[]{:S(2)}) collective-permute-start(f32[3,16,128]{2,1,0:T(8,128)S(1)} %get-tuple-element.56.refs_0_), channel_id=1, source_target_pairs={{0,4},{1,5},{2,6},{3,7},{4,0},{5,1},{6,2},{7,3},{8,12},{9,13},{10,... | collective-permute-start | bytes 73736 | tf_op jit(solution)/shard_map/ppermute | solution.py:334
  55.1 5.8 %shard_map.51 = (bf16[4352,384]{1,0:T(8,128)(2,1)S(1)}, f32[4352,128]{1,0:T(8,128)S(1)}, f32[4352,128]{1,0:T(8,128)S(1)}, bf16[13312,384]{1,0:T(8,128)(2,1)S(1)}...) custom-call(f32[3,16,128]{2,1,0:T(8,128)S(1)} %get-tuple-element.56., ...), custom_call_target="tpu_custom_call", output_to_operand_aliasing={{0}: (6, {}), {1}: (7, {}), {2}: (8, {}), {3}: (9, {}), {4}... | custom-call | flops 1073741824 | bytes 1048576 | tf_op jit(solution)/shard_map/pallas_call | solution.py:313
  60.9 0.0 collective-permute-done.5.refs_4_
  60.9 5.8 %shard_map.52 = (bf16[4352,384]{1,0:T(8,128)(2,1)S(1)}, f32[4352,128]{1,0:T(8,128)S(1)}, f32[4352,128]{1,0:T(8,128)S(1)}, bf16[13312,384]{1,0:T(8,128)(2,1)S(1)}...) custom-call(f32[3,16,128]{2,1,0:T(8,128)S(1)} %get-tuple-element.56., ...), custom_call_target="tpu_custom_call", output_to_operand_aliasing={{0}: (6, {}), {1}: (7, {}), {2}: (8, {}), {3}: (9, {}), {4}... | custom-call | flops 1073741824 | bytes 1048576 | tf_op jit(solution)/shard_map/pallas_call | solution.py:313
  66.8 0.0 collective-permute-done.3.refs_4_
  66.8 6.4 %shard_map.53 = (bf16[4352,384]{1,0:T(8,128)(2,1)S(1)}, f32[4352,128]{1,0:T(8,128)S(1)}, f32[4352,128]{1,0:T(8,128)S(1)}, bf16[13312,384]{1,0:T(8,128)(2,1)S(1)}...) custom-call(f32[3,16,128]{2,1,0:T(8,128)S(1)} %get-tuple-element.56., ...), custom_call_target="tpu_custom_call", output_to_operand_aliasing={{0}: (6, {}), {1}: (7, {}), {2}: (8, {}), {3}: (9, {}), {4}... | custom-call | flops 1073741824 | bytes 1048576 | tf_op jit(solution)/shard_map/pallas_call | solution.py:313
  73.2 0.1 collective-permute-start.13
  73.3 1.4 %collective-permute-start.6 = (bf16[1024,384]{1,0:T(8,128)(2,1)S(1)}, bf16[1024,384]{1,0:T(8,128)(2,1)S(1)}, u32[]{:S(2)}, u32[]{:S(2)}) collective-permute-start(bf16[1024,384]{1,0:T(8,128)(2,1)S(1)} %collective-permute-done.5.refs_4_), channel_id=1, source_target_pairs={{0,2},{1,7},{2,4},{3,1},{4,6},{5,3},{6,0},{7,5},{8,10},{9,15},{10,... | collective-permute-start | bytes 2359304 | tf_op jit(solution)/shard_map/ppermute | solution.py:334
  74.7 10.4 %collective-permute-done.6.refs_5_ = bf16[1024,384]{1,0:T(8,128)(2,1)S(1)} collective-permute-done((bf16[1024,384]{1,0:T(8,128)(2,1)S(1)}, bf16[1024,384]{1,0:T(8,128)(2,1)S(1)}, u32[]{:S(2)}, u32[]{:S(2)}) %collective-permute-start.6) | collective-permute-done | bytes 786464 | tf_op jit(solution)/shard_map/ppermute | solution.py:334
  85.1 1.8 %collective-permute-start.7 = (bf16[1024,384]{1,0:T(8,128)(2,1)S(1)}, bf16[1024,384]{1,0:T(8,128)(2,1)S(1)}, u32[]{:S(2)}, u32[]{:S(2)}) collective-permute-start(bf16[1024,384]{1,0:T(8,128)(2,1)S(1)} %collective-permute-done.6.refs_5_), channel_id=1, source_target_pairs={{0,1},{1,0},{2,3},{3,2},{4,5},{5,4},{6,7},{7,6},{8,9},{9,8},{10,11... | collective-permute-start | bytes 2359304 | tf_op jit(solution)/shard_map/ppermute | solution.py:334
  86.9 0.0 collective-permute-start.4
  86.9 0.3 shard_map.54
  87.2 0.0 collective-permute-done.13.refs_5_
  87.2 1.3 %shard_map.55 = (bf16[4352,384]{1,0:T(8,128)(2,1)S(1)}, f32[4352,128]{1,0:T(8,128)S(1)}, f32[4352,128]{1,0:T(8,128)S(1)}, bf16[13312,384]{1,0:T(8,128)(2,1)S(1)}...) custom-call(f32[3,16,128]{2,1,0:T(8,128)S(1)} %get-tuple-element.56., ...), custom_call_target="tpu_custom_call", output_to_operand_aliasing={{0}: (6, {}), {1}: (7, {}), {2}: (8, {}), {3}: (9, {}), {4}... | custom-call | flops 1073741824 | bytes 1048576 | tf_op jit(solution)/shard_map/pallas_call | solution.py:313
  88.5 0.3 collective-permute-done.4.refs_5_
  88.9 2.2 %shard_map.56 = (bf16[4352,384]{1,0:T(8,128)(2,1)S(1)}, f32[4352,128]{1,0:T(8,128)S(1)}, f32[4352,128]{1,0:T(8,128)S(1)}, bf16[13312,384]{1,0:T(8,128)(2,1)S(1)}...) custom-call(f32[3,16,128]{2,1,0:T(8,128)S(1)} %get-tuple-element.56., ...), custom_call_target="tpu_custom_call", output_to_operand_aliasing={{0}: (7, {}), {1}: (8, {}), {2}: (9, {}), {3}: (10, {}), {4... | custom-call | flops 1073741824 | bytes 1048576 | tf_op jit(solution)/shard_map/pallas_call | solution.py:313
  91.1 0.6 copy-done.1
  91.7 12.8 %energy.1 = f32[1]{0:T(128)} custom-call(f32[8,128]{1,0:T(8,128)} %copy-done.1), custom_call_target="tpu_custom_call" | custom-call | tf_op jit(solution)/shard_map/energy/pallas_call | solution.py:47
  (12 shorter events, 0.0 us)
Async XLA Ops:
  0.6 5.8 %copy-start = (bf16[2048,384]{1,0:T(8,128)(2,1)S(1)}, bf16[2048,384]{1,0:T(8,128)(2,1)}, u32[]{:S(2)}) copy-start(bf16[2048,384]{1,0:T(8,128)(2,1)} %pos_ref.1) | copy-start | bytes 4718596
  0.6 5.8 %copy-start.2 = (f32[2048]{0:T(1024)S(1)}, f32[2048]{0:T(1024)}, u32[]{:S(2)}) copy-start(f32[2048]{0:T(1024)} %param.4) | copy-start | bytes 24580
  0.6 26.9 %collective-permute-start.12 = (bf16[2048,384]{1,0:T(8,128)(2,1)}, bf16[2048,384]{1,0:T(8,128)(2,1)S(1)}, u32[]{:S(2)}, u32[]{:S(2)}) collective-permute-start(bf16[2048,384]{1,0:T(8,128)(2,1)} %pos_ref.1), channel_id=1, source_target_pairs={{0,1},{1,0},{2,3},{3,2},{4,5},{5,4},{6,7},{7,6},{8,9},{9,8},{10,11... | collective-permute-start | bytes 4718600 | tf_op jit(solution)/shard_map/ppermute | solution.py:334
  2.9 24.1 %collective-permute-start.8 = (bf16[1024,384]{1,0:T(8,128)(2,1)S(1)}, bf16[1024,384]{1,0:T(8,128)(2,1)S(1)}, u32[]{:S(2)}, u32[]{:S(2)}) collective-permute-start(bf16[1024,384]{1,0:T(8,128)(2,1)S(1)} %get-tuple-element.110), channel_id=1, source_target_pairs={{0,2},{1,7},{2,4},{3,1},{4,6},{5,3},{6,0},{7,5},{8,10},{9,15},{10,... | collective-permute-start | bytes 2359304 | tf_op jit(solution)/shard_map/ppermute | solution.py:334
  5.8 49.3 %collective-permute-start.11 = (bf16[1024,384]{1,0:T(8,128)(2,1)S(1)}, bf16[1024,384]{1,0:T(8,128)(2,1)S(1)}, u32[]{:S(2)}, u32[]{:S(2)}) collective-permute-start(bf16[1024,384]{1,0:T(8,128)(2,1)S(1)} %get-tuple-element.110), channel_id=1, source_target_pairs={{2,0},{7,1},{4,2},{1,3},{6,4},{3,5},{0,6},{5,7},{10,8},{15,9},{12,... | collective-permute-start | bytes 2359304 | tf_op jit(solution)/shard_map/ppermute | solution.py:334
  8.4 15.8 %collective-permute-start.2 = (f32[3,16,128]{2,1,0:T(8,128)S(1)}, f32[3,16,128]{2,1,0:T(8,128)S(1)}, u32[]{:S(2)}, u32[]{:S(2)}) collective-permute-start(f32[3,16,128]{2,1,0:T(8,128)S(1)} %get-tuple-element.56.refs_0_), channel_id=1, source_target_pairs={{2,0},{7,1},{4,2},{1,3},{6,4},{3,5},{0,6},{5,7},{10,8},{15,9},{12,... | collective-permute-start | bytes 73736 | tf_op jit(solution)/shard_map/ppermute | solution.py:334
  8.5 15.9 %collective-permute-start = (f32[3,16,128]{2,1,0:T(8,128)S(1)}, f32[3,16,128]{2,1,0:T(8,128)S(1)}, u32[]{:S(2)}, u32[]{:S(2)}) collective-permute-start(f32[3,16,128]{2,1,0:T(8,128)S(1)} %get-tuple-element.56.refs_0_), channel_id=1, source_target_pairs={{0,1},{1,0},{2,3},{3,2},{4,5},{5,4},{6,7},{7,6},{8,9},{9,8},{10,11... | collective-permute-start | bytes 73736 | tf_op jit(solution)/shard_map/ppermute | solution.py:334
  24.3 36.7 %collective-permute-start.10 = (bf16[1024,384]{1,0:T(8,128)(2,1)S(1)}, bf16[1024,384]{1,0:T(8,128)(2,1)S(1)}, u32[]{:S(2)}, u32[]{:S(2)}) collective-permute-start(bf16[1024,384]{1,0:T(8,128)(2,1)S(1)} %get-tuple-element.111), channel_id=1, source_target_pairs={{2,0},{7,1},{4,2},{1,3},{6,4},{3,5},{0,6},{5,7},{10,8},{15,9},{12,... | collective-permute-start | bytes 2359304 | tf_op jit(solution)/shard_map/ppermute | solution.py:334
  24.4 36.5 %collective-permute-start.5 = (bf16[1024,384]{1,0:T(8,128)(2,1)S(1)}, bf16[1024,384]{1,0:T(8,128)(2,1)S(1)}, u32[]{:S(2)}, u32[]{:S(2)}) collective-permute-start(bf16[1024,384]{1,0:T(8,128)(2,1)S(1)} %get-tuple-element.111), channel_id=1, source_target_pairs={{0,2},{1,7},{2,4},{3,1},{4,6},{5,3},{6,0},{7,5},{8,10},{9,15},{10,... | collective-permute-start | bytes 2359304 | tf_op jit(solution)/shard_map/ppermute | solution.py:334
  26.9 39.8 %collective-permute-start.9 = (bf16[1024,384]{1,0:T(8,128)(2,1)S(1)}, bf16[1024,384]{1,0:T(8,128)(2,1)S(1)}, u32[]{:S(2)}, u32[]{:S(2)}) collective-permute-start(bf16[1024,384]{1,0:T(8,128)(2,1)S(1)} %collective-permute-done.8.refs_4_), channel_id=1, source_target_pairs={{0,2},{1,7},{2,4},{3,1},{4,6},{5,3},{6,0},{7,5},{8,10},{9,15},{10,... | collective-permute-start | bytes 2359304 | tf_op jit(solution)/shard_map/ppermute | solution.py:334
  27.5 25.5 %collective-permute-start.1 = (f32[3,16,128]{2,1,0:T(8,128)S(1)}, f32[3,16,128]{2,1,0:T(8,128)S(1)}, u32[]{:S(2)}, u32[]{:S(2)}) collective-permute-start(f32[3,16,128]{2,1,0:T(8,128)S(1)} %get-tuple-element.56.refs_0_), channel_id=1, source_target_pairs={{0,2},{1,7},{2,4},{3,1},{4,6},{5,3},{6,0},{7,5},{8,10},{9,15},{10,... | collective-permute-start | bytes 73736 | tf_op jit(solution)/shard_map/ppermute | solution.py:334
  53.0 13.8 %collective-permute-start.3 = (f32[3,16,128]{2,1,0:T(8,128)S(1)}, f32[3,16,128]{2,1,0:T(8,128)S(1)}, u32[]{:S(2)}, u32[]{:S(2)}) collective-permute-start(f32[3,16,128]{2,1,0:T(8,128)S(1)} %get-tuple-element.56.refs_0_), channel_id=1, source_target_pairs={{0,4},{1,5},{2,6},{3,7},{4,0},{5,1},{6,2},{7,3},{8,12},{9,13},{10,... | collective-permute-start | bytes 73736 | tf_op jit(solution)/shard_map/ppermute | solution.py:334
  73.2 14.1 %collective-permute-start.13 = (f32[392,2048]{1,0:T(8,128)S(1)}, f32[392,2048]{1,0:T(8,128)S(1)}, u32[]{:S(2)}, u32[]{:S(2)}) collective-permute-start(f32[392,2048]{1,0:T(8,128)S(1)} %get-tuple-element.85), channel_id=1, source_target_pairs={{0,1},{1,0},{2,3},{3,2},{4,5},{5,4},{6,7},{7,6},{8,9},{9,8},{10,11... | collective-permute-start | bytes 9633800 | tf_op jit(solution)/shard_map/ppermute | solution.py:334
  73.3 11.8 %collective-permute-start.6 = (bf16[1024,384]{1,0:T(8,128)(2,1)S(1)}, bf16[1024,384]{1,0:T(8,128)(2,1)S(1)}, u32[]{:S(2)}, u32[]{:S(2)}) collective-permute-start(bf16[1024,384]{1,0:T(8,128)(2,1)S(1)} %collective-permute-done.5.refs_4_), channel_id=1, source_target_pairs={{0,2},{1,7},{2,4},{3,1},{4,6},{5,3},{6,0},{7,5},{8,10},{9,15},{10,... | collective-permute-start | bytes 2359304 | tf_op jit(solution)/shard_map/ppermute | solution.py:334
  85.1 3.8 %collective-permute-start.7 = (bf16[1024,384]{1,0:T(8,128)(2,1)S(1)}, bf16[1024,384]{1,0:T(8,128)(2,1)S(1)}, u32[]{:S(2)}, u32[]{:S(2)}) collective-permute-start(bf16[1024,384]{1,0:T(8,128)(2,1)S(1)} %collective-permute-done.6.refs_5_), channel_id=1, source_target_pairs={{0,1},{1,0},{2,3},{3,2},{4,5},{5,4},{6,7},{7,6},{8,9},{9,8},{10,11... | collective-permute-start | bytes 2359304 | tf_op jit(solution)/shard_map/ppermute | solution.py:334
  86.9 1.9 %collective-permute-start.4 = (f32[3,16,128]{2,1,0:T(8,128)S(1)}, f32[3,16,128]{2,1,0:T(8,128)S(1)}, u32[]{:S(2)}, u32[]{:S(2)}) collective-permute-start(f32[3,16,128]{2,1,0:T(8,128)S(1)} %collective-permute-done.3.refs_4_), channel_id=1, source_target_pairs={{0,1},{1,0},{2,3},{3,2},{4,5},{5,4},{6,7},{7,6},{8,9},{9,8},{10,11... | collective-permute-start | bytes 73736 | tf_op jit(solution)/shard_map/ppermute | solution.py:334
  91.1 0.6 copy-start.1
